TPU v7x, 128 devices: a whole 4x4x4 slice. The times are simulated.
128 devices in a mesh: grp: 4 (over y), col: 32 (over z, x, core).
Axes of the slice: x: 4, y: 4, z: 4, core: 2. Of those that a mesh axis runs over, the one named last changes fastest.
Arguments:
- start_block: float32 [16, 32768], P(None, ('grp', 'col')), may hold values from -6 to 6
- tile_values: float32 [4, 32, 32, 256, 256], P('grp', 'col'), may hold values from 0 to 1, as said below
- tile_row: int32 [4, 32, 32], P('grp', 'col'), may hold values from 0 to 127, as said below
- tile_col: int32 [4, 32, 32], P('grp', 'col'), may hold values from 0 to 127, as said below
- tile_count: int32 [4, 32], P('grp', 'col'), may hold values from 8 to 32, as said below
Outputs:
- basis: float32 [5, 16, 32768], P(None, None, ('grp', 'col'))
- projections: float32 [4, 4, 16, 16], replicated
- factors: float32 [5, 16, 16], replicated
Inputs may be any that keep to these rules, and one draw needn't show every extreme that they name: `tile_row`: A tile of the device at grp index g lies in tile rows g * 32 * 1 to (g + 1) * 32 - 1. `tile_col`: A tile column t of the device at col index c has (t) % 32 == c. Coordinate pairs may repeat; repeated tiles add. The live tiles of a device are its first tile_count slots; some device has all 32 slots live. `tile_values`: entries are nonnegative.
All inputs are finite; a program needn't handle non-finite values.
Results may differ from a plain program's by a relative error of at most 0.0003.
Values sent between devices are 32-bit elements; how exact they have to be, the bound alone decides.
No kernel may reach another device: no remote copies, remote signals or barrier semaphores. Data moves between devices by JAX's collectives and lax.ppermute only.
A program may use at most 64 MiB of HBM per device.

v0:
```python
import functools
import jax
import jax.numpy as jnp
from jax import lax
from jax.experimental import pallas as pl
from jax.experimental.pallas import tpu as pltpu
from jax.sharding import Mesh
from jax.sharding import PartitionSpec as P

ITERS = 4
ZX = ("col_0", "col_1")
CORE = "col_2"
GRP_COL = ("grp", "col_0", "col_1", "col_2")
GROUP = 4
highest = lax.Precision.HIGHEST
VMEM = pl.BlockSpec(memory_space=pltpu.VMEM)
SMEM = pl.BlockSpec(memory_space=pltpu.SMEM)
HBM = pl.BlockSpec(memory_space=pl.ANY)
f32 = jnp.float32
bf16 = jnp.bfloat16


def split(x):
    hi = x.astype(bf16)
    return hi, (x - hi.astype(f32)).astype(bf16)


def dot(a, b, dims):
    return lax.dot_general(a, b, (dims, ((), ())), preferred_element_type=f32)


def dot_f32(a, b, dims):
    return lax.dot_general(a, b, (dims, ((), ())), precision=highest, preferred_element_type=f32)


def tile_copies(tiles, buf, sems):
    slots = buf.shape[0]
    return [
        pltpu.make_async_copy(
            tiles.at[0, 0, pl.ds(q * GROUP, GROUP)], buf.at[pl.ds(q * GROUP, GROUP)], sems.at[q]
        )
        for q in range(slots // GROUP)
    ]


def products(lhs_hi, lhs_lo, tile, dims, first):
    hi, lo = split(tile)
    top = dot(lhs_hi, hi, dims)
    low = dot(lhs_lo, lo, dims)
    out = top[0:16] + top[16:32] + low[0:16]
    if first:
        out = jnp.concatenate([out, top[32:40] + low[16:24]], axis=0)
    return out


def stacked_lhs(piece, first):
    hi, lo = split(piece)
    if first:
        ones = jnp.ones((16, piece.shape[1]), bf16)
        return jnp.concatenate([hi, lo, ones], axis=0), jnp.concatenate([hi, ones], axis=0)
    return jnp.concatenate([hi, lo], axis=0), hi


def rows_kernel(first, info, tiles, own, one, two, three, mine, other, buf, lhs_hi, lhs_lo, sems):
    copies = tile_copies(tiles, buf, sems)
    for copy in copies:
        copy.start()
    for k, piece in enumerate((own, one, two, three)):
        lhs_hi[k], lhs_lo[k] = stacked_lhs(piece[0:16], first)
    mine[...] = jnp.zeros_like(mine)
    other[...] = jnp.zeros_like(other)
    for q, copy in enumerate(copies):
        copy.wait()

        @pl.when(q * GROUP < info[4, 0])
        def _():
            results = []
            for u in range(GROUP):
                s = q * GROUP + u
                k = info[2, s]
                results.append(
                    products(lhs_hi[k], lhs_lo[k], buf[s], ((1,), (1,)), first)
                    * (s < info[4, 0]).astype(f32)
                )
            for u in range(GROUP):
                s = q * GROUP + u

                @pl.when(info[1, s] == 0)
                def _():
                    mine[info[0, s]] += results[u]

                @pl.when(info[1, s] != 0)
                def _():
                    other[info[0, s]] += results[u]


def cols_kernel(first, info, tiles, near, far, own, one, two, three, buf, acc, sems):
    copies = tile_copies(tiles, buf, sems)
    for copy in copies:
        copy.start()
    acc[...] = jnp.zeros_like(acc)
    gram = jnp.zeros_like(near[0, 16:24])
    for p in range(near.shape[0]):
        gram = gram + (near[p, 16:24] + far[p, 16:24])
    for q, copy in enumerate(copies):
        copy.wait()

        @pl.when(q * GROUP < info[4, 0])
        def _():
            results = []
            for u in range(GROUP):
                s = q * GROUP + u
                place = info[0, s]
                piece = jnp.where(info[1, s] == 0, near[place, 0:16], far[place, 0:16])
                left_hi, left_lo = stacked_lhs(piece, first)
                results.append(
                    products(left_hi, left_lo, buf[s], ((1,), (0,)), first)
                    * (s < info[4, 0]).astype(f32)
                )
            for u in range(GROUP):
                s = q * GROUP + u
                acc[info[3, s]] += results[u]

    for k, out in enumerate((own, one, two, three)):
        out[...] = jnp.concatenate([acc[k], gram], axis=0)


def rows_product(first, info, tiles, pieces):
    height = 24 if first else 16
    slots, size = tiles.shape[2], tiles.shape[3]
    out = jax.ShapeDtypeStruct((16, height, size), f32)
    return pl.pallas_call(
        functools.partial(rows_kernel, first),
        name="rows_first" if first else "rows_next",
        out_shape=(out, out),
        in_specs=[SMEM, HBM] + [VMEM] * 4,
        out_specs=(VMEM, VMEM),
        scratch_shapes=[
            pltpu.VMEM((slots, size, size), f32),
            pltpu.VMEM((4, 48 if first else 32, size), bf16),
            pltpu.VMEM((4, 32 if first else 16, size), bf16),
            pltpu.SemaphoreType.DMA((slots // GROUP,)),
        ],
        cost_estimate=pl.CostEstimate(flops=400_000_000, bytes_accessed=8 << 20, transcendentals=0),
    )(info, tiles, *pieces)


def cols_product(first, info, tiles, near, far):
    height = 24 if first else 16
    slots, size = tiles.shape[2], tiles.shape[3]
    out = jax.ShapeDtypeStruct((height + 8, size), f32)
    return pl.pallas_call(
        functools.partial(cols_kernel, first),
        name="cols_first" if first else "cols_next",
        out_shape=(out,) * 4,
        in_specs=[SMEM, HBM, VMEM, VMEM],
        out_specs=(VMEM,) * 4,
        scratch_shapes=[
            pltpu.VMEM((slots, size, size), f32),
            pltpu.VMEM((4, height, size), f32),
            pltpu.SemaphoreType.DMA((slots // GROUP,)),
        ],
        cost_estimate=pl.CostEstimate(flops=400_000_000, bytes_accessed=8 << 20, transcendentals=0),
    )(info, tiles, near, far)


def unpack_gram(packed):
    return jnp.concatenate([packed[:, 0:128], packed[:, 128:256]], axis=0)


def pack_gram(gram):
    width = gram.shape[1]
    if width < 128:
        gram = jnp.concatenate([gram, jnp.zeros((16, 128 - width), f32)], axis=1)
    return jnp.concatenate([gram[0:8], gram[8:16]], axis=1)


def eye16():
    return (
        lax.broadcasted_iota(jnp.int32, (16, 16), 0) == lax.broadcasted_iota(jnp.int32, (16, 16), 1)
    ).astype(f32)


def factor_and_inverse(gram):
    work = jnp.concatenate([gram, eye16(), jnp.zeros((16, 96), f32)], axis=1)
    rows = lax.broadcasted_iota(jnp.int32, (16, 128), 0)
    pivots = jnp.zeros((16, 128), f32)
    for j in range(16):
        column = jnp.broadcast_to(work[:, j : j + 1], (16, 128))
        pivot = jnp.broadcast_to(column[j : j + 1], (16, 128))
        row = jnp.broadcast_to(work[j : j + 1], (16, 128))
        pivots = jnp.where(rows == j, pivot, pivots)
        work = work - jnp.where(rows > j, column / pivot, 0.0) * row
    scaled = work / jnp.sqrt(pivots)
    upper = jnp.where(
        lax.broadcasted_iota(jnp.int32, (16, 16), 0) <= lax.broadcasted_iota(jnp.int32, (16, 16), 1),
        scaled[:, 0:16],
        0.0,
    )
    return upper, scaled[:, 16:32]


def update_kernel(step, node_total, *refs):
    refs = list(refs)
    take = lambda count: [refs.pop(0) for _ in range(count)]
    (arrived,) = take(1)
    own, one, two, three = take(4)
    before, degree = (None, None) if step == 0 else take(2)
    shift_in = take(1)[0] if step > 1 else None
    (start,) = take(1) if step == 0 else (None,)
    outs = refs
    side = own[...] + one[...] + two[...] + three[...]
    height = arrived.shape[1]
    total = side[0:height]
    for p in range(arrived.shape[0]):
        total = total + arrived[p]
    gram = unpack_gram(side[height : height + 8]) * (1.0 / node_total)
    if step == 0:
        packed, state, degree_out, upper_out = outs
        level = total[16:17]
        upper, inverse = factor_and_inverse(gram[:, 0:16])
        block = start[...]
        applied = level * block - total[0:16]
        both = dot_f32(inverse, jnp.concatenate([block, applied], axis=1), ((1,), (0,)))
        degree_out[...] = total[16:24]
        stack = both
        new_vectors = both[:, 0:256]
        new_applied = both[:, 256:512]
        state[...] = both
        basis = new_vectors
        upper_out[...] = upper
    else:
        if step == 1:
            packed, state, coeff_out, upper_out, shift_out = outs
        else:
            packed, state, coeff_out, upper_out = outs
        width = 16 * step
        coeffs = gram[:, 0:width]
        square = gram[:, width : width + 16]
        square = square - dot_f32(coeffs, coeffs, ((1,), (1,)))
        upper, inverse = factor_and_inverse(square)
        stack = before[...]
        newest = stack[width - 16 : width]
        vectors, applied = newest[:, 0:256], newest[:, 256:512]
        level = degree[0:1]
        twice = level * applied - total[0:16]
        coeff_out[...] = jnp.concatenate([coeffs, jnp.zeros((16, 128 - width), f32)], axis=1)
        if step == 1:
            shift = jnp.broadcast_to(
                jnp.sum(coeffs * eye16(), axis=(0, 1), keepdims=True) * (1.0 / 16), (8, 128)
            )
            shift_out[...] = shift
            scalar = shift[0:1, 0:1]
            moved = applied - scalar * vectors
            twice = twice - scalar * applied - scalar * moved
            coeffs = coeffs - scalar * eye16()
            applied = moved
            stack = jnp.concatenate([vectors, applied], axis=1)
        else:
            scalar = shift_in[0:1, 0:1]
            twice = twice - scalar * applied
            coeff_out[:, width - 16 : width] = coeffs[:, width - 16 : width] + scalar * eye16()
        rest = jnp.concatenate([applied, twice], axis=1) - dot_f32(coeffs, stack, ((1,), (0,)))
        both = dot_f32(inverse, rest, ((1,), (0,)))
        state[0:width] = stack
        state[width : width + 16] = both
        upper_out[...] = upper
        new_applied = both[:, 256:512]
        basis = jnp.concatenate([stack[:, 0:256], both[:, 0:256]], axis=0)
    partial = dot_f32(new_applied, jnp.concatenate([basis, new_applied], axis=0), ((1,), (1,)))
    message = jnp.concatenate([new_applied, pack_gram(partial)], axis=0)
    for p in range(packed.shape[0]):
        packed[p] = message


def update(step, node_total, arrived, sides, state, degree, shift, start):
    size = arrived.shape[2]
    shapes = [
        jax.ShapeDtypeStruct((16, 24, size), f32),
        jax.ShapeDtypeStruct((16 * (step + 1), 2 * size), f32),
    ]
    if step == 0:
        shapes += [jax.ShapeDtypeStruct((8, size), f32), jax.ShapeDtypeStruct((16, 16), f32)]
        extra = [start]
    else:
        shapes += [jax.ShapeDtypeStruct((16, 128), f32), jax.ShapeDtypeStruct((16, 16), f32)]
        extra = [state, degree]
        if step == 1:
            shapes.append(jax.ShapeDtypeStruct((8, 128), f32))
        else:
            extra.append(shift)
    args = [arrived, *sides, *extra]
    return pl.pallas_call(
        functools.partial(update_kernel, step, node_total),
        name=f"update_{step}",
        out_shape=tuple(shapes),
        in_specs=[VMEM] * len(args),
        out_specs=(VMEM,) * len(shapes),
        cost_estimate=pl.CostEstimate(flops=400_000_000, bytes_accessed=1 << 20, transcendentals=0),
    )(*args)


def last_kernel(node_total, arrived, state, shift, block_out, coeff_out, upper_out):
    packed = arrived[0]
    for p in range(1, arrived.shape[0]):
        packed = packed + arrived[p]
    gram = unpack_gram(packed) * (1.0 / node_total)
    width = 16 * ITERS
    coeffs = gram[:, 0:width]
    square = gram[:, width : width + 16] - dot_f32(coeffs, coeffs, ((1,), (1,)))
    upper, inverse = factor_and_inverse(square)
    stack = state[...]
    rest = stack[width - 16 : width, 256:512] - dot_f32(coeffs, stack[:, 0:256], ((1,), (0,)))
    block_out[...] = dot_f32(inverse, rest, ((1,), (0,)))
    coeff_out[...] = jnp.concatenate([coeffs, jnp.zeros((16, 128 - width), f32)], axis=1)
    coeff_out[:, width - 16 : width] = coeffs[:, width - 16 : width] + shift[0:1, 0:1] * eye16()
    upper_out[...] = upper


def last(node_total, arrived, state, shift):
    size = 256
    return pl.pallas_call(
        functools.partial(last_kernel, node_total),
        name="last",
        out_shape=(
            jax.ShapeDtypeStruct((16, size), f32),
            jax.ShapeDtypeStruct((16, 128), f32),
            jax.ShapeDtypeStruct((16, 16), f32),
        ),
        in_specs=[VMEM] * 3,
        out_specs=(VMEM,) * 3,
    )(arrived, state, shift)


def first_message_kernel(block, packed):
    partial = dot_f32(block[...], block[...], ((1,), (1,)))
    message = jnp.concatenate([block[...], pack_gram(partial)], axis=0)
    for p in range(packed.shape[0]):
        packed[p] = message


def first_message(block):
    return pl.pallas_call(
        first_message_kernel,
        name="first_message",
        out_shape=jax.ShapeDtypeStruct((16, 24, block.shape[1]), f32),
        in_specs=[VMEM],
        out_specs=VMEM,
    )(block)


def shifted(value, hop):
    size = lax.axis_size("grp")
    return lax.ppermute(value, "grp", [(i, (i + hop) % size) for i in range(size)])


def swapped(value):
    return lax.ppermute(value, CORE, [(0, 1), (1, 0)])


def exchanged(value, axes):
    return lax.all_to_all(value, axes, split_axis=0, concat_axis=0, tiled=True)


def body(start_block, tile_values, tile_row, tile_col, tile_count):
    grp_size = lax.axis_size("grp")
    col_size = lax.axis_size(ZX) * lax.axis_size(CORE)
    node_total = float(start_block.shape[1] * grp_size * col_size)
    grp_index = lax.axis_index("grp")
    core_index = lax.axis_index(CORE)
    local_row = tile_row[0, 0] - grp_index * col_size
    home = tile_col[0, 0] // col_size
    info = jnp.stack(
        [
            local_row // 2,
            (local_row % 2) ^ core_index,
            (grp_index - home + grp_size) % grp_size,
            (home - grp_index + grp_size) % grp_size,
            jnp.broadcast_to(tile_count[0, 0], local_row.shape),
        ]
    )
    info = jnp.where(
        jnp.array([[15], [1], [3], [3], [1 << 20]], jnp.int32) < info, 0, jnp.maximum(info, 0)
    )
    message = first_message(start_block)
    piece = start_block
    state = degree = shift = None
    uppers, coeffs = [], []
    for step in range(ITERS):
        first = step == 0
        near = exchanged(message, ZX)
        pieces = [piece] + [shifted(piece, hop) for hop in range(1, grp_size)]
        mine, other = rows_product(first, info, tile_values, pieces)
        far = swapped(near)
        rows = mine + swapped(other)
        arrived = exchanged(rows, ZX)
        sides = cols_product(first, info, tile_values, near, far)
        sides = [sides[0]] + [shifted(sides[hop], hop) for hop in range(1, grp_size)]
        outs = update(step, node_total, arrived, sides, state, degree, shift, start_block)
        message, state = outs[0], outs[1]
        piece = message[0, 0:16]
        if first:
            degree = outs[2]
        else:
            coeffs.append(outs[2])
        uppers.append(outs[3])
        if step == 1:
            shift = outs[4]
    packed = message[0, 16:24].reshape(1, -1)
    packed = exchanged(jnp.broadcast_to(packed, (16, *packed.shape)), ("grp", "col_1")).sum(0)
    packed = exchanged(jnp.broadcast_to(packed, (8, *packed.shape)), ("col_0", "col_2"))
    block, coeff, upper = last(node_total, packed.reshape(8, 8, 256), state, shift)
    coeffs.append(coeff)
    uppers.append(upper)
    basis = jnp.concatenate(
        [state[:, 0:256].reshape(ITERS, 16, 256), block[None]], axis=0
    )
    shaped = jnp.stack(coeffs)[:, :, 0 : 16 * ITERS].reshape(ITERS, 16, ITERS, 16)
    return basis, shaped.transpose(0, 2, 1, 3), jnp.stack(uppers).transpose(0, 2, 1)


def solution(mesh):
    split_mesh = Mesh(
        mesh.devices.reshape(mesh.shape["grp"], 4, 4, 2), ("grp", "col_0", "col_1", "col_2")
    )
    col = ("col_0", "col_1", "col_2")
    placed = (
        P(None, GRP_COL),
        P("grp", col, None, None, None),
        P("grp", col, None),
        P("grp", col, None),
        P("grp", col),
    )
    return jax.shard_map(
        body,
        mesh=split_mesh,
        in_specs=placed,
        out_specs=(P(None, None, GRP_COL), P(), P()),
        check_vma=False,
    )
```

profile of v0, /device:TPU:1, one launch (start us, length us, event | category | flops | bytes accessed | tf_op | source)
XLA Modules:
  0.0 248.1 jit_solution(6928906820498954389)
XLA Ops:
  7.0 7.6 %all-to-all-start.1 = ((f32[16,24,256]{2,1,0:T(8,128)}), f32[16,24,256]{2,1,0:T(8,128)S(1)}, u32[]{:S(2)}, u32[]{:S(2)}) async-start(f32[16,24,256]{2,1,0:T(8,128)} %first_message.1), calls=%async_computation.1 | async-start | bytes 786432 | tf_op jit(solution)/shard_map/all_to_all | solution.py:362
  18.5 5.2 %rows_first.1 = (f32[16,24,256]{2,1,0:T(8,128)}, f32[16,24,256]{2,1,0:T(8,128)}) custom-call(s32[5,32]{1,0:T(8,128)} %maximum_select_fusion.info, f32[1,1,32,256,256]{4,3,2,1,0:T(8,128)} %tiles.15, f32[16,256]{1,0:T(8,128)} %refs_5_.1, f32[16,256]{1,0:T(8,128)} %copy-done.17, f32[16,256]{1,0:T(8,128)} %copy-done.16, f32[16,256]{1,0:T(8,128)} %copy-done.15), custom_call_target="tpu_custom_call" | custom-call | flops 400000000 | bytes 8388608 | tf_op jit(solution)/shard_map/rows_first/pallas_call | solution.py:132
  29.0 8.0 %all-to-all-start = ((f32[16,24,256]{2,1,0:T(8,128)}), f32[16,24,256]{2,1,0:T(8,128)S(1)}, u32[]{:S(2)}, u32[]{:S(2)}) async-start(f32[16,24,256]{2,1,0:T(8,128)} %add.92), calls=%async_computation | async-start | bytes 786432 | tf_op jit(solution)/shard_map/all_to_all | solution.py:362
  37.8 5.2 %cols_first.1 = (f32[32,256]{1,0:T(8,128)}, f32[32,256]{1,0:T(8,128)}, f32[32,256]{1,0:T(8,128)}, f32[32,256]{1,0:T(8,128)}) custom-call(s32[5,32]{1,0:T(8,128)} %maximum_select_fusion.info, f32[1,1,32,256,256]{4,3,2,1,0:T(8,128)} %tiles.15, f32[16,24,256]{2,1,0:T(8,128)} %copy-done, f32[16,24,256]{2,1,0:T(8,128)} %copy-done.5), custom_call_target="tpu_custom_call" | custom-call | flops 400000000 | bytes 8388608 | tf_op jit(solution)/shard_map/cols_first/pallas_call | solution.py:152
  49.6 4.1 %update_0.1 = (f32[16,24,256]{2,1,0:T(8,128)}, f32[16,512]{1,0:T(8,128)}, f32[8,256]{1,0:T(8,128)}, f32[16,16]{1,0:T(8,128)}) custom-call(f32[16,24,256]{2,1,0:T(8,128)} %copy-done.8, f32[32,256]{1,0:T(8,128)} %get-tuple-element.49.refs_1_, f32[32,256]{1,0:T(8,128)} %copy-done.33, f32[32,256]{1,0:T(8,128)} %copy-done.34, f32[32,256]{1,0:T(8,128)} %copy-done.35, ...), custom_call_target="tpu_custom_call" | custom-call | flops 400000000 | bytes 1048576 | tf_op jit(solution)/shard_map/update_0/pallas_call | solution.py:293
  53.7 6.7 %all-to-all-start.3 = ((f32[16,24,256]{2,1,0:T(8,128)}), f32[16,24,256]{2,1,0:T(8,128)S(1)}, u32[]{:S(2)}, u32[]{:S(2)}) async-start(f32[16,24,256]{2,1,0:T(8,128)} %get-tuple-element.53), calls=%async_computation.3 | async-start | bytes 786432 | tf_op jit(solution)/shard_map/all_to_all | solution.py:362
  68.6 5.1 %rows_next.3 = (f32[16,16,256]{2,1,0:T(8,128)}, f32[16,16,256]{2,1,0:T(8,128)}) custom-call(s32[5,32]{1,0:T(8,128)} %maximum_select_fusion.info, f32[1,1,32,256,256]{4,3,2,1,0:T(8,128)} %tiles.15, f32[16,256]{1,0:T(8,128)} %copy-done.13, f32[16,256]{1,0:T(8,128)} %copy-done.24, f32[16,256]{1,0:T(8,128)} %copy-done.21, f32[16,256]{1,0:T(8,128)} %copy-done.18), custom_call_target="tpu_custom_call" | custom-call | flops 400000000 | bytes 8388608 | tf_op jit(solution)/shard_map/rows_next/pallas_call | solution.py:132
  73.7 4.2 %collective-permute-start.11 = (f32[16,16,256]{2,1,0:T(8,128)}, f32[16,16,256]{2,1,0:T(8,128)S(1)}, u32[]{:S(2)}, u32[]{:S(2)}) collective-permute-start(f32[16,16,256]{2,1,0:T(8,128)} %get-tuple-element.55), channel_id=1, source_target_pairs={{0,1},{1,0},{2,3},{3,2},{4,5},{5,4},{6,7},{7,6},{8,9},{9,8},{10,11... | collective-permute-start | bytes 786440 | tf_op jit(solution)/shard_map/ppermute | solution.py:358
  81.0 7.8 %all-to-all-start.2 = ((f32[16,16,256]{2,1,0:T(8,128)}), f32[16,16,256]{2,1,0:T(8,128)S(1)}, u32[]{:S(2)}, u32[]{:S(2)}) async-start(f32[16,16,256]{2,1,0:T(8,128)} %add.93), calls=%async_computation.2 | async-start | bytes 524288 | tf_op jit(solution)/shard_map/all_to_all | solution.py:362
  89.5 5.2 %cols_next.3 = (f32[24,256]{1,0:T(8,128)}, f32[24,256]{1,0:T(8,128)}, f32[24,256]{1,0:T(8,128)}, f32[24,256]{1,0:T(8,128)}) custom-call(s32[5,32]{1,0:T(8,128)} %maximum_select_fusion.info, f32[1,1,32,256,256]{4,3,2,1,0:T(8,128)} %tiles.15, f32[16,24,256]{2,1,0:T(8,128)} %copy-done.1, f32[16,24,256]{2,1,0:T(8,128)} %copy-done.6), custom_call_target="tpu_custom_call" | custom-call | flops 400000000 | bytes 8388608 | tf_op jit(solution)/shard_map/cols_next/pallas_call | solution.py:152
  100.7 4.4 %update_1.1 = (f32[16,24,256]{2,1,0:T(8,128)}, f32[32,512]{1,0:T(8,128)}, f32[16,128]{1,0:T(8,128)}, f32[16,16]{1,0:T(8,128)}, f32[8,128]{1,0:T(8,128)}) custom-call(f32[16,16,256]{2,1,0:T(8,128)} %copy-done.10, f32[24,256]{1,0:T(8,128)} %get-tuple-element.56.refs_1_, f32[24,256]{1,0:T(8,128)} %copy-done.37, f32[24,256]{1,0:T(8,128)} %copy-done.40, ...), custom_call_target="tpu_custom_call" | custom-call | flops 400000000 | bytes 1048576 | tf_op jit(solution)/shard_map/update_1/pallas_call | solution.py:293
  105.1 6.7 %all-to-all-start.5 = ((f32[16,24,256]{2,1,0:T(8,128)}), f32[16,24,256]{2,1,0:T(8,128)S(1)}, u32[]{:S(2)}, u32[]{:S(2)}) async-start(f32[16,24,256]{2,1,0:T(8,128)} %get-tuple-element.62), calls=%async_computation.5 | async-start | bytes 786432 | tf_op jit(solution)/shard_map/all_to_all | solution.py:362
  120.3 5.1 %rows_next.4 = (f32[16,16,256]{2,1,0:T(8,128)}, f32[16,16,256]{2,1,0:T(8,128)}) custom-call(s32[5,32]{1,0:T(8,128)} %maximum_select_fusion.info, f32[1,1,32,256,256]{4,3,2,1,0:T(8,128)} %tiles.15, f32[16,256]{1,0:T(8,128)} %copy-done.14, f32[16,256]{1,0:T(8,128)} %copy-done.25, f32[16,256]{1,0:T(8,128)} %copy-done.22, f32[16,256]{1,0:T(8,128)} %copy-done.19), custom_call_target="tpu_custom_call" | custom-call | flops 400000000 | bytes 8388608 | tf_op jit(solution)/shard_map/rows_next/pallas_call | solution.py:132
  125.5 4.0 %collective-permute-start.19 = (f32[16,16,256]{2,1,0:T(8,128)}, f32[16,16,256]{2,1,0:T(8,128)S(1)}, u32[]{:S(2)}, u32[]{:S(2)}) collective-permute-start(f32[16,16,256]{2,1,0:T(8,128)} %get-tuple-element.64), channel_id=1, source_target_pairs={{0,1},{1,0},{2,3},{3,2},{4,5},{5,4},{6,7},{7,6},{8,9},{9,8},{10,11... | collective-permute-start | bytes 786440 | tf_op jit(solution)/shard_map/ppermute | solution.py:358
  132.5 7.8 %all-to-all-start.4 = ((f32[16,16,256]{2,1,0:T(8,128)}), f32[16,16,256]{2,1,0:T(8,128)S(1)}, u32[]{:S(2)}, u32[]{:S(2)}) async-start(f32[16,16,256]{2,1,0:T(8,128)} %add.94), calls=%async_computation.4 | async-start | bytes 524288 | tf_op jit(solution)/shard_map/all_to_all | solution.py:362
  141.1 5.2 %cols_next.4 = (f32[24,256]{1,0:T(8,128)}, f32[24,256]{1,0:T(8,128)}, f32[24,256]{1,0:T(8,128)}, f32[24,256]{1,0:T(8,128)}) custom-call(s32[5,32]{1,0:T(8,128)} %maximum_select_fusion.info, f32[1,1,32,256,256]{4,3,2,1,0:T(8,128)} %tiles.15, f32[16,24,256]{2,1,0:T(8,128)} %copy-done.2, f32[16,24,256]{2,1,0:T(8,128)} %copy-done.7), custom_call_target="tpu_custom_call" | custom-call | flops 400000000 | bytes 8388608 | tf_op jit(solution)/shard_map/cols_next/pallas_call | solution.py:152
  152.2 4.3 %update_2.1 = (f32[16,24,256]{2,1,0:T(8,128)}, f32[48,512]{1,0:T(8,128)}, f32[16,128]{1,0:T(8,128)}, f32[16,16]{1,0:T(8,128)}) custom-call(f32[16,16,256]{2,1,0:T(8,128)} %copy-done.11, f32[24,256]{1,0:T(8,128)} %get-tuple-element.65.refs_1_, f32[24,256]{1,0:T(8,128)} %copy-done.39, f32[24,256]{1,0:T(8,128)} %copy-done.42, f32[24,256]{1,0:T(8,128)} %copy-done.44, ...), custom_call_target="tpu_custom_call" | custom-call | flops 400000000 | bytes 1048576 | tf_op jit(solution)/shard_map/update_2/pallas_call | solution.py:293
  156.6 14.9 %all_to_all.50.near = f32[16,24,256]{2,1,0:T(8,128)S(1)} all-to-all(f32[16,24,256]{2,1,0:T(8,128)} %get-tuple-element.71), channel_id=1, replica_groups=mesh['grp'=4,'col_0'=4,'col_1'=4,'col_2'=2] {'col_0','col_1'}, dimensions={0} | all-to-all | bytes 786432 | tf_op jit(solution)/shard_map/all_to_all | solution.py:362
  183.6 5.1 %rows_next.5 = (f32[16,16,256]{2,1,0:T(8,128)}, f32[16,16,256]{2,1,0:T(8,128)}) custom-call(s32[5,32]{1,0:T(8,128)} %maximum_select_fusion.info, f32[1,1,32,256,256]{4,3,2,1,0:T(8,128)} %tiles.15, f32[16,256]{1,0:T(8,128)} %copy-done.12, f32[16,256]{1,0:T(8,128)} %copy-done.26, f32[16,256]{1,0:T(8,128)} %copy-done.23, f32[16,256]{1,0:T(8,128)} %copy-done.20), custom_call_target="tpu_custom_call" | custom-call | flops 400000000 | bytes 8388608 | tf_op jit(solution)/shard_map/rows_next/pallas_call | solution.py:132
  197.9 5.2 %cols_next.5 = (f32[24,256]{1,0:T(8,128)}, f32[24,256]{1,0:T(8,128)}, f32[24,256]{1,0:T(8,128)}, f32[24,256]{1,0:T(8,128)}) custom-call(s32[5,32]{1,0:T(8,128)} %maximum_select_fusion.info, f32[1,1,32,256,256]{4,3,2,1,0:T(8,128)} %tiles.15, f32[16,24,256]{2,1,0:T(8,128)} %copy-done.3, f32[16,24,256]{2,1,0:T(8,128)} %copy-done.4), custom_call_target="tpu_custom_call" | custom-call | flops 400000000 | bytes 8388608 | tf_op jit(solution)/shard_map/cols_next/pallas_call | solution.py:152
  209.0 4.4 %update_3.1 = (f32[16,24,256]{2,1,0:T(8,128)}, f32[64,512]{1,0:T(8,128)}, f32[16,128]{1,0:T(8,128)}, f32[16,16]{1,0:T(8,128)}) custom-call(f32[16,16,256]{2,1,0:T(8,128)} %copy-done.9, f32[24,256]{1,0:T(8,128)} %get-tuple-element.74.refs_1_, f32[24,256]{1,0:T(8,128)} %copy-done.36, f32[24,256]{1,0:T(8,128)} %copy-done.38, f32[24,256]{1,0:T(8,128)} %copy-done.41, ...), custom_call_target="tpu_custom_call" | custom-call | flops 400000000 | bytes 1048576 | tf_op jit(solution)/shard_map/update_3/pallas_call | solution.py:293
  214.8 6.5 %all-to-all-start.8 = ((f32[16,1,2048]{2,1,0:T(1,128)}), f32[16,1,2048]{2,1,0:T(1,128)S(1)}, u32[]{:S(2)}, u32[]{:S(2)}) async-start(f32[16,1,2048]{2,1,0:T(1,128)} %broadcast_in_dim.14), calls=%async_computation.8 | async-start | bytes 262144 | tf_op jit(solution)/shard_map/all_to_all | solution.py:362
  221.3 6.8 %all-to-all-done.8 = f32[16,1,2048]{2,1,0:T(1,128)S(1)} async-done(((f32[16,1,2048]{2,1,0:T(1,128)}), f32[16,1,2048]{2,1,0:T(1,128)S(1)}, u32[]{:S(2)}, u32[]{:S(2)}) %all-to-all-start.8) | async-done | bytes 131104 | tf_op jit(solution)/shard_map/all_to_all | solution.py:362
  228.9 8.1 %all-to-all-start.9 = ((f32[8,1,2048]{2,1,0:T(1,128)}), f32[8,1,2048]{2,1,0:T(1,128)S(1)}, u32[]{:S(2)}, u32[]{:S(2)}) async-start(f32[8,1,2048]{2,1,0:T(1,128)} %broadcast_in_dim.15), calls=%async_computation.9 | async-start | bytes 131072 | tf_op jit(solution)/shard_map/all_to_all | solution.py:362
  (192 shorter events, 98.6 us)
Async XLA Ops:
  0.6 16.6 %collective-permute-start.2 = (f32[16,256]{1,0:T(8,128)}, f32[16,256]{1,0:T(8,128)S(1)}, u32[]{:S(2)}, u32[]{:S(2)}) collective-permute-start(f32[16,256]{1,0:T(8,128)} %refs_5_.1), channel_id=1, source_target_pairs={{0,96},{32,0},{64,32},{96,64},{1,97},{33,1},{65,33},{97,65},{2,98}... | collective-permute-start | bytes 49160 | tf_op jit(solution)/shard_map/ppermute | solution.py:354
  4.3 13.0 %collective-permute-start.1 = (f32[16,256]{1,0:T(8,128)}, f32[16,256]{1,0:T(8,128)S(1)}, u32[]{:S(2)}, u32[]{:S(2)}) collective-permute-start(f32[16,256]{1,0:T(8,128)} %refs_5_.1), channel_id=1, source_target_pairs={{0,64},{32,96},{64,0},{96,32},{1,65},{33,97},{65,1},{97,33},{2,66}... | collective-permute-start | bytes 49160 | tf_op jit(solution)/shard_map/ppermute | solution.py:354
  4.6 12.7 %collective-permute-start = (f32[16,256]{1,0:T(8,128)}, f32[16,256]{1,0:T(8,128)S(1)}, u32[]{:S(2)}, u32[]{:S(2)}) collective-permute-start(f32[16,256]{1,0:T(8,128)} %refs_5_.1), channel_id=1, source_target_pairs={{0,32},{32,64},{64,96},{96,0},{1,33},{33,65},{65,97},{97,1},{2,34}... | collective-permute-start | bytes 49160 | tf_op jit(solution)/shard_map/ppermute | solution.py:354
  7.0 18.6 %all-to-all-start.1 = ((f32[16,24,256]{2,1,0:T(8,128)}), f32[16,24,256]{2,1,0:T(8,128)S(1)}, u32[]{:S(2)}, u32[]{:S(2)}) async-start(f32[16,24,256]{2,1,0:T(8,128)} %first_message.1), calls=%async_computation.1 | async-start | bytes 786432 | tf_op jit(solution)/shard_map/all_to_all | solution.py:362
  25.6 11.4 %collective-permute-start.4 = (f32[16,24,256]{2,1,0:T(8,128)S(1)}, f32[16,24,256]{2,1,0:T(8,128)S(1)}, u32[]{:S(2)}, u32[]{:S(2)}) collective-permute-start(f32[16,24,256]{2,1,0:T(8,128)S(1)} %all-to-all-done.1.near), channel_id=1, source_target_pairs={{0,1},{1,0},{2,3},{3,2},{4,5},{5,4},{6,7},{7,6},{8,9},{9,8},{10,11... | collective-permute-start | bytes 1179656 | tf_op jit(solution)/shard_map/ppermute | solution.py:358
  29.0 18.1 %all-to-all-start = ((f32[16,24,256]{2,1,0:T(8,128)}), f32[16,24,256]{2,1,0:T(8,128)S(1)}, u32[]{:S(2)}, u32[]{:S(2)}) async-start(f32[16,24,256]{2,1,0:T(8,128)} %add.92), calls=%async_computation | async-start | bytes 786432 | tf_op jit(solution)/shard_map/all_to_all | solution.py:362
  43.0 4.5 %collective-permute-start.5 = (f32[32,256]{1,0:T(8,128)}, f32[32,256]{1,0:T(8,128)S(1)}, u32[]{:S(2)}, u32[]{:S(2)}) collective-permute-start(f32[32,256]{1,0:T(8,128)} %get-tuple-element.50), channel_id=1, source_target_pairs={{0,32},{32,64},{64,96},{96,0},{1,33},{33,65},{65,97},{97,1},{2,34}... | collective-permute-start | bytes 98312 | tf_op jit(solution)/shard_map/ppermute | solution.py:354
  44.5 4.5 %collective-permute-start.6 = (f32[32,256]{1,0:T(8,128)}, f32[32,256]{1,0:T(8,128)S(1)}, u32[]{:S(2)}, u32[]{:S(2)}) collective-permute-start(f32[32,256]{1,0:T(8,128)} %get-tuple-element.51), channel_id=1, source_target_pairs={{0,64},{32,96},{64,0},{96,32},{1,65},{33,97},{65,1},{97,33},{2,66}... | collective-permute-start | bytes 98312 | tf_op jit(solution)/shard_map/ppermute | solution.py:354
  53.7 24.2 %all-to-all-start.3 = ((f32[16,24,256]{2,1,0:T(8,128)}), f32[16,24,256]{2,1,0:T(8,128)S(1)}, u32[]{:S(2)}, u32[]{:S(2)}) async-start(f32[16,24,256]{2,1,0:T(8,128)} %get-tuple-element.53), calls=%async_computation.3 | async-start | bytes 786432 | tf_op jit(solution)/shard_map/all_to_all | solution.py:362
  73.7 5.5 %collective-permute-start.11 = (f32[16,16,256]{2,1,0:T(8,128)}, f32[16,16,256]{2,1,0:T(8,128)S(1)}, u32[]{:S(2)}, u32[]{:S(2)}) collective-permute-start(f32[16,16,256]{2,1,0:T(8,128)} %get-tuple-element.55), channel_id=1, source_target_pairs={{0,1},{1,0},{2,3},{3,2},{4,5},{5,4},{6,7},{7,6},{8,9},{9,8},{10,11... | collective-permute-start | bytes 786440 | tf_op jit(solution)/shard_map/ppermute | solution.py:358
  77.9 10.9 %collective-permute-start.12 = (f32[16,24,256]{2,1,0:T(8,128)S(1)}, f32[16,24,256]{2,1,0:T(8,128)S(1)}, u32[]{:S(2)}, u32[]{:S(2)}) collective-permute-start(f32[16,24,256]{2,1,0:T(8,128)S(1)} %all-to-all-done.3.near), channel_id=1, source_target_pairs={{0,1},{1,0},{2,3},{3,2},{4,5},{5,4},{6,7},{7,6},{8,9},{9,8},{10,11... | collective-permute-start | bytes 1179656 | tf_op jit(solution)/shard_map/ppermute | solution.py:358
  81.0 16.6 %all-to-all-start.2 = ((f32[16,16,256]{2,1,0:T(8,128)}), f32[16,16,256]{2,1,0:T(8,128)S(1)}, u32[]{:S(2)}, u32[]{:S(2)}) async-start(f32[16,16,256]{2,1,0:T(8,128)} %add.93), calls=%async_computation.2 | async-start | bytes 524288 | tf_op jit(solution)/shard_map/all_to_all | solution.py:362
  94.9 4.5 %collective-permute-start.14 = (f32[24,256]{1,0:T(8,128)}, f32[24,256]{1,0:T(8,128)S(1)}, u32[]{:S(2)}, u32[]{:S(2)}) collective-permute-start(f32[24,256]{1,0:T(8,128)} %get-tuple-element.58), channel_id=1, source_target_pairs={{0,64},{32,96},{64,0},{96,32},{1,65},{33,97},{65,1},{97,33},{2,66}... | collective-permute-start | bytes 73736 | tf_op jit(solution)/shard_map/ppermute | solution.py:354
  95.5 4.6 %collective-permute-start.15 = (f32[24,256]{1,0:T(8,128)}, f32[24,256]{1,0:T(8,128)S(1)}, u32[]{:S(2)}, u32[]{:S(2)}) collective-permute-start(f32[24,256]{1,0:T(8,128)} %get-tuple-element.59), channel_id=1, source_target_pairs={{0,96},{32,0},{64,32},{96,64},{1,97},{33,1},{65,33},{97,65},{2,98}... | collective-permute-start | bytes 73736 | tf_op jit(solution)/shard_map/ppermute | solution.py:354
  105.1 24.4 %all-to-all-start.5 = ((f32[16,24,256]{2,1,0:T(8,128)}), f32[16,24,256]{2,1,0:T(8,128)S(1)}, u32[]{:S(2)}, u32[]{:S(2)}) async-start(f32[16,24,256]{2,1,0:T(8,128)} %get-tuple-element.62), calls=%async_computation.5 | async-start | bytes 786432 | tf_op jit(solution)/shard_map/all_to_all | solution.py:362
  125.5 5.4 %collective-permute-start.19 = (f32[16,16,256]{2,1,0:T(8,128)}, f32[16,16,256]{2,1,0:T(8,128)S(1)}, u32[]{:S(2)}, u32[]{:S(2)}) collective-permute-start(f32[16,16,256]{2,1,0:T(8,128)} %get-tuple-element.64), channel_id=1, source_target_pairs={{0,1},{1,0},{2,3},{3,2},{4,5},{5,4},{6,7},{7,6},{8,9},{9,8},{10,11... | collective-permute-start | bytes 786440 | tf_op jit(solution)/shard_map/ppermute | solution.py:358
  129.4 10.9 %collective-permute-start.20 = (f32[16,24,256]{2,1,0:T(8,128)S(1)}, f32[16,24,256]{2,1,0:T(8,128)S(1)}, u32[]{:S(2)}, u32[]{:S(2)}) collective-permute-start(f32[16,24,256]{2,1,0:T(8,128)S(1)} %all-to-all-done.5.near), channel_id=1, source_target_pairs={{0,1},{1,0},{2,3},{3,2},{4,5},{5,4},{6,7},{7,6},{8,9},{9,8},{10,11... | collective-permute-start | bytes 1179656 | tf_op jit(solution)/shard_map/ppermute | solution.py:358
  132.5 16.6 %all-to-all-start.4 = ((f32[16,16,256]{2,1,0:T(8,128)}), f32[16,16,256]{2,1,0:T(8,128)S(1)}, u32[]{:S(2)}, u32[]{:S(2)}) async-start(f32[16,16,256]{2,1,0:T(8,128)} %add.94), calls=%async_computation.4 | async-start | bytes 524288 | tf_op jit(solution)/shard_map/all_to_all | solution.py:362
  146.7 4.9 %collective-permute-start.23 = (f32[24,256]{1,0:T(8,128)}, f32[24,256]{1,0:T(8,128)S(1)}, u32[]{:S(2)}, u32[]{:S(2)}) collective-permute-start(f32[24,256]{1,0:T(8,128)} %get-tuple-element.68), channel_id=1, source_target_pairs={{0,96},{32,0},{64,32},{96,64},{1,97},{33,1},{65,33},{97,65},{2,98}... | collective-permute-start | bytes 73736 | tf_op jit(solution)/shard_map/ppermute | solution.py:354
  171.5 25.6 %collective-permute-start.28 = (f32[16,24,256]{2,1,0:T(8,128)S(1)}, f32[16,24,256]{2,1,0:T(8,128)S(1)}, u32[]{:S(2)}, u32[]{:S(2)}) collective-permute-start(f32[16,24,256]{2,1,0:T(8,128)S(1)} %all_to_all.50.near), channel_id=1, source_target_pairs={{0,1},{1,0},{2,3},{3,2},{4,5},{5,4},{6,7},{7,6},{8,9},{9,8},{10,11... | collective-permute-start | bytes 1179656 | tf_op jit(solution)/shard_map/ppermute | solution.py:358
  193.4 13.5 %all-to-all-start.6 = ((f32[16,16,256]{2,1,0:T(8,128)}), f32[16,16,256]{2,1,0:T(8,128)S(1)}, u32[]{:S(2)}, u32[]{:S(2)}) async-start(f32[16,16,256]{2,1,0:T(8,128)} %add.95), calls=%async_computation.6 | async-start | bytes 524288 | tf_op jit(solution)/shard_map/all_to_all | solution.py:362
  203.2 4.5 %collective-permute-start.30 = (f32[24,256]{1,0:T(8,128)}, f32[24,256]{1,0:T(8,128)S(1)}, u32[]{:S(2)}, u32[]{:S(2)}) collective-permute-start(f32[24,256]{1,0:T(8,128)} %get-tuple-element.76), channel_id=1, source_target_pairs={{0,64},{32,96},{64,0},{96,32},{1,65},{33,97},{65,1},{97,33},{2,66}... | collective-permute-start | bytes 73736 | tf_op jit(solution)/shard_map/ppermute | solution.py:354
  214.8 13.3 %all-to-all-start.8 = ((f32[16,1,2048]{2,1,0:T(1,128)}), f32[16,1,2048]{2,1,0:T(1,128)S(1)}, u32[]{:S(2)}, u32[]{:S(2)}) async-start(f32[16,1,2048]{2,1,0:T(1,128)} %broadcast_in_dim.14), calls=%async_computation.8 | async-start | bytes 262144 | tf_op jit(solution)/shard_map/all_to_all | solution.py:362
  228.9 12.9 %all-to-all-start.9 = ((f32[8,1,2048]{2,1,0:T(1,128)}), f32[8,1,2048]{2,1,0:T(1,128)S(1)}, u32[]{:S(2)}, u32[]{:S(2)}) async-start(f32[8,1,2048]{2,1,0:T(1,128)} %broadcast_in_dim.15), calls=%async_computation.9 | async-start | bytes 131072 | tf_op jit(solution)/shard_map/all_to_all | solution.py:362
  (62 other events, 478.0 us)
where the time goes:
time: 251 us; the launch traced here: 248 us
  starting transfers between devices  106 us (42%)
  Pallas kernels  60.4 us (24%)
  waiting for transfers between devices  35.4 us (14%)
  local copies, waits for them, and re-layouts  19.6 us (8%)
  blocking collectives  14.9 us (6%)
  other arithmetic  10.5 us (4%)
    all_to_all x9, starting transfers between devices, exchanged(): return lax.all_to_all(value, axes, split_axis=0, concat_axis=0, tiled=True)  62.8 us
    ppermute x24, starting transfers between devices, shifted(): lax.ppermute(value, 'grp', [(i, (i + hop) % size) for i in range(size)])  27.1 us
    pallas_call x4, Pallas kernels, cols_product(): pl.pallas_call(functools.partial(cols_kernel, first), name='cols_first' i...  20.9 us
    pallas_call x4, Pallas kernels, rows_product(): pl.pallas_call(functools.partial(rows_kernel, first), name='rows_first' i...  20.6 us
    ppermute x24, waiting for transfers between devices, shifted(): lax.ppermute(value, 'grp', [(i, (i + hop) % size) for i in range(size)])  20.1 us
    pallas_call x4, Pallas kernels, update(): pl.pallas_call(functools.partial(update_kernel, step, node_total), name=f...  17.2 us
    ppermute x8, starting transfers between devices, swapped(): return lax.ppermute(value, CORE, [(0, 1), (1, 0)])  15.6 us
    all_to_all x1, blocking collectives, exchanged(): return lax.all_to_all(value, axes, split_axis=0, concat_axis=0, tiled=True)  14.9 us
  transfers between devices with their start and end apart: 41, of which 23 were waited for; matrix products, arithmetic and copies ran while one was open for 5% of the time, Pallas kernels for 17%

commit v1 on v0

v1 whole, which is shorter than its diff:
```python
import functools
import jax
import jax.numpy as jnp
from jax import lax
from jax.experimental import pallas as pl
from jax.experimental.pallas import tpu as pltpu
from jax.sharding import Mesh
from jax.sharding import PartitionSpec as P

ITERS = 4
ZX = ("col_0", "col_1")
CORE = "col_2"
COL = ("col_0", "col_1", "col_2")
GRP_COL = ("grp", "col_0", "col_1", "col_2")
GROUP = 8
highest = lax.Precision.HIGHEST
VMEM = pl.BlockSpec(memory_space=pltpu.VMEM)
SMEM = pl.BlockSpec(memory_space=pltpu.SMEM)
HBM = pl.BlockSpec(memory_space=pltpu.MemorySpace.HBM)
MIB = 1 << 20
f32 = jnp.float32
bf16 = jnp.bfloat16


def split(x):
    hi = x.astype(bf16)
    return hi, (x - hi.astype(f32)).astype(bf16)


def dot(a, b, dims):
    return lax.dot_general(a, b, (dims, ((), ())), preferred_element_type=f32)


def dot_f32(a, b, dims):
    return lax.dot_general(a, b, (dims, ((), ())), precision=highest, preferred_element_type=f32)


def limits(mib):
    return pltpu.CompilerParams(vmem_limit_bytes=mib * MIB)


def cost(flops):
    return pl.CostEstimate(flops=flops, bytes_accessed=MIB, transcendentals=0)


def products(lhs_hi, lhs_lo, hi, lo, dims, first, live):
    top = dot(lhs_hi, hi, dims)
    low = dot(lhs_lo, lo, dims)
    out = top[0:16] + top[16:32] + low[0:16]
    if first:
        out = jnp.concatenate([out, top[32:40] + low[16:24]], axis=0)
    return out * live


def stacked_lhs(piece, first):
    hi, lo = split(piece)
    if first:
        ones = jnp.ones((16, piece.shape[1]), bf16)
        return jnp.concatenate([hi, lo, ones], axis=0), jnp.concatenate([hi, ones], axis=0)
    return jnp.concatenate([hi, lo], axis=0), hi


def fill_pieces(pieces, lhs_hi, lhs_lo, first):
    for k, piece in enumerate(pieces):
        lhs_hi[k], lhs_lo[k] = stacked_lhs(piece[...], first)


def group_rows(base, place, lhs_hi, lhs_lo, hi, lo, out, first):
    tile_row, tile_col, tile_count = place
    results = []
    for u in range(GROUP):
        s = base + u
        k = ((tile_row[0, 0, 0] >> 5) - (tile_col[0, 0, s] >> 5)) & 3
        live = (s < tile_count[0, 0]).astype(f32)
        results.append(
            products(lhs_hi[k], lhs_lo[k], hi[s], lo[s], ((1,), (1,)), first, live)
        )
    for u in range(GROUP):
        out[tile_row[0, 0, base + u] & 31] += results[u]


def rows_first_kernel(
    tile_row, tile_col, tile_count, tiles, own, one, two, three, out, hi, lo, buf, lhs_hi, lhs_lo, sems
):
    slots = buf.shape[0]
    copies = [
        pltpu.make_async_copy(
            tiles.at[0, 0, pl.ds(q * GROUP, GROUP)], buf.at[pl.ds(q * GROUP, GROUP)], sems.at[q]
        )
        for q in range(slots // GROUP)
    ]
    for copy in copies:
        copy.start()
    fill_pieces((own, one, two, three), lhs_hi, lhs_lo, True)
    out[...] = jnp.zeros_like(out)
    for q, copy in enumerate(copies):
        copy.wait()
        for u in range(GROUP):
            s = q * GROUP + u
            hi[s], lo[s] = split(buf[s])

        @pl.when(q * GROUP < tile_count[0, 0])
        def _():
            group_rows(
                q * GROUP, (tile_row, tile_col, tile_count), lhs_hi, lhs_lo, hi, lo, out, True
            )


def groups_of(tile_count):
    return (tile_count[0, 0] + (GROUP - 1)) // GROUP


def rows_next_kernel(
    tile_row, tile_col, tile_count, hi, lo, own, one, two, three, out, lhs_hi, lhs_lo
):
    fill_pieces((own, one, two, three), lhs_hi, lhs_lo, False)
    out[...] = jnp.zeros_like(out)

    @pl.loop(0, groups_of(tile_count))
    def _(q):
        group_rows(q * GROUP, (tile_row, tile_col, tile_count), lhs_hi, lhs_lo, hi, lo, out, False)


def cols_kernel(
    first, tile_row, tile_col, tile_count, hi, lo, near, far, own, one, two, three, acc
):
    acc[...] = jnp.zeros_like(acc)
    gram = jnp.zeros_like(near[0, 16:24])
    for p in range(near.shape[0]):
        gram = gram + (near[p, 16:24] + far[p, 16:24])

    @pl.loop(0, groups_of(tile_count))
    def _(q):
        results, slots = [], []
        for u in range(GROUP):
            s = q * GROUP + u
            row = tile_row[0, 0, s] & 31
            place = row >> 1
            same = ((row ^ tile_col[0, 0, 0]) & 1) == 0
            piece = jnp.where(same, near[place, 0:16], far[place, 0:16])
            left_hi, left_lo = stacked_lhs(piece, first)
            live = (s < tile_count[0, 0]).astype(f32)
            results.append(
                products(left_hi, left_lo, hi[s], lo[s], ((1,), (0,)), first, live)
            )
            slots.append(((tile_col[0, 0, s] >> 5) - (tile_row[0, 0, 0] >> 5)) & 3)
        for u in range(GROUP):
            acc[slots[u]] += results[u]

    for k, out in enumerate((own, one, two, three)):
        out[...] = jnp.concatenate([acc[k], gram], axis=0)


def rows_first(place, tiles, pieces):
    slots, size = tiles.shape[2], tiles.shape[3]
    return pl.pallas_call(
        rows_first_kernel,
        name="rows_first",
        out_shape=(
            jax.ShapeDtypeStruct((32, 24, size), f32),
            pltpu.VMEM((slots, size, size), bf16),
            pltpu.VMEM((slots, size, size), bf16),
        ),
        in_specs=[SMEM] * 3 + [HBM] + [VMEM] * 4,
        out_specs=(VMEM,) * 3,
        scratch_shapes=[
            pltpu.VMEM((slots, size, size), f32),
            pltpu.VMEM((4, 48, size), bf16),
            pltpu.VMEM((4, 32, size), bf16),
            pltpu.SemaphoreType.DMA((slots // GROUP,)),
        ],
        compiler_params=limits(28),
        cost_estimate=cost(400_000_000),
    )(*place, tiles, *pieces)


def rows_next(place, hi, lo, pieces):
    size = hi.shape[1]
    return pl.pallas_call(
        rows_next_kernel,
        name="rows_next",
        out_shape=jax.ShapeDtypeStruct((32, 16, size), f32),
        in_specs=[SMEM] * 3 + [VMEM] * 6,
        out_specs=VMEM,
        scratch_shapes=[pltpu.VMEM((4, 32, size), bf16), pltpu.VMEM((4, 16, size), bf16)],
        compiler_params=limits(20),
        cost_estimate=cost(400_000_000),
    )(*place, hi, lo, *pieces)


def cols_product(first, place, hi, lo, near, far):
    height = 24 if first else 16
    size = hi.shape[1]
    out = jax.ShapeDtypeStruct((height + 8, size), f32)
    return pl.pallas_call(
        functools.partial(cols_kernel, first),
        name="cols_first" if first else "cols_next",
        out_shape=(out,) * 4,
        in_specs=[SMEM] * 3 + [VMEM] * 4,
        out_specs=(VMEM,) * 4,
        scratch_shapes=[pltpu.VMEM((4, height, size), f32)],
        compiler_params=limits(20),
        cost_estimate=cost(400_000_000),
    )(*place, hi, lo, near, far)


def unpack_gram(packed):
    return jnp.concatenate([packed[:, 0:128], packed[:, 128:256]], axis=0)


def pack_gram(gram):
    width = gram.shape[1]
    if width < 128:
        gram = jnp.concatenate([gram, jnp.zeros((16, 128 - width), f32)], axis=1)
    return jnp.concatenate([gram[0:8], gram[8:16]], axis=1)


def eye16():
    return (
        lax.broadcasted_iota(jnp.int32, (16, 16), 0) == lax.broadcasted_iota(jnp.int32, (16, 16), 1)
    ).astype(f32)


def factor_and_inverse(gram):
    work = jnp.concatenate([gram, eye16(), jnp.zeros((16, 96), f32)], axis=1)
    rows = lax.broadcasted_iota(jnp.int32, (16, 128), 0)
    lanes = lax.broadcasted_iota(jnp.int32, (16, 128), 1)
    down = jnp.ones((16, 128), f32)
    across = jnp.ones((16, 128), f32)
    lower = jnp.zeros((16, 128), f32)
    for j in range(16):
        column = jnp.broadcast_to(work[:, j : j + 1], (16, 128))
        pivot = jnp.broadcast_to(column[j : j + 1], (16, 128))
        row = jnp.broadcast_to(work[j : j + 1], (16, 128))
        down = jnp.where(rows == j, pivot, down)
        across = jnp.where(lanes == j, pivot, across)
        lower = jnp.where((lanes == j) & (rows >= j), column, lower)
        work = work - jnp.where(rows > j, column / pivot, 0.0) * row
    lower = lower / jnp.sqrt(across)
    inverse = work / jnp.sqrt(down)
    return lower[:, 0:16], inverse[:, 16:32]


def update_kernel(step, node_total, *refs):
    refs = list(refs)
    take = lambda count: [refs.pop(0) for _ in range(count)]
    (arrived,) = take(1)
    own, one, two, three = take(4)
    before, degree = (None, None) if step == 0 else take(2)
    shift_in = take(1)[0] if step > 1 else None
    (start,) = take(1) if step == 0 else (None,)
    outs = refs
    side = own[...] + one[...] + two[...] + three[...]
    height = arrived.shape[1]
    total = side[0:height]
    for p in range(arrived.shape[0]):
        total = total + arrived[p]
    gram = unpack_gram(side[height : height + 8]) * (1.0 / node_total)
    if step == 0:
        packed, piece_out, state, degree_out, lower_out = outs
        level = total[16:17]
        lower, inverse = factor_and_inverse(gram[:, 0:16])
        block = start[...]
        applied = level * block - total[0:16]
        both = dot_f32(inverse, jnp.concatenate([block, applied], axis=1), ((1,), (0,)))
        degree_out[...] = total[16:24]
        stack = both
        new_vectors = both[:, 0:256]
        new_applied = both[:, 256:512]
        state[...] = both
        basis = new_vectors
        lower_out[...] = lower
    else:
        if step == 1:
            packed, piece_out, state, coeff_out, lower_out, shift_out = outs
        else:
            packed, piece_out, state, coeff_out, lower_out = outs
        width = 16 * step
        coeffs = gram[:, 0:width]
        square = gram[:, width : width + 16]
        square = square - dot_f32(coeffs, coeffs, ((1,), (1,)))
        lower, inverse = factor_and_inverse(square)
        stack = before[...]
        newest = stack[width - 16 : width]
        vectors, applied = newest[:, 0:256], newest[:, 256:512]
        level = degree[0:1]
        twice = level * applied - total[0:16]
        coeff_out[...] = jnp.concatenate([coeffs, jnp.zeros((16, 128 - width), f32)], axis=1)
        if step == 1:
            shift = jnp.broadcast_to(
                jnp.sum(coeffs * eye16(), axis=(0, 1), keepdims=True) * (1.0 / 16), (8, 128)
            )
            shift_out[...] = shift
            scalar = shift[0:1, 0:1]
            moved = applied - scalar * vectors
            twice = twice - scalar * applied - scalar * moved
            coeffs = coeffs - scalar * eye16()
            applied = moved
            stack = jnp.concatenate([vectors, applied], axis=1)
        else:
            scalar = shift_in[0:1, 0:1]
            twice = twice - scalar * applied
            coeff_out[:, width - 16 : width] = coeffs[:, width - 16 : width] + scalar * eye16()
        rest = jnp.concatenate([applied, twice], axis=1) - dot_f32(coeffs, stack, ((1,), (0,)))
        both = dot_f32(inverse, rest, ((1,), (0,)))
        state[0:width] = stack
        state[width : width + 16] = both
        lower_out[...] = lower
        new_applied = both[:, 256:512]
        basis = jnp.concatenate([stack[:, 0:256], both[:, 0:256]], axis=0)
    partial = dot_f32(new_applied, jnp.concatenate([basis, new_applied], axis=0), ((1,), (1,)))
    piece_out[...] = new_applied
    gram_rows = pack_gram(partial)
    if step == ITERS - 1:
        for p in range(packed.shape[0]):
            packed[p] = gram_rows
    else:
        message = jnp.concatenate([new_applied, gram_rows], axis=0)
        for p in range(packed.shape[0]):
            packed[p] = message


def update(step, node_total, arrived, sides, state, degree, shift, start):
    size = arrived.shape[2]
    shapes = [
        jax.ShapeDtypeStruct((8, 8, size) if step == ITERS - 1 else (16, 24, size), f32),
        jax.ShapeDtypeStruct((16, size), f32),
        jax.ShapeDtypeStruct((16 * (step + 1), 2 * size), f32),
    ]
    if step == 0:
        shapes += [jax.ShapeDtypeStruct((8, size), f32), jax.ShapeDtypeStruct((16, 16), f32)]
        extra = [start]
    else:
        shapes += [jax.ShapeDtypeStruct((16, 128), f32), jax.ShapeDtypeStruct((16, 16), f32)]
        extra = [state, degree]
        if step == 1:
            shapes.append(jax.ShapeDtypeStruct((8, 128), f32))
        else:
            extra.append(shift)
    args = [arrived, *sides, *extra]
    return pl.pallas_call(
        functools.partial(update_kernel, step, node_total),
        name=f"update_{step}",
        out_shape=tuple(shapes),
        in_specs=[VMEM] * len(args),
        out_specs=(VMEM,) * len(shapes),
        compiler_params=limits(16),
        cost_estimate=cost(400_000_000),
    )(*args)


def fold_kernel(arrived, packed):
    total = arrived[0]
    for p in range(1, arrived.shape[0]):
        total = total + arrived[p]
    for p in range(packed.shape[0]):
        packed[p] = total


def fold(arrived):
    return pl.pallas_call(
        fold_kernel,
        name="fold",
        out_shape=jax.ShapeDtypeStruct((16, 8, arrived.shape[2]), f32),
        in_specs=[VMEM],
        out_specs=VMEM,
        compiler_params=limits(8),
    )(arrived)


def last_kernel(node_total, arrived, state, shift, *refs):
    coeffs_in, lowers_in = refs[0 : ITERS - 1], refs[ITERS - 1 : 2 * ITERS - 1]
    basis_out, coeffs_out, lowers_out = refs[2 * ITERS - 1 :]
    packed = arrived[0]
    for p in range(1, arrived.shape[0]):
        packed = packed + arrived[p]
    gram = unpack_gram(packed) * (1.0 / node_total)
    width = 16 * ITERS
    coeffs = gram[:, 0:width]
    square = gram[:, width : width + 16] - dot_f32(coeffs, coeffs, ((1,), (1,)))
    stack = state[...]
    rest = stack[width - 16 : width, 256:512] - dot_f32(coeffs, stack[:, 0:256], ((1,), (0,)))
    for k in range(ITERS):
        basis_out[k] = stack[16 * k : 16 * k + 16, 0:256]
        lowers_out[k] = lowers_in[k][...]
        for j in range(ITERS):
            if j > k:
                coeffs_out[k, j] = jnp.zeros((16, 16), f32)
            elif k < ITERS - 1:
                coeffs_out[k, j] = coeffs_in[k][:, 16 * j : 16 * j + 16]
            elif j < k:
                coeffs_out[k, j] = coeffs[:, 16 * j : 16 * j + 16]
            else:
                coeffs_out[k, j] = coeffs[:, 16 * j : 16 * j + 16] + shift[0:1, 0:1] * eye16()
    lower, inverse = factor_and_inverse(square)
    basis_out[ITERS] = dot_f32(inverse, rest, ((1,), (0,)))
    lowers_out[ITERS] = lower


def last(node_total, arrived, state, shift, coeffs, lowers):
    args = [arrived, state, shift, *coeffs, *lowers]
    return pl.pallas_call(
        functools.partial(last_kernel, node_total),
        name="last",
        out_shape=(
            jax.ShapeDtypeStruct((ITERS + 1, 16, arrived.shape[2]), f32),
            jax.ShapeDtypeStruct((ITERS, ITERS, 16, 16), f32),
            jax.ShapeDtypeStruct((ITERS + 1, 16, 16), f32),
        ),
        in_specs=[VMEM] * len(args),
        out_specs=(VMEM,) * 3,
        compiler_params=limits(8),
    )(*args)


def first_message_kernel(block, packed):
    partial = dot_f32(block[...], block[...], ((1,), (1,)))
    message = jnp.concatenate([block[...], pack_gram(partial)], axis=0)
    for p in range(packed.shape[0]):
        packed[p] = message


def first_message(block):
    return pl.pallas_call(
        first_message_kernel,
        name="first_message",
        out_shape=jax.ShapeDtypeStruct((16, 24, block.shape[1]), f32),
        in_specs=[VMEM],
        out_specs=VMEM,
        compiler_params=limits(8),
    )(block)


def shifted(value, hop):
    size = lax.axis_size("grp")
    return lax.ppermute(value, "grp", [(i, (i + hop) % size) for i in range(size)])


def swapped(value):
    return lax.ppermute(value, CORE, [(0, 1), (1, 0)])


def exchanged(value, axes):
    return lax.all_to_all(value, axes, split_axis=0, concat_axis=0, tiled=True)


def body(start_block, tile_values, tile_row, tile_col, tile_count):
    grp_size = lax.axis_size("grp")
    node_total = float(start_block.shape[1] * grp_size * lax.axis_size(COL))
    place = (tile_row, tile_col, tile_count)
    message = first_message(start_block)
    piece = start_block
    state = degree = shift = hi = lo = None
    lowers, coeffs = [], []
    for step in range(ITERS):
        first = step == 0
        pieces = [piece] + [shifted(piece, hop) for hop in range(1, grp_size)]
        near = exchanged(message, ZX)
        if first:
            rows, hi, lo = rows_first(place, tile_values, pieces)
        else:
            rows = rows_next(place, hi, lo, pieces)
        far = swapped(near)
        arrived = exchanged(rows, COL)
        sides = cols_product(first, place, hi, lo, near, far)
        sides = [sides[0]] + [shifted(sides[hop], hop) for hop in range(1, grp_size)]
        outs = update(step, node_total, arrived, sides, state, degree, shift, start_block)
        message, piece, state = outs[0:3]
        if first:
            degree = outs[3]
        else:
            coeffs.append(outs[3])
        lowers.append(outs[4])
        if step == 1:
            shift = outs[5]
    packed = fold(exchanged(message, ("col_1", "col_2")))
    packed = exchanged(packed, ("grp", "col_0"))
    return last(node_total, packed, state, shift, coeffs, lowers)


def solution(mesh):
    split_mesh = Mesh(
        mesh.devices.reshape(mesh.shape["grp"], 4, 4, 2), ("grp", "col_0", "col_1", "col_2")
    )
    placed = (
        P(None, GRP_COL),
        P("grp", COL, None, None, None),
        P("grp", COL, None),
        P("grp", COL, None),
        P("grp", COL),
    )
    return jax.shard_map(
        body,
        mesh=split_mesh,
        in_specs=placed,
        out_specs=(P(None, None, GRP_COL), P(), P()),
        check_vma=False,
    )
```

time: 251 us -> 237 us (0.944)
  local copies, waits for them, and re-layouts: 19.6 us -> 40.8 us
  Pallas kernels: 60.4 us -> 40.1 us
  waiting for transfers between devices: 35.4 us -> 21.8 us
  other arithmetic: 10.5 us -> 0 us
  blocking collectives: 14.9 us -> 22.9 us
    unnamed x98 -> x48, local copies, waits for them, and re-layouts: 11.2 us -> 40.8 us
    ppermute x8 -> x4, starting transfers between devices: 15.6 us -> 1.26 us  [swapped(): return lax.ppermute(value, CORE, [(0, 1), (1, 0)])]
    pallas_call x4, Pallas kernels: 20.9 us -> 7.52 us  [cols_product(): pl.pallas_call(functools.partial(cols_kernel, first), name='cols_first' i...]
    all_to_all x9 -> x8, starting transfers between devices: 62.8 us -> 72.2 us  [exchanged(): return lax.all_to_all(value, axes, split_axis=0, concat_axis=0, tiled=True)]
    all_to_all x9 -> x8, waiting for transfers between devices: 10.1 us -> 1.67 us  [exchanged(): return lax.all_to_all(value, axes, split_axis=0, concat_axis=0, tiled=True)]
    all_to_all x1 -> x2, blocking collectives: 14.9 us -> 22.9 us  [exchanged(): return lax.all_to_all(value, axes, split_axis=0, concat_axis=0, tiled=True)]
    add x4 -> x0, other arithmetic: 6.88 us -> none  [body(): rows = mine + swapped(other)]
    ppermute x24, starting transfers between devices: 27.1 us -> 34 us  [shifted(): lax.ppermute(value, 'grp', [(i, (i + hop) % size) for i in range(size)])]
  transfers between devices with their start and end apart: 41 -> 36, of which waited for: 23 -> 21; matrix products, arithmetic and copies ran while one was open for 5% -> 0% of each run, Pallas kernels for 17% -> 10%
where the time goes in v1:
time: 237 us; the launch traced here: 235 us
  starting transfers between devices  107 us (45%)
  local copies, waits for them, and re-layouts  40.8 us (17%)
  Pallas kernels  40.1 us (17%)
  blocking collectives  22.9 us (10%)
  waiting for transfers between devices  21.8 us (9%)
    all_to_all x8, starting transfers between devices, exchanged(): return lax.all_to_all(value, axes, split_axis=0, concat_axis=0, tiled=True)  72.2 us
    unnamed x48, local copies, waits for them, and re-layouts  40.8 us
    ppermute x24, starting transfers between devices, shifted(): lax.ppermute(value, 'grp', [(i, (i + hop) % size) for i in range(size)])  34 us
    all_to_all x2, blocking collectives, exchanged(): return lax.all_to_all(value, axes, split_axis=0, concat_axis=0, tiled=True)  22.9 us
    ppermute x24, waiting for transfers between devices, shifted(): lax.ppermute(value, 'grp', [(i, (i + hop) % size) for i in range(size)])  14.2 us
    pallas_call x4, Pallas kernels, update(): pl.pallas_call(functools.partial(update_kernel, step, node_total), name=f...  12.7 us
    pallas_call x3, Pallas kernels, rows_next(): pl.pallas_call(rows_next_kernel, name='rows_next', out_shape=jax.ShapeDty...  10.4 us
    pallas_call x4, Pallas kernels, cols_product(): pl.pallas_call(functools.partial(cols_kernel, first), name='cols_first' i...  7.52 us
  transfers between devices with their start and end apart: 36, of which 21 were waited for; matrix products, arithmetic and copies ran while one was open for 0% of the time, Pallas kernels for 10%

profile of v1, /device:TPU:1, one launch (start us, length us, event | category | flops | bytes accessed | tf_op | source)
XLA Modules:
  0.0 234.6 jit_solution(2348909490474931187)
XLA Ops:
  2.3 8.4 %all-to-all-start.1 = ((f32[16,24,256]{2,1,0:T(8,128)}), f32[16,24,256]{2,1,0:T(8,128)S(1)}, u32[]{:S(2)}, u32[]{:S(2)}) async-start(f32[16,24,256]{2,1,0:T(8,128)} %first_message.1), calls=%async_computation.1 | async-start | bytes 786432 | tf_op jit(solution)/shard_map/all_to_all | solution.py:444
  17.8 3.4 %copy-done.16 = f32[1,1,32,256,256]{4,3,2,1,0:T(8,128)S(1)} copy-done((f32[1,1,32,256,256]{4,3,2,1,0:T(8,128)S(1)}, f32[1,1,32,256,256]{4,3,2,1,0:T(8,128)}, u32[]{:S(2)}) %copy-start.16) | copy-done | bytes 8388632
  23.2 5.6 %rows_first.1 = (f32[32,24,256]{2,1,0:T(8,128)}, bf16[32,256,256]{2,1,0:T(8,128)(2,1)S(1)}, bf16[32,256,256]{2,1,0:T(8,128)(2,1)S(1)}) custom-call(s32[1,1,32]{2,1,0:T(1,128)S(1)} %copy-done.20, s32[1,1,32]{2,1,0:T(1,128)S(1)} %copy-done.22, s32[1,1]{1,0:T(1,128)S(6)} %copy.8.tile_count, f32[1,1,32,256,256]{4,3,2,1,0:T(8,128)S(1)} %copy-done.16, ...), custom_call_target="tpu_custom_call" | custom-call | flops 400000000 | bytes 1048576 | tf_op jit(solution)/shard_map/rows_first/pallas_call | solution.py:156
  32.8 9.7 %all-to-all-start = ((f32[32,24,256]{2,1,0:T(8,128)}), f32[32,24,256]{2,1,0:T(8,128)S(1)}, u32[]{:S(2)}, u32[]{:S(2)}) async-start(f32[32,24,256]{2,1,0:T(8,128)} %get-tuple-element.44), calls=%async_computation | async-start | bytes 1572864 | tf_op jit(solution)/shard_map/all_to_all | solution.py:444
  50.8 4.0 %collective-permute-start.5 = (f32[32,256]{1,0:T(8,128)S(1)}, f32[32,256]{1,0:T(8,128)S(1)}, u32[]{:S(2)}, u32[]{:S(2)}) collective-permute-start(f32[32,256]{1,0:T(8,128)S(1)} %get-tuple-element.47), channel_id=1, source_target_pairs={{0,64},{32,96},{64,0},{96,32},{1,65},{33,97},{65,1},{97,33},{2,66}... | collective-permute-start | bytes 98312 | tf_op jit(solution)/shard_map/ppermute | solution.py:436
  57.9 3.0 %update_0.1 = (f32[16,24,256]{2,1,0:T(8,128)}, f32[16,256]{1,0:T(8,128)S(1)}, f32[16,512]{1,0:T(8,128)S(1)}, f32[8,256]{1,0:T(8,128)S(1)}, f32[16,16]{1,0:T(8,128)S(1)}) custom-call(f32[32,24,256]{2,1,0:T(8,128)S(1)} %all-to-all-done.refs_0_, f32[32,256]{1,0:T(8,128)S(1)} %get-tuple-element.45.refs_1_, f32[32,256]{1,0:T(8,128)S(1)} %collective-permute-done.4.refs_2_, ...), custom_call_target="tpu_custom_call" | custom-call | flops 400000000 | bytes 1048576 | tf_op jit(solution)/shard_map/update_0/pallas_call | solution.py:341
  60.9 6.6 %all-to-all-start.3 = ((f32[16,24,256]{2,1,0:T(8,128)}), f32[16,24,256]{2,1,0:T(8,128)S(1)}, u32[]{:S(2)}, u32[]{:S(2)}) async-start(f32[16,24,256]{2,1,0:T(8,128)} %get-tuple-element.50), calls=%async_computation.3 | async-start | bytes 786432 | tf_op jit(solution)/shard_map/all_to_all | solution.py:444
  77.0 3.5 %rows_next.3 = f32[32,16,256]{2,1,0:T(8,128)} custom-call(s32[1,1,32]{2,1,0:T(1,128)S(1)} %copy-done.21, s32[1,1,32]{2,1,0:T(1,128)S(1)} %copy-done.23, s32[1,1]{1,0:T(1,128)S(6)} %copy.8.tile_count, bf16[32,256,256]{2,1,0:T(8,128)(2,1)S(1)} %copy-done.2, bf16[32,256,256]{2,1,0:T(8,128)(2,1)S(1)} %copy-done.10, f32[16,256]{1,0:T(8,128)S(1)} %get-tuple-element.49.own, ...), custom_call_target="tpu_custom_call" | custom-call | flops 400000000 | bytes 1048576 | tf_op jit(solution)/shard_map/rows_next/pallas_call | solution.py:179
  80.5 11.4 %all-to-all-start.2 = ((f32[32,16,256]{2,1,0:T(8,128)}), f32[32,16,256]{2,1,0:T(8,128)S(1)}, u32[]{:S(2)}, u32[]{:S(2)}) async-start(f32[32,16,256]{2,1,0:T(8,128)} %rows_next.3), calls=%async_computation.2 | async-start | bytes 1048576 | tf_op jit(solution)/shard_map/all_to_all | solution.py:444
  101.0 3.0 %collective-permute-start.12 = (f32[24,256]{1,0:T(8,128)S(1)}, f32[24,256]{1,0:T(8,128)S(1)}, u32[]{:S(2)}, u32[]{:S(2)}) collective-permute-start(f32[24,256]{1,0:T(8,128)S(1)} %get-tuple-element.53), channel_id=1, source_target_pairs={{0,64},{32,96},{64,0},{96,32},{1,65},{33,97},{65,1},{97,33},{2,66}... | collective-permute-start | bytes 73736 | tf_op jit(solution)/shard_map/ppermute | solution.py:436
  106.9 3.4 %update_1.1 = (f32[16,24,256]{2,1,0:T(8,128)}, f32[16,256]{1,0:T(8,128)S(1)}, f32[32,512]{1,0:T(8,128)S(1)}, f32[16,128]{1,0:T(8,128)S(1)}, f32[16,16]{1,0:T(8,128)S(1)}, /*index=5*/f32[8,128]{1,0:T(8,128)S(1)}) custom-call(f32[32,16,256]{2,1,0:T(8,128)S(1)} %all-to-all-done.2.refs_0_, f32[24,256]{1,0:T(8,128)S(1)} %get-tuple-element.51.refs_1_, ...), custom_call_target="tpu_custom_call" | custom-call | flops 400000000 | bytes 1048576 | tf_op jit(solution)/shard_map/update_1/pallas_call | solution.py:341
  110.3 6.6 %all-to-all-start.5 = ((f32[16,24,256]{2,1,0:T(8,128)}), f32[16,24,256]{2,1,0:T(8,128)S(1)}, u32[]{:S(2)}, u32[]{:S(2)}) async-start(f32[16,24,256]{2,1,0:T(8,128)} %get-tuple-element.58), calls=%async_computation.5 | async-start | bytes 786432 | tf_op jit(solution)/shard_map/all_to_all | solution.py:444
  126.4 3.5 %rows_next.4 = f32[32,16,256]{2,1,0:T(8,128)} custom-call(s32[1,1,32]{2,1,0:T(1,128)S(1)} %copy-done.21, s32[1,1,32]{2,1,0:T(1,128)S(1)} %copy-done.23, s32[1,1]{1,0:T(1,128)S(6)} %copy.8.tile_count, bf16[32,256,256]{2,1,0:T(8,128)(2,1)S(1)} %copy-done.4, bf16[32,256,256]{2,1,0:T(8,128)(2,1)S(1)} %copy-done.12, f32[16,256]{1,0:T(8,128)S(1)} %get-tuple-element.57.own, ...), custom_call_target="tpu_custom_call" | custom-call | flops 400000000 | bytes 1048576 | tf_op jit(solution)/shard_map/rows_next/pallas_call | solution.py:179
  129.9 11.4 %all-to-all-start.4 = ((f32[32,16,256]{2,1,0:T(8,128)}), f32[32,16,256]{2,1,0:T(8,128)S(1)}, u32[]{:S(2)}, u32[]{:S(2)}) async-start(f32[32,16,256]{2,1,0:T(8,128)} %rows_next.4), calls=%async_computation.4 | async-start | bytes 1048576 | tf_op jit(solution)/shard_map/all_to_all | solution.py:444
  150.4 3.0 %collective-permute-start.19 = (f32[24,256]{1,0:T(8,128)S(1)}, f32[24,256]{1,0:T(8,128)S(1)}, u32[]{:S(2)}, u32[]{:S(2)}) collective-permute-start(f32[24,256]{1,0:T(8,128)S(1)} %get-tuple-element.61), channel_id=1, source_target_pairs={{0,64},{32,96},{64,0},{96,32},{1,65},{33,97},{65,1},{97,33},{2,66}... | collective-permute-start | bytes 73736 | tf_op jit(solution)/shard_map/ppermute | solution.py:436
  156.3 3.3 %update_2.1 = (f32[16,24,256]{2,1,0:T(8,128)}, f32[16,256]{1,0:T(8,128)S(1)}, f32[48,512]{1,0:T(8,128)S(1)}, f32[16,128]{1,0:T(8,128)S(1)}, f32[16,16]{1,0:T(8,128)S(1)}) custom-call(f32[32,16,256]{2,1,0:T(8,128)S(1)} %all-to-all-done.4.refs_0_, f32[24,256]{1,0:T(8,128)S(1)} %get-tuple-element.59.refs_1_, f32[24,256]{1,0:T(8,128)S(1)} %collective-permute-done.18.refs_2_, ...), custom_call_target="tpu_custom_call" | custom-call | flops 400000000 | bytes 1048576 | tf_op jit(solution)/shard_map/update_2/pallas_call | solution.py:341
  159.6 6.6 %all-to-all-start.7 = ((f32[16,24,256]{2,1,0:T(8,128)}), f32[16,24,256]{2,1,0:T(8,128)S(1)}, u32[]{:S(2)}, u32[]{:S(2)}) async-start(f32[16,24,256]{2,1,0:T(8,128)} %get-tuple-element.66), calls=%async_computation.7 | async-start | bytes 786432 | tf_op jit(solution)/shard_map/all_to_all | solution.py:444
  175.7 3.5 %rows_next.5 = f32[32,16,256]{2,1,0:T(8,128)} custom-call(s32[1,1,32]{2,1,0:T(1,128)S(1)} %copy-done.21, s32[1,1,32]{2,1,0:T(1,128)S(1)} %copy-done.23, s32[1,1]{1,0:T(1,128)S(6)} %copy.8.tile_count, bf16[32,256,256]{2,1,0:T(8,128)(2,1)S(1)} %copy-done.6, bf16[32,256,256]{2,1,0:T(8,128)(2,1)S(1)} %copy-done.14, f32[16,256]{1,0:T(8,128)S(1)} %get-tuple-element.65.own, ...), custom_call_target="tpu_custom_call" | custom-call | flops 400000000 | bytes 1048576 | tf_op jit(solution)/shard_map/rows_next/pallas_call | solution.py:179
  179.2 11.4 %all-to-all-start.6 = ((f32[32,16,256]{2,1,0:T(8,128)}), f32[32,16,256]{2,1,0:T(8,128)S(1)}, u32[]{:S(2)}, u32[]{:S(2)}) async-start(f32[32,16,256]{2,1,0:T(8,128)} %rows_next.5), calls=%async_computation.6 | async-start | bytes 1048576 | tf_op jit(solution)/shard_map/all_to_all | solution.py:444
  199.8 3.0 %collective-permute-start.26 = (f32[24,256]{1,0:T(8,128)S(1)}, f32[24,256]{1,0:T(8,128)S(1)}, u32[]{:S(2)}, u32[]{:S(2)}) collective-permute-start(f32[24,256]{1,0:T(8,128)S(1)} %get-tuple-element.69), channel_id=1, source_target_pairs={{0,64},{32,96},{64,0},{96,32},{1,65},{33,97},{65,1},{97,33},{2,66}... | collective-permute-start | bytes 73736 | tf_op jit(solution)/shard_map/ppermute | solution.py:436
  205.7 3.0 %update_3.1 = (f32[8,8,256]{2,1,0:T(8,128)S(1)}, f32[16,256]{1,0:T(8,128)}, f32[64,512]{1,0:T(8,128)S(1)}, f32[16,128]{1,0:T(8,128)S(1)}, f32[16,16]{1,0:T(8,128)S(1)}) custom-call(f32[32,16,256]{2,1,0:T(8,128)S(1)} %all-to-all-done.6.refs_0_, f32[24,256]{1,0:T(8,128)S(1)} %get-tuple-element.67.refs_1_, f32[24,256]{1,0:T(8,128)S(1)} %collective-permute-done.25.refs_2_, ...), custom_call_target="tpu_custom_call" | custom-call | flops 400000000 | bytes 1048576 | tf_op jit(solution)/shard_map/update_3/pallas_call | solution.py:341
  208.6 10.9 %all_to_all.50.arrived = f32[8,8,256]{2,1,0:T(8,128)S(1)} all-to-all(f32[8,8,256]{2,1,0:T(8,128)S(1)} %get-tuple-element.72), channel_id=1, replica_groups=mesh['grp'=4,'col_0'=4,'col_1'=4,'col_2'=2] {'col_1','col_2'}, dimensions={0} | all-to-all | bytes 131072 | tf_op jit(solution)/shard_map/all_to_all | solution.py:444
  219.6 12.0 %all_to_all.51.arrived = f32[16,8,256]{2,1,0:T(8,128)S(1)} all-to-all(f32[16,8,256]{2,1,0:T(8,128)S(1)} %fold.1), channel_id=1, replica_groups=mesh['grp'=4,'col_0'=4,'col_1'=4,'col_2'=2] {'grp','col_0'}, dimensions={0} | all-to-all | bytes 262144 | tf_op jit(solution)/shard_map/all_to_all | solution.py:444
  231.6 3.0 %last.1 = (f32[5,16,256]{2,1,0:T(8,128)}, f32[4,4,16,16]{3,2,1,0:T(8,128)}, f32[5,16,16]{2,1,0:T(8,128)}) custom-call(f32[16,8,256]{2,1,0:T(8,128)S(1)} %all_to_all.51.arrived, f32[64,512]{1,0:T(8,128)S(1)} %get-tuple-element.73.state, f32[8,128]{1,0:T(8,128)S(1)} %get-tuple-element.64.refs_7_.shift, f32[16,128]{1,0:T(8,128)S(1)} %get-tuple-element.74.refs_0_, ...), custom_call_target="tpu_custom_call" | custom-call | tf_op jit(solution)/shard_map/last/pallas_call | solution.py:402
  (113 shorter events, 90.0 us)
Async XLA Ops:
  2.3 30.5 %all-to-all-start.1 = ((f32[16,24,256]{2,1,0:T(8,128)}), f32[16,24,256]{2,1,0:T(8,128)S(1)}, u32[]{:S(2)}, u32[]{:S(2)}) async-start(f32[16,24,256]{2,1,0:T(8,128)} %first_message.1), calls=%async_computation.1 | async-start | bytes 786432 | tf_op jit(solution)/shard_map/all_to_all | solution.py:444
  10.7 5.7 %collective-permute-start = (f32[16,256]{1,0:T(8,128)}, f32[16,256]{1,0:T(8,128)S(1)}, u32[]{:S(2)}, u32[]{:S(2)}) collective-permute-start(f32[16,256]{1,0:T(8,128)} %refs_5_.1), channel_id=1, source_target_pairs={{0,32},{32,64},{64,96},{96,0},{1,33},{33,65},{65,97},{97,1},{2,34}... | collective-permute-start | bytes 49160 | tf_op jit(solution)/shard_map/ppermute | solution.py:436
  12.1 4.4 %collective-permute-start.1 = (f32[16,256]{1,0:T(8,128)}, f32[16,256]{1,0:T(8,128)S(1)}, u32[]{:S(2)}, u32[]{:S(2)}) collective-permute-start(f32[16,256]{1,0:T(8,128)} %refs_5_.1), channel_id=1, source_target_pairs={{0,64},{32,96},{64,0},{96,32},{1,65},{33,97},{65,1},{97,33},{2,66}... | collective-permute-start | bytes 49160 | tf_op jit(solution)/shard_map/ppermute | solution.py:436
  32.8 24.0 %all-to-all-start = ((f32[32,24,256]{2,1,0:T(8,128)}), f32[32,24,256]{2,1,0:T(8,128)S(1)}, u32[]{:S(2)}, u32[]{:S(2)}) async-start(f32[32,24,256]{2,1,0:T(8,128)} %get-tuple-element.44), calls=%async_computation | async-start | bytes 1572864 | tf_op jit(solution)/shard_map/all_to_all | solution.py:444
  50.7 6.1 %collective-permute-start.4 = (f32[32,256]{1,0:T(8,128)S(1)}, f32[32,256]{1,0:T(8,128)S(1)}, u32[]{:S(2)}, u32[]{:S(2)}) collective-permute-start(f32[32,256]{1,0:T(8,128)S(1)} %get-tuple-element.46), channel_id=1, source_target_pairs={{0,32},{32,64},{64,96},{96,0},{1,33},{33,65},{65,97},{97,1},{2,34}... | collective-permute-start | bytes 98312 | tf_op jit(solution)/shard_map/ppermute | solution.py:436
  50.8 6.0 %collective-permute-start.5 = (f32[32,256]{1,0:T(8,128)S(1)}, f32[32,256]{1,0:T(8,128)S(1)}, u32[]{:S(2)}, u32[]{:S(2)}) collective-permute-start(f32[32,256]{1,0:T(8,128)S(1)} %get-tuple-element.47), channel_id=1, source_target_pairs={{0,64},{32,96},{64,0},{96,32},{1,65},{33,97},{65,1},{97,33},{2,66}... | collective-permute-start | bytes 98312 | tf_op jit(solution)/shard_map/ppermute | solution.py:436
  60.9 19.6 %all-to-all-start.3 = ((f32[16,24,256]{2,1,0:T(8,128)}), f32[16,24,256]{2,1,0:T(8,128)S(1)}, u32[]{:S(2)}, u32[]{:S(2)}) async-start(f32[16,24,256]{2,1,0:T(8,128)} %get-tuple-element.50), calls=%async_computation.3 | async-start | bytes 786432 | tf_op jit(solution)/shard_map/all_to_all | solution.py:444
  67.5 4.1 %collective-permute-start.7 = (f32[16,256]{1,0:T(8,128)S(1)}, f32[16,256]{1,0:T(8,128)S(1)}, u32[]{:S(2)}, u32[]{:S(2)}) collective-permute-start(f32[16,256]{1,0:T(8,128)S(1)} %get-tuple-element.49.own), channel_id=1, source_target_pairs={{0,32},{32,64},{64,96},{96,0},{1,33},{33,65},{65,97},{97,1},{2,34}... | collective-permute-start | bytes 49160 | tf_op jit(solution)/shard_map/ppermute | solution.py:436
  67.6 4.2 %collective-permute-start.8 = (f32[16,256]{1,0:T(8,128)S(1)}, f32[16,256]{1,0:T(8,128)S(1)}, u32[]{:S(2)}, u32[]{:S(2)}) collective-permute-start(f32[16,256]{1,0:T(8,128)S(1)} %get-tuple-element.49.own), channel_id=1, source_target_pairs={{0,64},{32,96},{64,0},{96,32},{1,65},{33,97},{65,1},{97,33},{2,66}... | collective-permute-start | bytes 49160 | tf_op jit(solution)/shard_map/ppermute | solution.py:436
  80.5 23.8 %all-to-all-start.2 = ((f32[32,16,256]{2,1,0:T(8,128)}), f32[32,16,256]{2,1,0:T(8,128)S(1)}, u32[]{:S(2)}, u32[]{:S(2)}) async-start(f32[32,16,256]{2,1,0:T(8,128)} %rows_next.3), calls=%async_computation.2 | async-start | bytes 1048576 | tf_op jit(solution)/shard_map/all_to_all | solution.py:444
  99.9 4.4 %collective-permute-start.11 = (f32[24,256]{1,0:T(8,128)S(1)}, f32[24,256]{1,0:T(8,128)S(1)}, u32[]{:S(2)}, u32[]{:S(2)}) collective-permute-start(f32[24,256]{1,0:T(8,128)S(1)} %get-tuple-element.52), channel_id=1, source_target_pairs={{0,32},{32,64},{64,96},{96,0},{1,33},{33,65},{65,97},{97,1},{2,34}... | collective-permute-start | bytes 73736 | tf_op jit(solution)/shard_map/ppermute | solution.py:436
  101.0 4.5 %collective-permute-start.12 = (f32[24,256]{1,0:T(8,128)S(1)}, f32[24,256]{1,0:T(8,128)S(1)}, u32[]{:S(2)}, u32[]{:S(2)}) collective-permute-start(f32[24,256]{1,0:T(8,128)S(1)} %get-tuple-element.53), channel_id=1, source_target_pairs={{0,64},{32,96},{64,0},{96,32},{1,65},{33,97},{65,1},{97,33},{2,66}... | collective-permute-start | bytes 73736 | tf_op jit(solution)/shard_map/ppermute | solution.py:436
  110.3 19.6 %all-to-all-start.5 = ((f32[16,24,256]{2,1,0:T(8,128)}), f32[16,24,256]{2,1,0:T(8,128)S(1)}, u32[]{:S(2)}, u32[]{:S(2)}) async-start(f32[16,24,256]{2,1,0:T(8,128)} %get-tuple-element.58), calls=%async_computation.5 | async-start | bytes 786432 | tf_op jit(solution)/shard_map/all_to_all | solution.py:444
  116.9 3.9 %collective-permute-start.14 = (f32[16,256]{1,0:T(8,128)S(1)}, f32[16,256]{1,0:T(8,128)S(1)}, u32[]{:S(2)}, u32[]{:S(2)}) collective-permute-start(f32[16,256]{1,0:T(8,128)S(1)} %get-tuple-element.57.own), channel_id=1, source_target_pairs={{0,32},{32,64},{64,96},{96,0},{1,33},{33,65},{65,97},{97,1},{2,34}... | collective-permute-start | bytes 49160 | tf_op jit(solution)/shard_map/ppermute | solution.py:436
  117.0 4.2 %collective-permute-start.15 = (f32[16,256]{1,0:T(8,128)S(1)}, f32[16,256]{1,0:T(8,128)S(1)}, u32[]{:S(2)}, u32[]{:S(2)}) collective-permute-start(f32[16,256]{1,0:T(8,128)S(1)} %get-tuple-element.57.own), channel_id=1, source_target_pairs={{0,64},{32,96},{64,0},{96,32},{1,65},{33,97},{65,1},{97,33},{2,66}... | collective-permute-start | bytes 49160 | tf_op jit(solution)/shard_map/ppermute | solution.py:436
  129.9 23.8 %all-to-all-start.4 = ((f32[32,16,256]{2,1,0:T(8,128)}), f32[32,16,256]{2,1,0:T(8,128)S(1)}, u32[]{:S(2)}, u32[]{:S(2)}) async-start(f32[32,16,256]{2,1,0:T(8,128)} %rows_next.4), calls=%async_computation.4 | async-start | bytes 1048576 | tf_op jit(solution)/shard_map/all_to_all | solution.py:444
  149.3 4.4 %collective-permute-start.18 = (f32[24,256]{1,0:T(8,128)S(1)}, f32[24,256]{1,0:T(8,128)S(1)}, u32[]{:S(2)}, u32[]{:S(2)}) collective-permute-start(f32[24,256]{1,0:T(8,128)S(1)} %get-tuple-element.60), channel_id=1, source_target_pairs={{0,32},{32,64},{64,96},{96,0},{1,33},{33,65},{65,97},{97,1},{2,34}... | collective-permute-start | bytes 73736 | tf_op jit(solution)/shard_map/ppermute | solution.py:436
  150.4 4.5 %collective-permute-start.19 = (f32[24,256]{1,0:T(8,128)S(1)}, f32[24,256]{1,0:T(8,128)S(1)}, u32[]{:S(2)}, u32[]{:S(2)}) collective-permute-start(f32[24,256]{1,0:T(8,128)S(1)} %get-tuple-element.61), channel_id=1, source_target_pairs={{0,64},{32,96},{64,0},{96,32},{1,65},{33,97},{65,1},{97,33},{2,66}... | collective-permute-start | bytes 73736 | tf_op jit(solution)/shard_map/ppermute | solution.py:436
  159.6 19.6 %all-to-all-start.7 = ((f32[16,24,256]{2,1,0:T(8,128)}), f32[16,24,256]{2,1,0:T(8,128)S(1)}, u32[]{:S(2)}, u32[]{:S(2)}) async-start(f32[16,24,256]{2,1,0:T(8,128)} %get-tuple-element.66), calls=%async_computation.7 | async-start | bytes 786432 | tf_op jit(solution)/shard_map/all_to_all | solution.py:444
  166.3 3.9 %collective-permute-start.21 = (f32[16,256]{1,0:T(8,128)S(1)}, f32[16,256]{1,0:T(8,128)S(1)}, u32[]{:S(2)}, u32[]{:S(2)}) collective-permute-start(f32[16,256]{1,0:T(8,128)S(1)} %get-tuple-element.65.own), channel_id=1, source_target_pairs={{0,32},{32,64},{64,96},{96,0},{1,33},{33,65},{65,97},{97,1},{2,34}... | collective-permute-start | bytes 49160 | tf_op jit(solution)/shard_map/ppermute | solution.py:436
  166.3 4.2 %collective-permute-start.22 = (f32[16,256]{1,0:T(8,128)S(1)}, f32[16,256]{1,0:T(8,128)S(1)}, u32[]{:S(2)}, u32[]{:S(2)}) collective-permute-start(f32[16,256]{1,0:T(8,128)S(1)} %get-tuple-element.65.own), channel_id=1, source_target_pairs={{0,64},{32,96},{64,0},{96,32},{1,65},{33,97},{65,1},{97,33},{2,66}... | collective-permute-start | bytes 49160 | tf_op jit(solution)/shard_map/ppermute | solution.py:436
  179.2 23.8 %all-to-all-start.6 = ((f32[32,16,256]{2,1,0:T(8,128)}), f32[32,16,256]{2,1,0:T(8,128)S(1)}, u32[]{:S(2)}, u32[]{:S(2)}) async-start(f32[32,16,256]{2,1,0:T(8,128)} %rows_next.5), calls=%async_computation.6 | async-start | bytes 1048576 | tf_op jit(solution)/shard_map/all_to_all | solution.py:444
  198.6 4.4 %collective-permute-start.25 = (f32[24,256]{1,0:T(8,128)S(1)}, f32[24,256]{1,0:T(8,128)S(1)}, u32[]{:S(2)}, u32[]{:S(2)}) collective-permute-start(f32[24,256]{1,0:T(8,128)S(1)} %get-tuple-element.68), channel_id=1, source_target_pairs={{0,32},{32,64},{64,96},{96,0},{1,33},{33,65},{65,97},{97,1},{2,34}... | collective-permute-start | bytes 73736 | tf_op jit(solution)/shard_map/ppermute | solution.py:436
  199.8 4.5 %collective-permute-start.26 = (f32[24,256]{1,0:T(8,128)S(1)}, f32[24,256]{1,0:T(8,128)S(1)}, u32[]{:S(2)}, u32[]{:S(2)}) collective-permute-start(f32[24,256]{1,0:T(8,128)S(1)} %get-tuple-element.69), channel_id=1, source_target_pairs={{0,64},{32,96},{64,0},{96,32},{1,65},{33,97},{65,1},{97,33},{2,66}... | collective-permute-start | bytes 73736 | tf_op jit(solution)/shard_map/ppermute | solution.py:436
  (36 other events, 136.9 us)

commit v2 on v1

--- a/solution.py
+++ b/solution.py
@@ -12,7 +12,8 @@
 CORE = "col_2"
 COL = ("col_0", "col_1", "col_2")
 GRP_COL = ("grp", "col_0", "col_1", "col_2")
-GROUP = 8
+ROW_GROUP = 8
+COL_GROUP = 4
 highest = lax.Precision.HIGHEST
 VMEM = pl.BlockSpec(memory_space=pltpu.VMEM)
 SMEM = pl.BlockSpec(memory_space=pltpu.SMEM)
@@ -68,72 +69,105 @@
 def group_rows(base, place, lhs_hi, lhs_lo, hi, lo, out, first):
     tile_row, tile_col, tile_count = place
     results = []
-    for u in range(GROUP):
+    for u in range(ROW_GROUP):
         s = base + u
         k = ((tile_row[0, 0, 0] >> 5) - (tile_col[0, 0, s] >> 5)) & 3
         live = (s < tile_count[0, 0]).astype(f32)
         results.append(
             products(lhs_hi[k], lhs_lo[k], hi[s], lo[s], ((1,), (1,)), first, live)
         )
-    for u in range(GROUP):
+    for u in range(ROW_GROUP):
         out[tile_row[0, 0, base + u] & 31] += results[u]
 
 
+def groups_of(tile_count, group):
+    return (tile_count[0, 0] + (group - 1)) // group
+
+
+def group_copies(q, group, source_hi, source_lo, hi, lo, sems):
+    part = pl.ds(q * group, group)
+    return (
+        pltpu.make_async_copy(source_hi.at[part], hi.at[part], sems.at[0, q]),
+        pltpu.make_async_copy(source_lo.at[part], lo.at[part], sems.at[1, q]),
+    )
+
+
+def start_groups(tile_count, group, *refs):
+    @pl.loop(0, groups_of(tile_count, group))
+    def _(q):
+        for copy in group_copies(q, group, *refs):
+            copy.start()
+
+
 def rows_first_kernel(
-    tile_row, tile_col, tile_count, tiles, own, one, two, three, out, hi, lo, buf, lhs_hi, lhs_lo, sems
+    tile_row, tile_col, tile_count, tiles, own, one, two, three, out, hi_out, lo_out,
+    buf, hi, lo, lhs_hi, lhs_lo, sems, out_sems
 ):
-    slots = buf.shape[0]
-    copies = [
-        pltpu.make_async_copy(
-            tiles.at[0, 0, pl.ds(q * GROUP, GROUP)], buf.at[pl.ds(q * GROUP, GROUP)], sems.at[q]
-        )
-        for q in range(slots // GROUP)
-    ]
-    for copy in copies:
-        copy.start()
+    group = ROW_GROUP
+    count = groups_of(tile_count, group)
+
+    def arriving(q):
+        part = pl.ds(q * group, group)
+        return pltpu.make_async_copy(tiles.at[0, 0, part], buf.at[part], sems.at[q])
+
+    @pl.loop(0, count)
+    def _(q):
+        arriving(q).start()
+
     fill_pieces((own, one, two, three), lhs_hi, lhs_lo, True)
     out[...] = jnp.zeros_like(out)
-    for q, copy in enumerate(copies):
-        copy.wait()
-        for u in range(GROUP):
-            s = q * GROUP + u
+
+    @pl.loop(0, count)
+    def _(q):
+        arriving(q).wait()
+        for u in range(group):
+            s = q * group + u
             hi[s], lo[s] = split(buf[s])
-
-        @pl.when(q * GROUP < tile_count[0, 0])
-        def _():
-            group_rows(
-                q * GROUP, (tile_row, tile_col, tile_count), lhs_hi, lhs_lo, hi, lo, out, True
-            )
-
-
-def groups_of(tile_count):
-    return (tile_count[0, 0] + (GROUP - 1)) // GROUP
+        for copy in group_copies(q, group, hi, lo, hi_out, lo_out, out_sems):
+            copy.start()
+        group_rows(
+            q * group, (tile_row, tile_col, tile_count), lhs_hi, lhs_lo, hi, lo, out, True
+        )
+
+    @pl.loop(0, count)
+    def _(q):
+        for copy in group_copies(q, group, hi, lo, hi_out, lo_out, out_sems):
+            copy.wait()
 
 
 def rows_next_kernel(
-    tile_row, tile_col, tile_count, hi, lo, own, one, two, three, out, lhs_hi, lhs_lo
+    tile_row, tile_col, tile_count, hi_in, lo_in, own, one, two, three, out, hi, lo, lhs_hi, lhs_lo, sems
 ):
+    group = ROW_GROUP
+    start_groups(tile_count, group, hi_in, lo_in, hi, lo, sems)
     fill_pieces((own, one, two, three), lhs_hi, lhs_lo, False)
     out[...] = jnp.zeros_like(out)
 
-    @pl.loop(0, groups_of(tile_count))
+    @pl.loop(0, groups_of(tile_count, group))
     def _(q):
-        group_rows(q * GROUP, (tile_row, tile_col, tile_count), lhs_hi, lhs_lo, hi, lo, out, False)
+        for copy in group_copies(q, group, hi_in, lo_in, hi, lo, sems):
+            copy.wait()
+        group_rows(q * group, (tile_row, tile_col, tile_count), lhs_hi, lhs_lo, hi, lo, out, False)
 
 
 def cols_kernel(
-    first, tile_row, tile_col, tile_count, hi, lo, near, far, own, one, two, three, acc
+    first, tile_row, tile_col, tile_count, hi_in, lo_in, near, far, own, one, two, three,
+    hi, lo, acc, sems
 ):
+    group = COL_GROUP
+    start_groups(tile_count, group, hi_in, lo_in, hi, lo, sems)
     acc[...] = jnp.zeros_like(acc)
     gram = jnp.zeros_like(near[0, 16:24])
     for p in range(near.shape[0]):
         gram = gram + (near[p, 16:24] + far[p, 16:24])
 
-    @pl.loop(0, groups_of(tile_count))
+    @pl.loop(0, groups_of(tile_count, group))
     def _(q):
+        for copy in group_copies(q, group, hi_in, lo_in, hi, lo, sems):
+            copy.wait()
         results, slots = [], []
-        for u in range(GROUP):
-            s = q * GROUP + u
+        for u in range(group):
+            s = q * group + u
             row = tile_row[0, 0, s] & 31
             place = row >> 1
             same = ((row ^ tile_col[0, 0, 0]) & 1) == 0
@@ -144,7 +178,7 @@
                 products(left_hi, left_lo, hi[s], lo[s], ((1,), (0,)), first, live)
             )
             slots.append(((tile_col[0, 0, s] >> 5) - (tile_row[0, 0, 0] >> 5)) & 3)
-        for u in range(GROUP):
+        for u in range(group):
             acc[slots[u]] += results[u]
 
     for k, out in enumerate((own, one, two, three)):
@@ -158,16 +192,19 @@
         name="rows_first",
         out_shape=(
             jax.ShapeDtypeStruct((32, 24, size), f32),
+            pltpu.MemorySpace.HBM((slots, size, size), bf16),
+            pltpu.MemorySpace.HBM((slots, size, size), bf16),
+        ),
+        in_specs=[SMEM] * 3 + [HBM] + [VMEM] * 4,
+        out_specs=(VMEM, HBM, HBM),
+        scratch_shapes=[
+            pltpu.VMEM((slots, size, size), f32),
             pltpu.VMEM((slots, size, size), bf16),
             pltpu.VMEM((slots, size, size), bf16),
-        ),
-        in_specs=[SMEM] * 3 + [HBM] + [VMEM] * 4,
-        out_specs=(VMEM,) * 3,
-        scratch_shapes=[
-            pltpu.VMEM((slots, size, size), f32),
             pltpu.VMEM((4, 48, size), bf16),
             pltpu.VMEM((4, 32, size), bf16),
-            pltpu.SemaphoreType.DMA((slots // GROUP,)),
+            pltpu.SemaphoreType.DMA((slots // ROW_GROUP,)),
+            pltpu.SemaphoreType.DMA((2, slots // ROW_GROUP)),
         ],
         compiler_params=limits(28),
         cost_estimate=cost(400_000_000),
@@ -175,14 +212,20 @@
 
 
 def rows_next(place, hi, lo, pieces):
-    size = hi.shape[1]
+    slots, size = hi.shape[0], hi.shape[1]
     return pl.pallas_call(
         rows_next_kernel,
         name="rows_next",
         out_shape=jax.ShapeDtypeStruct((32, 16, size), f32),
-        in_specs=[SMEM] * 3 + [VMEM] * 6,
+        in_specs=[SMEM] * 3 + [HBM] * 2 + [VMEM] * 4,
         out_specs=VMEM,
-        scratch_shapes=[pltpu.VMEM((4, 32, size), bf16), pltpu.VMEM((4, 16, size), bf16)],
+        scratch_shapes=[
+            pltpu.VMEM((slots, size, size), bf16),
+            pltpu.VMEM((slots, size, size), bf16),
+            pltpu.VMEM((4, 32, size), bf16),
+            pltpu.VMEM((4, 16, size), bf16),
+            pltpu.SemaphoreType.DMA((2, slots // ROW_GROUP)),
+        ],
         compiler_params=limits(20),
         cost_estimate=cost(400_000_000),
     )(*place, hi, lo, *pieces)
@@ -190,15 +233,20 @@
 
 def cols_product(first, place, hi, lo, near, far):
     height = 24 if first else 16
-    size = hi.shape[1]
+    slots, size = hi.shape[0], hi.shape[1]
     out = jax.ShapeDtypeStruct((height + 8, size), f32)
     return pl.pallas_call(
         functools.partial(cols_kernel, first),
         name="cols_first" if first else "cols_next",
         out_shape=(out,) * 4,
-        in_specs=[SMEM] * 3 + [VMEM] * 4,
+        in_specs=[SMEM] * 3 + [HBM] * 2 + [VMEM] * 2,
         out_specs=(VMEM,) * 4,
-        scratch_shapes=[pltpu.VMEM((4, height, size), f32)],
+        scratch_shapes=[
+            pltpu.VMEM((slots, size, size), bf16),
+            pltpu.VMEM((slots, size, size), bf16),
+            pltpu.VMEM((4, height, size), f32),
+            pltpu.SemaphoreType.DMA((2, slots // COL_GROUP)),
+        ],
         compiler_params=limits(20),
         cost_estimate=cost(400_000_000),
     )(*place, hi, lo, near, far)
@@ -340,7 +388,6 @@
     args = [arrived, *sides, *extra]
     return pl.pallas_call(
         functools.partial(update_kernel, step, node_total),
-        name=f"update_{step}",
         out_shape=tuple(shapes),
         in_specs=[VMEM] * len(args),
         out_specs=(VMEM,) * len(shapes),
@@ -447,17 +494,27 @@
 def body(start_block, tile_values, tile_row, tile_col, tile_count):
     grp_size = lax.axis_size("grp")
     node_total = float(start_block.shape[1] * grp_size * lax.axis_size(COL))
-    place = (tile_row, tile_col, tile_count)
+    place = tuple(
+        pltpu.with_memory_space_constraint(part, pltpu.MemorySpace.HBM)
+        for part in (tile_row, tile_col)
+    )
+    place = (*place, tile_count)
+    start_block = pltpu.with_memory_space_constraint(start_block, pltpu.MemorySpace.HBM)
+    tile_values = pltpu.with_memory_space_constraint(tile_values, pltpu.MemorySpace.HBM)
     message = first_message(start_block)
     piece = start_block
     state = degree = shift = hi = lo = None
     lowers, coeffs = [], []
     for step in range(ITERS):
         first = step == 0
-        pieces = [piece] + [shifted(piece, hop) for hop in range(1, grp_size)]
+        pieces = [piece]
+        for hop in range(1, grp_size):
+            pieces.append(shifted(piece, hop))
         near = exchanged(message, ZX)
         if first:
             rows, hi, lo = rows_first(place, tile_values, pieces)
+            hi = pltpu.with_memory_space_constraint(hi, pltpu.MemorySpace.HBM)
+            lo = pltpu.with_memory_space_constraint(lo, pltpu.MemorySpace.HBM)
         else:
             rows = rows_next(place, hi, lo, pieces)
         far = swapped(near)

time: 237 us -> 214 us (0.903)
  local copies, waits for them, and re-layouts: 40.8 us -> 0.62 us
  Pallas kernels: 40.1 us -> 54.7 us
  waiting for transfers between devices: 21.8 us -> 31.3 us
  starting transfers between devices: 107 us -> 100 us
    unnamed x48 -> x6, local copies, waits for them, and re-layouts: 40.8 us -> 0.62 us
    all_to_all x8, waiting for transfers between devices: 1.67 us -> 15.4 us  [exchanged(): return lax.all_to_all(value, axes, split_axis=0, concat_axis=0, tiled=True)]
    pallas_call x4, Pallas kernels: 7.52 us -> 14.3 us  [cols_product(): pl.pallas_call(functools.partial(cols_kernel, first), name='cols_first' i...]
    ppermute x24, starting transfers between devices: 34 us -> 28.1 us  [shifted(): lax.ppermute(value, 'grp', [(i, (i + hop) % size) for i in range(size)])]
    pallas_call x3, Pallas kernels: 10.4 us -> 15.5 us  [rows_next(): pl.pallas_call(rows_next_kernel, name='rows_next', out_shape=jax.ShapeDty...]
    ppermute x24, waiting for transfers between devices: 14.2 us -> 10 us  [shifted(): lax.ppermute(value, 'grp', [(i, (i + hop) % size) for i in range(size)])]
  transfers between devices with their start and end apart: 36 -> 36, of which waited for: 21 -> 17; matrix products, arithmetic and copies ran while one was open for 0% -> 0% of each run, Pallas kernels for 10% -> 17%
where the time goes in v2:
time: 214 us; the launch traced here: 212 us
  starting transfers between devices  100 us (47%)
  Pallas kernels  54.7 us (26%)
  waiting for transfers between devices  31.3 us (15%)
  blocking collectives  23.6 us (11%)
    all_to_all x8, starting transfers between devices, exchanged(): return lax.all_to_all(value, axes, split_axis=0, concat_axis=0, tiled=True)  70.7 us
    ppermute x24, starting transfers between devices, shifted(): lax.ppermute(value, 'grp', [(i, (i + hop) % size) for i in range(size)])  28.1 us
    all_to_all x2, blocking collectives, exchanged(): return lax.all_to_all(value, axes, split_axis=0, concat_axis=0, tiled=True)  23.6 us
    pallas_call x3, Pallas kernels, rows_next(): pl.pallas_call(rows_next_kernel, name='rows_next', out_shape=jax.ShapeDty...  15.5 us
    all_to_all x8, waiting for transfers between devices, exchanged(): return lax.all_to_all(value, axes, split_axis=0, concat_axis=0, tiled=True)  15.4 us
    pallas_call x4, Pallas kernels, cols_product(): pl.pallas_call(functools.partial(cols_kernel, first), name='cols_first' i...  14.3 us
    pallas_call x4, Pallas kernels, update(): pl.pallas_call(functools.partial(update_kernel, step, node_total), out_sh...  13.5 us
    ppermute x24, waiting for transfers between devices, shifted(): lax.ppermute(value, 'grp', [(i, (i + hop) % size) for i in range(size)])  10 us
  transfers between devices with their start and end apart: 36, of which 17 were waited for; matrix products, arithmetic and copies ran while one was open for 0% of the time, Pallas kernels for 17%

profile of v2, /device:TPU:1, one launch (start us, length us, event | category | flops | bytes accessed | tf_op | source)
XLA Modules:
  0.0 211.9 jit_solution(3137260436617451595)
XLA Ops:
  2.2 8.4 %all-to-all-start.1 = ((f32[16,24,256]{2,1,0:T(8,128)}), f32[16,24,256]{2,1,0:T(8,128)S(1)}, u32[]{:S(2)}, u32[]{:S(2)}) async-start(f32[16,24,256]{2,1,0:T(8,128)} %first_message.1), calls=%async_computation.1 | async-start | bytes 786432 | tf_op jit(solution)/shard_map/all_to_all | solution.py:491
  18.4 6.8 %rows_first.1 = (f32[32,24,256]{2,1,0:T(8,128)}, bf16[32,256,256]{2,1,0:T(8,128)(2,1)}, bf16[32,256,256]{2,1,0:T(8,128)(2,1)}) custom-call(s32[1,1,32]{2,1,0:T(1,128)} %tile_row.15, s32[1,1,32]{2,1,0:T(1,128)} %tile_col.15, s32[1,1]{1,0:T(1,128)S(6)} %copy.8.tile_count, f32[1,1,32,256,256]{4,3,2,1,0:T(8,128)} %tiles.1, f32[16,256]{1,0:T(8,128)} %refs_5_.1, ...), custom_call_target="tpu_custom_call" | custom-call | flops 400000000 | bytes 1048576 | tf_op jit(solution)/shard_map/rows_first/pallas_call | solution.py:190
  25.2 10.7 %all-to-all-start = ((f32[32,24,256]{2,1,0:T(8,128)}), f32[32,24,256]{2,1,0:T(8,128)S(1)}, u32[]{:S(2)}, u32[]{:S(2)}) async-start(f32[32,24,256]{2,1,0:T(8,128)} %get-tuple-element.44), calls=%async_computation | async-start | bytes 1572864 | tf_op jit(solution)/shard_map/all_to_all | solution.py:491
  37.7 3.6 %cols_first.1 = (f32[32,256]{1,0:T(8,128)S(1)}, f32[32,256]{1,0:T(8,128)S(1)}, f32[32,256]{1,0:T(8,128)S(1)}, f32[32,256]{1,0:T(8,128)S(1)}) custom-call(s32[1,1,32]{2,1,0:T(1,128)} %tile_row.15, s32[1,1,32]{2,1,0:T(1,128)} %tile_col.15, s32[1,1]{1,0:T(1,128)S(6)} %copy.8.tile_count, bf16[32,256,256]{2,1,0:T(8,128)(2,1)} %get-tuple-element.42.hi_in, ...), custom_call_target="tpu_custom_call" | custom-call | flops 400000000 | bytes 1048576 | tf_op jit(solution)/shard_map/cols_first/pallas_call | solution.py:238
  44.7 5.5 %all-to-all-done.refs_0_ = f32[32,24,256]{2,1,0:T(8,128)S(1)} async-done(((f32[32,24,256]{2,1,0:T(8,128)}), f32[32,24,256]{2,1,0:T(8,128)S(1)}, u32[]{:S(2)}, u32[]{:S(2)}) %all-to-all-start) | async-done | bytes 786464 | tf_op jit(solution)/shard_map/all_to_all | solution.py:491
  50.2 3.8 %shard_map.76 = (f32[16,24,256]{2,1,0:T(8,128)}, f32[16,256]{1,0:T(8,128)S(1)}, f32[16,512]{1,0:T(8,128)S(1)}, f32[8,256]{1,0:T(8,128)S(1)}, f32[16,16]{1,0:T(8,128)S(1)}) custom-call(f32[32,24,256]{2,1,0:T(8,128)S(1)} %all-to-all-done.refs_0_, f32[32,256]{1,0:T(8,128)S(1)} %get-tuple-element.45.refs_1_, f32[32,256]{1,0:T(8,128)S(1)} %collective-permute-done.4.refs_2_, ...), custom_call_target="tpu_custom_call" | custom-call | flops 400000000 | bytes 1048576 | tf_op jit(solution)/shard_map/pallas_call | solution.py:389
  54.0 4.0 %all-to-all-start.3 = ((f32[16,24,256]{2,1,0:T(8,128)}), f32[16,24,256]{2,1,0:T(8,128)S(1)}, u32[]{:S(2)}, u32[]{:S(2)}) async-start(f32[16,24,256]{2,1,0:T(8,128)} %get-tuple-element.50), calls=%async_computation.3 | async-start | bytes 786432 | tf_op jit(solution)/shard_map/all_to_all | solution.py:491
  58.6 3.9 %collective-permute-start.8 = (f32[16,256]{1,0:T(8,128)S(1)}, f32[16,256]{1,0:T(8,128)S(1)}, u32[]{:S(2)}, u32[]{:S(2)}) collective-permute-start(f32[16,256]{1,0:T(8,128)S(1)} %get-tuple-element.49.own), channel_id=1, source_target_pairs={{0,64},{32,96},{64,0},{96,32},{1,65},{33,97},{65,1},{97,33},{2,66}... | collective-permute-start | bytes 49160 | tf_op jit(solution)/shard_map/ppermute | solution.py:483
  65.3 5.2 %rows_next.3 = f32[32,16,256]{2,1,0:T(8,128)} custom-call(s32[1,1,32]{2,1,0:T(1,128)} %tile_row.15, s32[1,1,32]{2,1,0:T(1,128)} %tile_col.15, s32[1,1]{1,0:T(1,128)S(6)} %copy.8.tile_count, bf16[32,256,256]{2,1,0:T(8,128)(2,1)} %get-tuple-element.42.hi_in, bf16[32,256,256]{2,1,0:T(8,128)(2,1)} %get-tuple-element.43.lo_in, ...), custom_call_target="tpu_custom_call" | custom-call | flops 400000000 | bytes 1048576 | tf_op jit(solution)/shard_map/rows_next/pallas_call | solution.py:216
  70.5 11.1 %all-to-all-start.2 = ((f32[32,16,256]{2,1,0:T(8,128)}), f32[32,16,256]{2,1,0:T(8,128)S(1)}, u32[]{:S(2)}, u32[]{:S(2)}) async-start(f32[32,16,256]{2,1,0:T(8,128)} %rows_next.3), calls=%async_computation.2 | async-start | bytes 1048576 | tf_op jit(solution)/shard_map/all_to_all | solution.py:491
  83.5 3.6 %cols_next.3 = (f32[24,256]{1,0:T(8,128)S(1)}, f32[24,256]{1,0:T(8,128)S(1)}, f32[24,256]{1,0:T(8,128)S(1)}, f32[24,256]{1,0:T(8,128)S(1)}) custom-call(s32[1,1,32]{2,1,0:T(1,128)} %tile_row.15, s32[1,1,32]{2,1,0:T(1,128)} %tile_col.15, s32[1,1]{1,0:T(1,128)S(6)} %copy.8.tile_count, bf16[32,256,256]{2,1,0:T(8,128)(2,1)} %get-tuple-element.42.hi_in, ...), custom_call_target="tpu_custom_call" | custom-call | flops 400000000 | bytes 1048576 | tf_op jit(solution)/shard_map/cols_next/pallas_call | solution.py:238
  89.8 3.3 %all-to-all-done.2.refs_0_ = f32[32,16,256]{2,1,0:T(8,128)S(1)} async-done(((f32[32,16,256]{2,1,0:T(8,128)}), f32[32,16,256]{2,1,0:T(8,128)S(1)}, u32[]{:S(2)}, u32[]{:S(2)}) %all-to-all-start.2) | async-done | bytes 524320 | tf_op jit(solution)/shard_map/all_to_all | solution.py:491
  93.1 3.4 %shard_map.77 = (f32[16,24,256]{2,1,0:T(8,128)}, f32[16,256]{1,0:T(8,128)S(1)}, f32[32,512]{1,0:T(8,128)S(1)}, f32[16,128]{1,0:T(8,128)S(1)}, f32[16,16]{1,0:T(8,128)S(1)}, /*index=5*/f32[8,128]{1,0:T(8,128)S(1)}) custom-call(f32[32,16,256]{2,1,0:T(8,128)S(1)} %all-to-all-done.2.refs_0_, f32[24,256]{1,0:T(8,128)S(1)} %get-tuple-element.51.refs_1_, ...), custom_call_target="tpu_custom_call" | custom-call | flops 400000000 | bytes 1048576 | tf_op jit(solution)/shard_map/pallas_call | solution.py:389
  96.5 6.3 %all-to-all-start.5 = ((f32[16,24,256]{2,1,0:T(8,128)}), f32[16,24,256]{2,1,0:T(8,128)S(1)}, u32[]{:S(2)}, u32[]{:S(2)}) async-start(f32[16,24,256]{2,1,0:T(8,128)} %get-tuple-element.58), calls=%async_computation.5 | async-start | bytes 786432 | tf_op jit(solution)/shard_map/all_to_all | solution.py:491
  109.2 5.2 %rows_next.4 = f32[32,16,256]{2,1,0:T(8,128)} custom-call(s32[1,1,32]{2,1,0:T(1,128)} %tile_row.15, s32[1,1,32]{2,1,0:T(1,128)} %tile_col.15, s32[1,1]{1,0:T(1,128)S(6)} %copy.8.tile_count, bf16[32,256,256]{2,1,0:T(8,128)(2,1)} %get-tuple-element.42.hi_in, bf16[32,256,256]{2,1,0:T(8,128)(2,1)} %get-tuple-element.43.lo_in, ...), custom_call_target="tpu_custom_call" | custom-call | flops 400000000 | bytes 1048576 | tf_op jit(solution)/shard_map/rows_next/pallas_call | solution.py:216
  114.4 11.9 %all-to-all-start.4 = ((f32[32,16,256]{2,1,0:T(8,128)}), f32[32,16,256]{2,1,0:T(8,128)S(1)}, u32[]{:S(2)}, u32[]{:S(2)}) async-start(f32[32,16,256]{2,1,0:T(8,128)} %rows_next.4), calls=%async_computation.4 | async-start | bytes 1048576 | tf_op jit(solution)/shard_map/all_to_all | solution.py:491
  128.1 3.6 %cols_next.4 = (f32[24,256]{1,0:T(8,128)S(1)}, f32[24,256]{1,0:T(8,128)S(1)}, f32[24,256]{1,0:T(8,128)S(1)}, f32[24,256]{1,0:T(8,128)S(1)}) custom-call(s32[1,1,32]{2,1,0:T(1,128)} %tile_row.15, s32[1,1,32]{2,1,0:T(1,128)} %tile_col.15, s32[1,1]{1,0:T(1,128)S(6)} %copy.8.tile_count, bf16[32,256,256]{2,1,0:T(8,128)(2,1)} %get-tuple-element.42.hi_in, ...), custom_call_target="tpu_custom_call" | custom-call | flops 400000000 | bytes 1048576 | tf_op jit(solution)/shard_map/cols_next/pallas_call | solution.py:238
  137.7 3.3 %shard_map.78 = (f32[16,24,256]{2,1,0:T(8,128)}, f32[16,256]{1,0:T(8,128)S(1)}, f32[48,512]{1,0:T(8,128)S(1)}, f32[16,128]{1,0:T(8,128)S(1)}, f32[16,16]{1,0:T(8,128)S(1)}) custom-call(f32[32,16,256]{2,1,0:T(8,128)S(1)} %all-to-all-done.4.refs_0_, f32[24,256]{1,0:T(8,128)S(1)} %get-tuple-element.59.refs_1_, f32[24,256]{1,0:T(8,128)S(1)} %collective-permute-done.18.refs_2_, ...), custom_call_target="tpu_custom_call" | custom-call | flops 400000000 | bytes 1048576 | tf_op jit(solution)/shard_map/pallas_call | solution.py:389
  141.0 6.3 %all-to-all-start.7 = ((f32[16,24,256]{2,1,0:T(8,128)}), f32[16,24,256]{2,1,0:T(8,128)S(1)}, u32[]{:S(2)}, u32[]{:S(2)}) async-start(f32[16,24,256]{2,1,0:T(8,128)} %get-tuple-element.66), calls=%async_computation.7 | async-start | bytes 786432 | tf_op jit(solution)/shard_map/all_to_all | solution.py:491
  153.7 5.2 %rows_next.5 = f32[32,16,256]{2,1,0:T(8,128)} custom-call(s32[1,1,32]{2,1,0:T(1,128)} %tile_row.15, s32[1,1,32]{2,1,0:T(1,128)} %tile_col.15, s32[1,1]{1,0:T(1,128)S(6)} %copy.8.tile_count, bf16[32,256,256]{2,1,0:T(8,128)(2,1)} %get-tuple-element.42.hi_in, bf16[32,256,256]{2,1,0:T(8,128)(2,1)} %get-tuple-element.43.lo_in, ...), custom_call_target="tpu_custom_call" | custom-call | flops 400000000 | bytes 1048576 | tf_op jit(solution)/shard_map/rows_next/pallas_call | solution.py:216
  158.9 11.9 %all-to-all-start.6 = ((f32[32,16,256]{2,1,0:T(8,128)}), f32[32,16,256]{2,1,0:T(8,128)S(1)}, u32[]{:S(2)}, u32[]{:S(2)}) async-start(f32[32,16,256]{2,1,0:T(8,128)} %rows_next.5), calls=%async_computation.6 | async-start | bytes 1048576 | tf_op jit(solution)/shard_map/all_to_all | solution.py:491
  172.6 3.6 %cols_next.5 = (f32[24,256]{1,0:T(8,128)S(1)}, f32[24,256]{1,0:T(8,128)S(1)}, f32[24,256]{1,0:T(8,128)S(1)}, f32[24,256]{1,0:T(8,128)S(1)}) custom-call(s32[1,1,32]{2,1,0:T(1,128)} %tile_row.15, s32[1,1,32]{2,1,0:T(1,128)} %tile_col.15, s32[1,1]{1,0:T(1,128)S(6)} %copy.8.tile_count, bf16[32,256,256]{2,1,0:T(8,128)(2,1)} %get-tuple-element.42.hi_in, ...), custom_call_target="tpu_custom_call" | custom-call | flops 400000000 | bytes 1048576 | tf_op jit(solution)/shard_map/cols_next/pallas_call | solution.py:238
  185.3 10.2 %all_to_all.50.arrived = f32[8,8,256]{2,1,0:T(8,128)S(1)} all-to-all(f32[8,8,256]{2,1,0:T(8,128)S(1)} %get-tuple-element.72), channel_id=1, replica_groups=mesh['grp'=4,'col_0'=4,'col_1'=4,'col_2'=2] {'col_1','col_2'}, dimensions={0} | all-to-all | bytes 131072 | tf_op jit(solution)/shard_map/all_to_all | solution.py:491
  195.5 13.4 %all_to_all.51.arrived = f32[16,8,256]{2,1,0:T(8,128)S(1)} all-to-all(f32[16,8,256]{2,1,0:T(8,128)S(1)} %fold.1), channel_id=1, replica_groups=mesh['grp'=4,'col_0'=4,'col_1'=4,'col_2'=2] {'grp','col_0'}, dimensions={0} | all-to-all | bytes 262144 | tf_op jit(solution)/shard_map/all_to_all | solution.py:491
  (71 shorter events, 56.3 us)
Async XLA Ops:
  2.2 22.9 %all-to-all-start.1 = ((f32[16,24,256]{2,1,0:T(8,128)}), f32[16,24,256]{2,1,0:T(8,128)S(1)}, u32[]{:S(2)}, u32[]{:S(2)}) async-start(f32[16,24,256]{2,1,0:T(8,128)} %first_message.1), calls=%async_computation.1 | async-start | bytes 786432 | tf_op jit(solution)/shard_map/all_to_all | solution.py:491
  10.7 5.7 %collective-permute-start = (f32[16,256]{1,0:T(8,128)}, f32[16,256]{1,0:T(8,128)S(1)}, u32[]{:S(2)}, u32[]{:S(2)}) collective-permute-start(f32[16,256]{1,0:T(8,128)} %refs_5_.1), channel_id=1, source_target_pairs={{0,32},{32,64},{64,96},{96,0},{1,33},{33,65},{65,97},{97,1},{2,34}... | collective-permute-start | bytes 49160 | tf_op jit(solution)/shard_map/ppermute | solution.py:483
  12.0 4.4 %collective-permute-start.1 = (f32[16,256]{1,0:T(8,128)}, f32[16,256]{1,0:T(8,128)S(1)}, u32[]{:S(2)}, u32[]{:S(2)}) collective-permute-start(f32[16,256]{1,0:T(8,128)} %refs_5_.1), channel_id=1, source_target_pairs={{0,64},{32,96},{64,0},{96,32},{1,65},{33,97},{65,1},{97,33},{2,66}... | collective-permute-start | bytes 49160 | tf_op jit(solution)/shard_map/ppermute | solution.py:483
  25.2 25.0 %all-to-all-start = ((f32[32,24,256]{2,1,0:T(8,128)}), f32[32,24,256]{2,1,0:T(8,128)S(1)}, u32[]{:S(2)}, u32[]{:S(2)}) async-start(f32[32,24,256]{2,1,0:T(8,128)} %get-tuple-element.44), calls=%async_computation | async-start | bytes 1572864 | tf_op jit(solution)/shard_map/all_to_all | solution.py:491
  41.3 8.8 %collective-permute-start.4 = (f32[32,256]{1,0:T(8,128)S(1)}, f32[32,256]{1,0:T(8,128)S(1)}, u32[]{:S(2)}, u32[]{:S(2)}) collective-permute-start(f32[32,256]{1,0:T(8,128)S(1)} %get-tuple-element.46), channel_id=1, source_target_pairs={{0,32},{32,64},{64,96},{96,0},{1,33},{33,65},{65,97},{97,1},{2,34}... | collective-permute-start | bytes 98312 | tf_op jit(solution)/shard_map/ppermute | solution.py:483
  41.6 8.6 %collective-permute-start.5 = (f32[32,256]{1,0:T(8,128)S(1)}, f32[32,256]{1,0:T(8,128)S(1)}, u32[]{:S(2)}, u32[]{:S(2)}) collective-permute-start(f32[32,256]{1,0:T(8,128)S(1)} %get-tuple-element.47), channel_id=1, source_target_pairs={{0,64},{32,96},{64,0},{96,32},{1,65},{33,97},{65,1},{97,33},{2,66}... | collective-permute-start | bytes 98312 | tf_op jit(solution)/shard_map/ppermute | solution.py:483
  44.0 6.1 %collective-permute-start.6 = (f32[32,256]{1,0:T(8,128)S(1)}, f32[32,256]{1,0:T(8,128)S(1)}, u32[]{:S(2)}, u32[]{:S(2)}) collective-permute-start(f32[32,256]{1,0:T(8,128)S(1)} %get-tuple-element.48), channel_id=1, source_target_pairs={{0,96},{32,0},{64,32},{96,64},{1,97},{33,1},{65,33},{97,65},{2,98}... | collective-permute-start | bytes 98312 | tf_op jit(solution)/shard_map/ppermute | solution.py:483
  54.0 16.5 %all-to-all-start.3 = ((f32[16,24,256]{2,1,0:T(8,128)}), f32[16,24,256]{2,1,0:T(8,128)S(1)}, u32[]{:S(2)}, u32[]{:S(2)}) async-start(f32[16,24,256]{2,1,0:T(8,128)} %get-tuple-element.50), calls=%async_computation.3 | async-start | bytes 786432 | tf_op jit(solution)/shard_map/all_to_all | solution.py:491
  57.9 4.5 %collective-permute-start.7 = (f32[16,256]{1,0:T(8,128)S(1)}, f32[16,256]{1,0:T(8,128)S(1)}, u32[]{:S(2)}, u32[]{:S(2)}) collective-permute-start(f32[16,256]{1,0:T(8,128)S(1)} %get-tuple-element.49.own), channel_id=1, source_target_pairs={{0,32},{32,64},{64,96},{96,0},{1,33},{33,65},{65,97},{97,1},{2,34}... | collective-permute-start | bytes 49160 | tf_op jit(solution)/shard_map/ppermute | solution.py:483
  58.6 5.2 %collective-permute-start.8 = (f32[16,256]{1,0:T(8,128)S(1)}, f32[16,256]{1,0:T(8,128)S(1)}, u32[]{:S(2)}, u32[]{:S(2)}) collective-permute-start(f32[16,256]{1,0:T(8,128)S(1)} %get-tuple-element.49.own), channel_id=1, source_target_pairs={{0,64},{32,96},{64,0},{96,32},{1,65},{33,97},{65,1},{97,33},{2,66}... | collective-permute-start | bytes 49160 | tf_op jit(solution)/shard_map/ppermute | solution.py:483
  70.5 22.6 %all-to-all-start.2 = ((f32[32,16,256]{2,1,0:T(8,128)}), f32[32,16,256]{2,1,0:T(8,128)S(1)}, u32[]{:S(2)}, u32[]{:S(2)}) async-start(f32[32,16,256]{2,1,0:T(8,128)} %rows_next.3), calls=%async_computation.2 | async-start | bytes 1048576 | tf_op jit(solution)/shard_map/all_to_all | solution.py:491
  87.0 6.0 %collective-permute-start.11 = (f32[24,256]{1,0:T(8,128)S(1)}, f32[24,256]{1,0:T(8,128)S(1)}, u32[]{:S(2)}, u32[]{:S(2)}) collective-permute-start(f32[24,256]{1,0:T(8,128)S(1)} %get-tuple-element.52), channel_id=1, source_target_pairs={{0,32},{32,64},{64,96},{96,0},{1,33},{33,65},{65,97},{97,1},{2,34}... | collective-permute-start | bytes 73736 | tf_op jit(solution)/shard_map/ppermute | solution.py:483
  87.1 6.0 %collective-permute-start.12 = (f32[24,256]{1,0:T(8,128)S(1)}, f32[24,256]{1,0:T(8,128)S(1)}, u32[]{:S(2)}, u32[]{:S(2)}) collective-permute-start(f32[24,256]{1,0:T(8,128)S(1)} %get-tuple-element.53), channel_id=1, source_target_pairs={{0,64},{32,96},{64,0},{96,32},{1,65},{33,97},{65,1},{97,33},{2,66}... | collective-permute-start | bytes 73736 | tf_op jit(solution)/shard_map/ppermute | solution.py:483
  88.9 4.2 %collective-permute-start.13 = (f32[24,256]{1,0:T(8,128)S(1)}, f32[24,256]{1,0:T(8,128)S(1)}, u32[]{:S(2)}, u32[]{:S(2)}) collective-permute-start(f32[24,256]{1,0:T(8,128)S(1)} %get-tuple-element.54), channel_id=1, source_target_pairs={{0,96},{32,0},{64,32},{96,64},{1,97},{33,1},{65,33},{97,65},{2,98}... | collective-permute-start | bytes 73736 | tf_op jit(solution)/shard_map/ppermute | solution.py:483
  96.5 17.9 %all-to-all-start.5 = ((f32[16,24,256]{2,1,0:T(8,128)}), f32[16,24,256]{2,1,0:T(8,128)S(1)}, u32[]{:S(2)}, u32[]{:S(2)}) async-start(f32[16,24,256]{2,1,0:T(8,128)} %get-tuple-element.58), calls=%async_computation.5 | async-start | bytes 786432 | tf_op jit(solution)/shard_map/all_to_all | solution.py:491
  114.4 23.4 %all-to-all-start.4 = ((f32[32,16,256]{2,1,0:T(8,128)}), f32[32,16,256]{2,1,0:T(8,128)S(1)}, u32[]{:S(2)}, u32[]{:S(2)}) async-start(f32[32,16,256]{2,1,0:T(8,128)} %rows_next.4), calls=%async_computation.4 | async-start | bytes 1048576 | tf_op jit(solution)/shard_map/all_to_all | solution.py:491
  131.7 6.0 %collective-permute-start.18 = (f32[24,256]{1,0:T(8,128)S(1)}, f32[24,256]{1,0:T(8,128)S(1)}, u32[]{:S(2)}, u32[]{:S(2)}) collective-permute-start(f32[24,256]{1,0:T(8,128)S(1)} %get-tuple-element.60), channel_id=1, source_target_pairs={{0,32},{32,64},{64,96},{96,0},{1,33},{33,65},{65,97},{97,1},{2,34}... | collective-permute-start | bytes 73736 | tf_op jit(solution)/shard_map/ppermute | solution.py:483
  131.8 6.0 %collective-permute-start.19 = (f32[24,256]{1,0:T(8,128)S(1)}, f32[24,256]{1,0:T(8,128)S(1)}, u32[]{:S(2)}, u32[]{:S(2)}) collective-permute-start(f32[24,256]{1,0:T(8,128)S(1)} %get-tuple-element.61), channel_id=1, source_target_pairs={{0,64},{32,96},{64,0},{96,32},{1,65},{33,97},{65,1},{97,33},{2,66}... | collective-permute-start | bytes 73736 | tf_op jit(solution)/shard_map/ppermute | solution.py:483
  133.5 4.2 %collective-permute-start.20 = (f32[24,256]{1,0:T(8,128)S(1)}, f32[24,256]{1,0:T(8,128)S(1)}, u32[]{:S(2)}, u32[]{:S(2)}) collective-permute-start(f32[24,256]{1,0:T(8,128)S(1)} %get-tuple-element.62), channel_id=1, source_target_pairs={{0,96},{32,0},{64,32},{96,64},{1,97},{33,1},{65,33},{97,65},{2,98}... | collective-permute-start | bytes 73736 | tf_op jit(solution)/shard_map/ppermute | solution.py:483
  141.0 17.9 %all-to-all-start.7 = ((f32[16,24,256]{2,1,0:T(8,128)}), f32[16,24,256]{2,1,0:T(8,128)S(1)}, u32[]{:S(2)}, u32[]{:S(2)}) async-start(f32[16,24,256]{2,1,0:T(8,128)} %get-tuple-element.66), calls=%async_computation.7 | async-start | bytes 786432 | tf_op jit(solution)/shard_map/all_to_all | solution.py:491
  158.9 23.4 %all-to-all-start.6 = ((f32[32,16,256]{2,1,0:T(8,128)}), f32[32,16,256]{2,1,0:T(8,128)S(1)}, u32[]{:S(2)}, u32[]{:S(2)}) async-start(f32[32,16,256]{2,1,0:T(8,128)} %rows_next.5), calls=%async_computation.6 | async-start | bytes 1048576 | tf_op jit(solution)/shard_map/all_to_all | solution.py:491
  176.2 6.0 %collective-permute-start.25 = (f32[24,256]{1,0:T(8,128)S(1)}, f32[24,256]{1,0:T(8,128)S(1)}, u32[]{:S(2)}, u32[]{:S(2)}) collective-permute-start(f32[24,256]{1,0:T(8,128)S(1)} %get-tuple-element.68), channel_id=1, source_target_pairs={{0,32},{32,64},{64,96},{96,0},{1,33},{33,65},{65,97},{97,1},{2,34}... | collective-permute-start | bytes 73736 | tf_op jit(solution)/shard_map/ppermute | solution.py:483
  176.3 6.0 %collective-permute-start.26 = (f32[24,256]{1,0:T(8,128)S(1)}, f32[24,256]{1,0:T(8,128)S(1)}, u32[]{:S(2)}, u32[]{:S(2)}) collective-permute-start(f32[24,256]{1,0:T(8,128)S(1)} %get-tuple-element.69), channel_id=1, source_target_pairs={{0,64},{32,96},{64,0},{96,32},{1,65},{33,97},{65,1},{97,33},{2,66}... | collective-permute-start | bytes 73736 | tf_op jit(solution)/shard_map/ppermute | solution.py:483
  178.0 4.2 %collective-permute-start.27 = (f32[24,256]{1,0:T(8,128)S(1)}, f32[24,256]{1,0:T(8,128)S(1)}, u32[]{:S(2)}, u32[]{:S(2)}) collective-permute-start(f32[24,256]{1,0:T(8,128)S(1)} %get-tuple-element.70), channel_id=1, source_target_pairs={{0,96},{32,0},{64,32},{96,64},{1,97},{33,1},{65,33},{97,65},{2,98}... | collective-permute-start | bytes 73736 | tf_op jit(solution)/shard_map/ppermute | solution.py:483
  (15 other events, 38.2 us)

commit v3 on v2

--- a/solution.py
+++ b/solution.py
@@ -92,16 +92,28 @@
     )
 
 
-def start_groups(tile_count, group, *refs):
-    @pl.loop(0, groups_of(tile_count, group))
+def start_groups(tile_count, group, index_copies, *refs):
+    for copy in group_copies(0, group, *refs):
+        copy.start()
+    for copy in index_copies:
+        copy.start()
+
+    @pl.loop(1, groups_of(tile_count, group))
     def _(q):
         for copy in group_copies(q, group, *refs):
             copy.start()
 
 
+def index_fetch(row_in, col_in, tile_row, tile_col, sems):
+    return (
+        pltpu.make_async_copy(row_in, tile_row, sems.at[0]),
+        pltpu.make_async_copy(col_in, tile_col, sems.at[1]),
+    )
+
+
 def rows_first_kernel(
-    tile_row, tile_col, tile_count, tiles, own, one, two, three, out, hi_out, lo_out,
-    buf, hi, lo, lhs_hi, lhs_lo, sems, out_sems
+    row_in, col_in, tile_count, tiles, own, one, two, three, out, hi_out, lo_out,
+    buf, hi, lo, lhs_hi, lhs_lo, tile_row, tile_col, sems, out_sems, index_sems
 ):
     group = ROW_GROUP
     count = groups_of(tile_count, group)
@@ -110,12 +122,19 @@
         part = pl.ds(q * group, group)
         return pltpu.make_async_copy(tiles.at[0, 0, part], buf.at[part], sems.at[q])
 
-    @pl.loop(0, count)
+    arriving(0).start()
+    index_copies = index_fetch(row_in, col_in, tile_row, tile_col, index_sems)
+    for copy in index_copies:
+        copy.start()
+
+    @pl.loop(1, count)
     def _(q):
         arriving(q).start()
 
     fill_pieces((own, one, two, three), lhs_hi, lhs_lo, True)
     out[...] = jnp.zeros_like(out)
+    for copy in index_copies:
+        copy.wait()
 
     @pl.loop(0, count)
     def _(q):
@@ -136,12 +155,16 @@
 
 
 def rows_next_kernel(
-    tile_row, tile_col, tile_count, hi_in, lo_in, own, one, two, three, out, hi, lo, lhs_hi, lhs_lo, sems
+    row_in, col_in, tile_count, hi_in, lo_in, own, one, two, three, out,
+    hi, lo, lhs_hi, lhs_lo, tile_row, tile_col, sems, index_sems
 ):
     group = ROW_GROUP
-    start_groups(tile_count, group, hi_in, lo_in, hi, lo, sems)
+    index_copies = index_fetch(row_in, col_in, tile_row, tile_col, index_sems)
+    start_groups(tile_count, group, index_copies, hi_in, lo_in, hi, lo, sems)
     fill_pieces((own, one, two, three), lhs_hi, lhs_lo, False)
     out[...] = jnp.zeros_like(out)
+    for copy in index_copies:
+        copy.wait()
 
     @pl.loop(0, groups_of(tile_count, group))
     def _(q):
@@ -151,15 +174,25 @@
 
 
 def cols_kernel(
-    first, tile_row, tile_col, tile_count, hi_in, lo_in, near, far, own, one, two, three,
-    hi, lo, acc, sems
+    first, row_in, col_in, tile_count, hi_in, lo_in, near, far, own, one, two, three,
+    hi, lo, acc, tile_row, tile_col, sems, index_sems
 ):
     group = COL_GROUP
-    start_groups(tile_count, group, hi_in, lo_in, hi, lo, sems)
+    index_copies = index_fetch(row_in, col_in, tile_row, tile_col, index_sems)
+    start_groups(tile_count, group, index_copies, hi_in, lo_in, hi, lo, sems)
     acc[...] = jnp.zeros_like(acc)
-    gram = jnp.zeros_like(near[0, 16:24])
-    for p in range(near.shape[0]):
-        gram = gram + (near[p, 16:24] + far[p, 16:24])
+    if first:
+        total = jnp.zeros((16, 16), f32)
+        for part in (near, far):
+            for p in range(part.shape[0]):
+                total = total + dot_f32(part[p], part[p], ((1,), (1,)))
+        gram = pack_gram(total)
+    else:
+        gram = jnp.zeros_like(near[0, 16:24])
+        for p in range(near.shape[0]):
+            gram = gram + (near[p, 16:24] + far[p, 16:24])
+    for copy in index_copies:
+        copy.wait()
 
     @pl.loop(0, groups_of(tile_count, group))
     def _(q):
@@ -195,7 +228,7 @@
             pltpu.MemorySpace.HBM((slots, size, size), bf16),
             pltpu.MemorySpace.HBM((slots, size, size), bf16),
         ),
-        in_specs=[SMEM] * 3 + [HBM] + [VMEM] * 4,
+        in_specs=[HBM, HBM, SMEM] + [HBM] + [VMEM] * 4,
         out_specs=(VMEM, HBM, HBM),
         scratch_shapes=[
             pltpu.VMEM((slots, size, size), f32),
@@ -203,8 +236,11 @@
             pltpu.VMEM((slots, size, size), bf16),
             pltpu.VMEM((4, 48, size), bf16),
             pltpu.VMEM((4, 32, size), bf16),
+            pltpu.SMEM((1, 1, slots), jnp.int32),
+            pltpu.SMEM((1, 1, slots), jnp.int32),
             pltpu.SemaphoreType.DMA((slots // ROW_GROUP,)),
             pltpu.SemaphoreType.DMA((2, slots // ROW_GROUP)),
+            pltpu.SemaphoreType.DMA((2,)),
         ],
         compiler_params=limits(28),
         cost_estimate=cost(400_000_000),
@@ -217,14 +253,17 @@
         rows_next_kernel,
         name="rows_next",
         out_shape=jax.ShapeDtypeStruct((32, 16, size), f32),
-        in_specs=[SMEM] * 3 + [HBM] * 2 + [VMEM] * 4,
+        in_specs=[HBM, HBM, SMEM] + [HBM] * 2 + [VMEM] * 4,
         out_specs=VMEM,
         scratch_shapes=[
             pltpu.VMEM((slots, size, size), bf16),
             pltpu.VMEM((slots, size, size), bf16),
             pltpu.VMEM((4, 32, size), bf16),
             pltpu.VMEM((4, 16, size), bf16),
+            pltpu.SMEM((1, 1, slots), jnp.int32),
+            pltpu.SMEM((1, 1, slots), jnp.int32),
             pltpu.SemaphoreType.DMA((2, slots // ROW_GROUP)),
+            pltpu.SemaphoreType.DMA((2,)),
         ],
         compiler_params=limits(20),
         cost_estimate=cost(400_000_000),
@@ -239,13 +278,16 @@
         functools.partial(cols_kernel, first),
         name="cols_first" if first else "cols_next",
         out_shape=(out,) * 4,
-        in_specs=[SMEM] * 3 + [HBM] * 2 + [VMEM] * 2,
+        in_specs=[HBM, HBM, SMEM] + [HBM] * 2 + [VMEM] * 2,
         out_specs=(VMEM,) * 4,
         scratch_shapes=[
             pltpu.VMEM((slots, size, size), bf16),
             pltpu.VMEM((slots, size, size), bf16),
             pltpu.VMEM((4, height, size), f32),
+            pltpu.SMEM((1, 1, slots), jnp.int32),
+            pltpu.SMEM((1, 1, slots), jnp.int32),
             pltpu.SemaphoreType.DMA((2, slots // COL_GROUP)),
+            pltpu.SemaphoreType.DMA((2,)),
         ],
         compiler_params=limits(20),
         cost_estimate=cost(400_000_000),
@@ -460,24 +502,6 @@
     )(*args)
 
 
-def first_message_kernel(block, packed):
-    partial = dot_f32(block[...], block[...], ((1,), (1,)))
-    message = jnp.concatenate([block[...], pack_gram(partial)], axis=0)
-    for p in range(packed.shape[0]):
-        packed[p] = message
-
-
-def first_message(block):
-    return pl.pallas_call(
-        first_message_kernel,
-        name="first_message",
-        out_shape=jax.ShapeDtypeStruct((16, 24, block.shape[1]), f32),
-        in_specs=[VMEM],
-        out_specs=VMEM,
-        compiler_params=limits(8),
-    )(block)
-
-
 def shifted(value, hop):
     size = lax.axis_size("grp")
     return lax.ppermute(value, "grp", [(i, (i + hop) % size) for i in range(size)])
@@ -494,6 +518,7 @@
 def body(start_block, tile_values, tile_row, tile_col, tile_count):
     grp_size = lax.axis_size("grp")
     node_total = float(start_block.shape[1] * grp_size * lax.axis_size(COL))
+    message = jnp.broadcast_to(start_block, (lax.axis_size(ZX), *start_block.shape))
     place = tuple(
         pltpu.with_memory_space_constraint(part, pltpu.MemorySpace.HBM)
         for part in (tile_row, tile_col)
@@ -501,7 +526,6 @@
     place = (*place, tile_count)
     start_block = pltpu.with_memory_space_constraint(start_block, pltpu.MemorySpace.HBM)
     tile_values = pltpu.with_memory_space_constraint(tile_values, pltpu.MemorySpace.HBM)
-    message = first_message(start_block)
     piece = start_block
     state = degree = shift = hi = lo = None
     lowers, coeffs = [], []

time: 214 us -> 209 us (0.977)
  Pallas kernels: 54.7 us -> 48.4 us
  waiting for transfers between devices: 31.3 us -> 33.9 us
    pallas_call x4, Pallas kernels: 14.3 us -> 11.6 us  [cols_product(): pl.pallas_call(functools.partial(cols_kernel, first), name='cols_first' i...]
    ppermute x24, waiting for transfers between devices: 10 us -> 12.6 us  [shifted(): lax.ppermute(value, 'grp', [(i, (i + hop) % size) for i in range(size)])]
  transfers between devices with their start and end apart: 36 -> 36, of which waited for: 17 -> 20; matrix products, arithmetic and copies ran while one was open for 0% -> 0% of each run, Pallas kernels for 17% -> 15%
where the time goes in v3:
time: 209 us; the launch traced here: 207 us
  starting transfers between devices  98.2 us (47%)
  Pallas kernels  48.4 us (23%)
  waiting for transfers between devices  33.9 us (16%)
  blocking collectives  22.9 us (11%)
    all_to_all x8, starting transfers between devices, exchanged(): return lax.all_to_all(value, axes, split_axis=0, concat_axis=0, tiled=True)  69.1 us
    ppermute x24, starting transfers between devices, shifted(): lax.ppermute(value, 'grp', [(i, (i + hop) % size) for i in range(size)])  27.8 us
    all_to_all x2, blocking collectives, exchanged(): return lax.all_to_all(value, axes, split_axis=0, concat_axis=0, tiled=True)  22.9 us
    all_to_all x8, waiting for transfers between devices, exchanged(): return lax.all_to_all(value, axes, split_axis=0, concat_axis=0, tiled=True)  15.5 us
    pallas_call x4, Pallas kernels, update(): pl.pallas_call(functools.partial(update_kernel, step, node_total), out_sh...  13.5 us
    pallas_call x3, Pallas kernels, rows_next(): pl.pallas_call(rows_next_kernel, name='rows_next', out_shape=jax.ShapeDty...  13.5 us
    ppermute x24, waiting for transfers between devices, shifted(): lax.ppermute(value, 'grp', [(i, (i + hop) % size) for i in range(size)])  12.6 us
    pallas_call x4, Pallas kernels, cols_product(): pl.pallas_call(functools.partial(cols_kernel, first), name='cols_first' i...  11.6 us
  transfers between devices with their start and end apart: 36, of which 20 were waited for; matrix products, arithmetic and copies ran while one was open for 0% of the time, Pallas kernels for 15%

profile of v3, /device:TPU:1, one launch (start us, length us, event | category | flops | bytes accessed | tf_op | source)
XLA Modules:
  0.0 207.0 jit_solution(6322096709749247666)
XLA Ops:
  2.1 8.4 %all-to-all-start.1 = ((f32[16,16,256]{2,1,0:T(8,128)}), f32[16,16,256]{2,1,0:T(8,128)S(1)}, u32[]{:S(2)}, u32[]{:S(2)}) async-start(f32[16,16,256]{2,1,0:T(8,128)} %broadcast_in_dim.3), calls=%async_computation.1 | async-start | bytes 524288 | tf_op jit(solution)/shard_map/all_to_all | solution.py:515
  18.2 6.8 %rows_first.1 = (f32[32,24,256]{2,1,0:T(8,128)}, bf16[32,256,256]{2,1,0:T(8,128)(2,1)}, bf16[32,256,256]{2,1,0:T(8,128)(2,1)}) custom-call(s32[1,1,32]{2,1,0:T(1,128)} %row_in.15, s32[1,1,32]{2,1,0:T(1,128)} %col_in.15, s32[1,1]{1,0:T(1,128)S(6)} %copy.8.tile_count, f32[1,1,32,256,256]{4,3,2,1,0:T(8,128)} %tiles.1, f32[16,256]{1,0:T(8,128)} %refs_5_.1, ...), custom_call_target="tpu_custom_call" | custom-call | flops 400000000 | bytes 1048576 | tf_op jit(solution)/shard_map/rows_first/pallas_call | solution.py:223
  25.0 10.7 %all-to-all-start = ((f32[32,24,256]{2,1,0:T(8,128)}), f32[32,24,256]{2,1,0:T(8,128)S(1)}, u32[]{:S(2)}, u32[]{:S(2)}) async-start(f32[32,24,256]{2,1,0:T(8,128)} %get-tuple-element.44), calls=%async_computation | async-start | bytes 1572864 | tf_op jit(solution)/shard_map/all_to_all | solution.py:515
  46.2 3.7 %all-to-all-done.refs_0_ = f32[32,24,256]{2,1,0:T(8,128)S(1)} async-done(((f32[32,24,256]{2,1,0:T(8,128)}), f32[32,24,256]{2,1,0:T(8,128)S(1)}, u32[]{:S(2)}, u32[]{:S(2)}) %all-to-all-start) | async-done | bytes 786464 | tf_op jit(solution)/shard_map/all_to_all | solution.py:515
  49.9 3.8 %shard_map.76 = (f32[16,24,256]{2,1,0:T(8,128)}, f32[16,256]{1,0:T(8,128)S(1)}, f32[16,512]{1,0:T(8,128)S(1)}, f32[8,256]{1,0:T(8,128)S(1)}, f32[16,16]{1,0:T(8,128)S(1)}) custom-call(f32[32,24,256]{2,1,0:T(8,128)S(1)} %all-to-all-done.refs_0_, f32[32,256]{1,0:T(8,128)S(1)} %get-tuple-element.45.refs_1_, f32[32,256]{1,0:T(8,128)S(1)} %collective-permute-done.4.refs_2_, ...), custom_call_target="tpu_custom_call" | custom-call | flops 400000000 | bytes 1048576 | tf_op jit(solution)/shard_map/pallas_call | solution.py:431
  53.7 3.6 %all-to-all-start.3 = ((f32[16,24,256]{2,1,0:T(8,128)}), f32[16,24,256]{2,1,0:T(8,128)S(1)}, u32[]{:S(2)}, u32[]{:S(2)}) async-start(f32[16,24,256]{2,1,0:T(8,128)} %get-tuple-element.50), calls=%async_computation.3 | async-start | bytes 786432 | tf_op jit(solution)/shard_map/all_to_all | solution.py:515
  57.9 3.5 %collective-permute-start.8 = (f32[16,256]{1,0:T(8,128)S(1)}, f32[16,256]{1,0:T(8,128)S(1)}, u32[]{:S(2)}, u32[]{:S(2)}) collective-permute-start(f32[16,256]{1,0:T(8,128)S(1)} %get-tuple-element.49.own), channel_id=1, source_target_pairs={{0,64},{32,96},{64,0},{96,32},{1,65},{33,97},{65,1},{97,33},{2,66}... | collective-permute-start | bytes 49160 | tf_op jit(solution)/shard_map/ppermute | solution.py:507
  64.3 4.5 %rows_next.3 = f32[32,16,256]{2,1,0:T(8,128)} custom-call(s32[1,1,32]{2,1,0:T(1,128)} %row_in.15, s32[1,1,32]{2,1,0:T(1,128)} %col_in.15, s32[1,1]{1,0:T(1,128)S(6)} %copy.8.tile_count, bf16[32,256,256]{2,1,0:T(8,128)(2,1)} %get-tuple-element.42.hi_in, bf16[32,256,256]{2,1,0:T(8,128)(2,1)} %get-tuple-element.43.lo_in, f32[16,256]{1,0:T(8,128)S(1)} %get-tuple-element.49.own, ...), custom_call_target="tpu_custom_call" | custom-call | flops 400000000 | bytes 1048576 | tf_op jit(solution)/shard_map/rows_next/pallas_call | solution.py:252
  68.8 11.1 %all-to-all-start.2 = ((f32[32,16,256]{2,1,0:T(8,128)}), f32[32,16,256]{2,1,0:T(8,128)S(1)}, u32[]{:S(2)}, u32[]{:S(2)}) async-start(f32[32,16,256]{2,1,0:T(8,128)} %rows_next.3), calls=%async_computation.2 | async-start | bytes 1048576 | tf_op jit(solution)/shard_map/all_to_all | solution.py:515
  87.4 4.0 %all-to-all-done.2.refs_0_ = f32[32,16,256]{2,1,0:T(8,128)S(1)} async-done(((f32[32,16,256]{2,1,0:T(8,128)}), f32[32,16,256]{2,1,0:T(8,128)S(1)}, u32[]{:S(2)}, u32[]{:S(2)}) %all-to-all-start.2) | async-done | bytes 524320 | tf_op jit(solution)/shard_map/all_to_all | solution.py:515
  91.4 3.4 %shard_map.77 = (f32[16,24,256]{2,1,0:T(8,128)}, f32[16,256]{1,0:T(8,128)S(1)}, f32[32,512]{1,0:T(8,128)S(1)}, f32[16,128]{1,0:T(8,128)S(1)}, f32[16,16]{1,0:T(8,128)S(1)}, /*index=5*/f32[8,128]{1,0:T(8,128)S(1)}) custom-call(f32[32,16,256]{2,1,0:T(8,128)S(1)} %all-to-all-done.2.refs_0_, f32[24,256]{1,0:T(8,128)S(1)} %get-tuple-element.51.refs_1_, ...), custom_call_target="tpu_custom_call" | custom-call | flops 400000000 | bytes 1048576 | tf_op jit(solution)/shard_map/pallas_call | solution.py:431
  94.7 5.6 %all-to-all-start.5 = ((f32[16,24,256]{2,1,0:T(8,128)}), f32[16,24,256]{2,1,0:T(8,128)S(1)}, u32[]{:S(2)}, u32[]{:S(2)}) async-start(f32[16,24,256]{2,1,0:T(8,128)} %get-tuple-element.58), calls=%async_computation.5 | async-start | bytes 786432 | tf_op jit(solution)/shard_map/all_to_all | solution.py:515
  106.8 4.5 %rows_next.4 = f32[32,16,256]{2,1,0:T(8,128)} custom-call(s32[1,1,32]{2,1,0:T(1,128)} %row_in.15, s32[1,1,32]{2,1,0:T(1,128)} %col_in.15, s32[1,1]{1,0:T(1,128)S(6)} %copy.8.tile_count, bf16[32,256,256]{2,1,0:T(8,128)(2,1)} %get-tuple-element.42.hi_in, bf16[32,256,256]{2,1,0:T(8,128)(2,1)} %get-tuple-element.43.lo_in, f32[16,256]{1,0:T(8,128)S(1)} %get-tuple-element.57.own, ...), custom_call_target="tpu_custom_call" | custom-call | flops 400000000 | bytes 1048576 | tf_op jit(solution)/shard_map/rows_next/pallas_call | solution.py:252
  111.3 11.9 %all-to-all-start.4 = ((f32[32,16,256]{2,1,0:T(8,128)}), f32[32,16,256]{2,1,0:T(8,128)S(1)}, u32[]{:S(2)}, u32[]{:S(2)}) async-start(f32[32,16,256]{2,1,0:T(8,128)} %rows_next.4), calls=%async_computation.4 | async-start | bytes 1048576 | tf_op jit(solution)/shard_map/all_to_all | solution.py:515
  130.8 3.8 %all-to-all-done.4.refs_0_ = f32[32,16,256]{2,1,0:T(8,128)S(1)} async-done(((f32[32,16,256]{2,1,0:T(8,128)}), f32[32,16,256]{2,1,0:T(8,128)S(1)}, u32[]{:S(2)}, u32[]{:S(2)}) %all-to-all-start.4) | async-done | bytes 524320 | tf_op jit(solution)/shard_map/all_to_all | solution.py:515
  134.6 3.3 %shard_map.78 = (f32[16,24,256]{2,1,0:T(8,128)}, f32[16,256]{1,0:T(8,128)S(1)}, f32[48,512]{1,0:T(8,128)S(1)}, f32[16,128]{1,0:T(8,128)S(1)}, f32[16,16]{1,0:T(8,128)S(1)}) custom-call(f32[32,16,256]{2,1,0:T(8,128)S(1)} %all-to-all-done.4.refs_0_, f32[24,256]{1,0:T(8,128)S(1)} %get-tuple-element.59.refs_1_, f32[24,256]{1,0:T(8,128)S(1)} %collective-permute-done.18.refs_2_, ...), custom_call_target="tpu_custom_call" | custom-call | flops 400000000 | bytes 1048576 | tf_op jit(solution)/shard_map/pallas_call | solution.py:431
  138.0 5.8 %all-to-all-start.7 = ((f32[16,24,256]{2,1,0:T(8,128)}), f32[16,24,256]{2,1,0:T(8,128)S(1)}, u32[]{:S(2)}, u32[]{:S(2)}) async-start(f32[16,24,256]{2,1,0:T(8,128)} %get-tuple-element.66), calls=%async_computation.7 | async-start | bytes 786432 | tf_op jit(solution)/shard_map/all_to_all | solution.py:515
  150.2 4.5 %rows_next.5 = f32[32,16,256]{2,1,0:T(8,128)} custom-call(s32[1,1,32]{2,1,0:T(1,128)} %row_in.15, s32[1,1,32]{2,1,0:T(1,128)} %col_in.15, s32[1,1]{1,0:T(1,128)S(6)} %copy.8.tile_count, bf16[32,256,256]{2,1,0:T(8,128)(2,1)} %get-tuple-element.42.hi_in, bf16[32,256,256]{2,1,0:T(8,128)(2,1)} %get-tuple-element.43.lo_in, f32[16,256]{1,0:T(8,128)S(1)} %get-tuple-element.65.own, ...), custom_call_target="tpu_custom_call" | custom-call | flops 400000000 | bytes 1048576 | tf_op jit(solution)/shard_map/rows_next/pallas_call | solution.py:252
  154.7 11.9 %all-to-all-start.6 = ((f32[32,16,256]{2,1,0:T(8,128)}), f32[32,16,256]{2,1,0:T(8,128)S(1)}, u32[]{:S(2)}, u32[]{:S(2)}) async-start(f32[32,16,256]{2,1,0:T(8,128)} %rows_next.5), calls=%async_computation.6 | async-start | bytes 1048576 | tf_op jit(solution)/shard_map/all_to_all | solution.py:515
  174.1 4.0 %all-to-all-done.6.refs_0_ = f32[32,16,256]{2,1,0:T(8,128)S(1)} async-done(((f32[32,16,256]{2,1,0:T(8,128)}), f32[32,16,256]{2,1,0:T(8,128)S(1)}, u32[]{:S(2)}, u32[]{:S(2)}) %all-to-all-start.6) | async-done | bytes 524320 | tf_op jit(solution)/shard_map/all_to_all | solution.py:515
  178.0 3.0 %shard_map.79 = (f32[8,8,256]{2,1,0:T(8,128)S(1)}, f32[16,256]{1,0:T(8,128)}, f32[64,512]{1,0:T(8,128)S(1)}, f32[16,128]{1,0:T(8,128)S(1)}, f32[16,16]{1,0:T(8,128)S(1)}) custom-call(f32[32,16,256]{2,1,0:T(8,128)S(1)} %all-to-all-done.6.refs_0_, f32[24,256]{1,0:T(8,128)S(1)} %get-tuple-element.67.refs_1_, f32[24,256]{1,0:T(8,128)S(1)} %collective-permute-done.25.refs_2_, ...), custom_call_target="tpu_custom_call" | custom-call | flops 400000000 | bytes 1048576 | tf_op jit(solution)/shard_map/pallas_call | solution.py:431
  181.0 9.6 %all_to_all.50.arrived = f32[8,8,256]{2,1,0:T(8,128)S(1)} all-to-all(f32[8,8,256]{2,1,0:T(8,128)S(1)} %get-tuple-element.72), channel_id=1, replica_groups=mesh['grp'=4,'col_0'=4,'col_1'=4,'col_2'=2] {'col_1','col_2'}, dimensions={0} | all-to-all | bytes 131072 | tf_op jit(solution)/shard_map/all_to_all | solution.py:515
  190.6 13.4 %all_to_all.51.arrived = f32[16,8,256]{2,1,0:T(8,128)S(1)} all-to-all(f32[16,8,256]{2,1,0:T(8,128)S(1)} %fold.1), channel_id=1, replica_groups=mesh['grp'=4,'col_0'=4,'col_1'=4,'col_2'=2] {'grp','col_0'}, dimensions={0} | all-to-all | bytes 262144 | tf_op jit(solution)/shard_map/all_to_all | solution.py:515
  203.9 3.0 %last.1 = (f32[5,16,256]{2,1,0:T(8,128)}, f32[4,4,16,16]{3,2,1,0:T(8,128)}, f32[5,16,16]{2,1,0:T(8,128)}) custom-call(f32[16,8,256]{2,1,0:T(8,128)S(1)} %all_to_all.51.arrived, f32[64,512]{1,0:T(8,128)S(1)} %get-tuple-element.73.state, f32[8,128]{1,0:T(8,128)S(1)} %get-tuple-element.64.refs_7_.shift, f32[16,128]{1,0:T(8,128)S(1)} %get-tuple-element.74.refs_0_, ...), custom_call_target="tpu_custom_call" | custom-call | tf_op jit(solution)/shard_map/last/pallas_call | solution.py:491
  (71 shorter events, 57.7 us)
Async XLA Ops:
  2.1 22.9 %all-to-all-start.1 = ((f32[16,16,256]{2,1,0:T(8,128)}), f32[16,16,256]{2,1,0:T(8,128)S(1)}, u32[]{:S(2)}, u32[]{:S(2)}) async-start(f32[16,16,256]{2,1,0:T(8,128)} %broadcast_in_dim.3), calls=%async_computation.1 | async-start | bytes 524288 | tf_op jit(solution)/shard_map/all_to_all | solution.py:515
  10.5 5.7 %collective-permute-start = (f32[16,256]{1,0:T(8,128)}, f32[16,256]{1,0:T(8,128)S(1)}, u32[]{:S(2)}, u32[]{:S(2)}) collective-permute-start(f32[16,256]{1,0:T(8,128)} %refs_5_.1), channel_id=1, source_target_pairs={{0,32},{32,64},{64,96},{96,0},{1,33},{33,65},{65,97},{97,1},{2,34}... | collective-permute-start | bytes 49160 | tf_op jit(solution)/shard_map/ppermute | solution.py:507
  11.9 4.4 %collective-permute-start.1 = (f32[16,256]{1,0:T(8,128)}, f32[16,256]{1,0:T(8,128)S(1)}, u32[]{:S(2)}, u32[]{:S(2)}) collective-permute-start(f32[16,256]{1,0:T(8,128)} %refs_5_.1), channel_id=1, source_target_pairs={{0,64},{32,96},{64,0},{96,32},{1,65},{33,97},{65,1},{97,33},{2,66}... | collective-permute-start | bytes 49160 | tf_op jit(solution)/shard_map/ppermute | solution.py:507
  25.0 25.0 %all-to-all-start = ((f32[32,24,256]{2,1,0:T(8,128)}), f32[32,24,256]{2,1,0:T(8,128)S(1)}, u32[]{:S(2)}, u32[]{:S(2)}) async-start(f32[32,24,256]{2,1,0:T(8,128)} %get-tuple-element.44), calls=%async_computation | async-start | bytes 1572864 | tf_op jit(solution)/shard_map/all_to_all | solution.py:515
  40.2 4.3 %collective-permute-start.4 = (f32[32,256]{1,0:T(8,128)S(1)}, f32[32,256]{1,0:T(8,128)S(1)}, u32[]{:S(2)}, u32[]{:S(2)}) collective-permute-start(f32[32,256]{1,0:T(8,128)S(1)} %get-tuple-element.46), channel_id=1, source_target_pairs={{0,32},{32,64},{64,96},{96,0},{1,33},{33,65},{65,97},{97,1},{2,34}... | collective-permute-start | bytes 98312 | tf_op jit(solution)/shard_map/ppermute | solution.py:507
  40.5 4.6 %collective-permute-start.5 = (f32[32,256]{1,0:T(8,128)S(1)}, f32[32,256]{1,0:T(8,128)S(1)}, u32[]{:S(2)}, u32[]{:S(2)}) collective-permute-start(f32[32,256]{1,0:T(8,128)S(1)} %get-tuple-element.47), channel_id=1, source_target_pairs={{0,64},{32,96},{64,0},{96,32},{1,65},{33,97},{65,1},{97,33},{2,66}... | collective-permute-start | bytes 98312 | tf_op jit(solution)/shard_map/ppermute | solution.py:507
  53.7 15.0 %all-to-all-start.3 = ((f32[16,24,256]{2,1,0:T(8,128)}), f32[16,24,256]{2,1,0:T(8,128)S(1)}, u32[]{:S(2)}, u32[]{:S(2)}) async-start(f32[16,24,256]{2,1,0:T(8,128)} %get-tuple-element.50), calls=%async_computation.3 | async-start | bytes 786432 | tf_op jit(solution)/shard_map/all_to_all | solution.py:515
  57.3 4.1 %collective-permute-start.7 = (f32[16,256]{1,0:T(8,128)S(1)}, f32[16,256]{1,0:T(8,128)S(1)}, u32[]{:S(2)}, u32[]{:S(2)}) collective-permute-start(f32[16,256]{1,0:T(8,128)S(1)} %get-tuple-element.49.own), channel_id=1, source_target_pairs={{0,32},{32,64},{64,96},{96,0},{1,33},{33,65},{65,97},{97,1},{2,34}... | collective-permute-start | bytes 49160 | tf_op jit(solution)/shard_map/ppermute | solution.py:507
  57.9 4.8 %collective-permute-start.8 = (f32[16,256]{1,0:T(8,128)S(1)}, f32[16,256]{1,0:T(8,128)S(1)}, u32[]{:S(2)}, u32[]{:S(2)}) collective-permute-start(f32[16,256]{1,0:T(8,128)S(1)} %get-tuple-element.49.own), channel_id=1, source_target_pairs={{0,64},{32,96},{64,0},{96,32},{1,65},{33,97},{65,1},{97,33},{2,66}... | collective-permute-start | bytes 49160 | tf_op jit(solution)/shard_map/ppermute | solution.py:507
  68.8 22.6 %all-to-all-start.2 = ((f32[32,16,256]{2,1,0:T(8,128)}), f32[32,16,256]{2,1,0:T(8,128)S(1)}, u32[]{:S(2)}, u32[]{:S(2)}) async-start(f32[32,16,256]{2,1,0:T(8,128)} %rows_next.3), calls=%async_computation.2 | async-start | bytes 1048576 | tf_op jit(solution)/shard_map/all_to_all | solution.py:515
  84.6 6.7 %collective-permute-start.11 = (f32[24,256]{1,0:T(8,128)S(1)}, f32[24,256]{1,0:T(8,128)S(1)}, u32[]{:S(2)}, u32[]{:S(2)}) collective-permute-start(f32[24,256]{1,0:T(8,128)S(1)} %get-tuple-element.52), channel_id=1, source_target_pairs={{0,32},{32,64},{64,96},{96,0},{1,33},{33,65},{65,97},{97,1},{2,34}... | collective-permute-start | bytes 73736 | tf_op jit(solution)/shard_map/ppermute | solution.py:507
  84.7 6.6 %collective-permute-start.12 = (f32[24,256]{1,0:T(8,128)S(1)}, f32[24,256]{1,0:T(8,128)S(1)}, u32[]{:S(2)}, u32[]{:S(2)}) collective-permute-start(f32[24,256]{1,0:T(8,128)S(1)} %get-tuple-element.53), channel_id=1, source_target_pairs={{0,64},{32,96},{64,0},{96,32},{1,65},{33,97},{65,1},{97,33},{2,66}... | collective-permute-start | bytes 73736 | tf_op jit(solution)/shard_map/ppermute | solution.py:507
  86.4 4.9 %collective-permute-start.13 = (f32[24,256]{1,0:T(8,128)S(1)}, f32[24,256]{1,0:T(8,128)S(1)}, u32[]{:S(2)}, u32[]{:S(2)}) collective-permute-start(f32[24,256]{1,0:T(8,128)S(1)} %get-tuple-element.54), channel_id=1, source_target_pairs={{0,96},{32,0},{64,32},{96,64},{1,97},{33,1},{65,33},{97,65},{2,98}... | collective-permute-start | bytes 73736 | tf_op jit(solution)/shard_map/ppermute | solution.py:507
  94.7 16.5 %all-to-all-start.5 = ((f32[16,24,256]{2,1,0:T(8,128)}), f32[16,24,256]{2,1,0:T(8,128)S(1)}, u32[]{:S(2)}, u32[]{:S(2)}) async-start(f32[16,24,256]{2,1,0:T(8,128)} %get-tuple-element.58), calls=%async_computation.5 | async-start | bytes 786432 | tf_op jit(solution)/shard_map/all_to_all | solution.py:515
  101.4 4.1 %collective-permute-start.15 = (f32[16,256]{1,0:T(8,128)S(1)}, f32[16,256]{1,0:T(8,128)S(1)}, u32[]{:S(2)}, u32[]{:S(2)}) collective-permute-start(f32[16,256]{1,0:T(8,128)S(1)} %get-tuple-element.57.own), channel_id=1, source_target_pairs={{0,64},{32,96},{64,0},{96,32},{1,65},{33,97},{65,1},{97,33},{2,66}... | collective-permute-start | bytes 49160 | tf_op jit(solution)/shard_map/ppermute | solution.py:507
  111.3 23.4 %all-to-all-start.4 = ((f32[32,16,256]{2,1,0:T(8,128)}), f32[32,16,256]{2,1,0:T(8,128)S(1)}, u32[]{:S(2)}, u32[]{:S(2)}) async-start(f32[32,16,256]{2,1,0:T(8,128)} %rows_next.4), calls=%async_computation.4 | async-start | bytes 1048576 | tf_op jit(solution)/shard_map/all_to_all | solution.py:515
  127.9 6.7 %collective-permute-start.18 = (f32[24,256]{1,0:T(8,128)S(1)}, f32[24,256]{1,0:T(8,128)S(1)}, u32[]{:S(2)}, u32[]{:S(2)}) collective-permute-start(f32[24,256]{1,0:T(8,128)S(1)} %get-tuple-element.60), channel_id=1, source_target_pairs={{0,32},{32,64},{64,96},{96,0},{1,33},{33,65},{65,97},{97,1},{2,34}... | collective-permute-start | bytes 73736 | tf_op jit(solution)/shard_map/ppermute | solution.py:507
  128.2 6.5 %collective-permute-start.19 = (f32[24,256]{1,0:T(8,128)S(1)}, f32[24,256]{1,0:T(8,128)S(1)}, u32[]{:S(2)}, u32[]{:S(2)}) collective-permute-start(f32[24,256]{1,0:T(8,128)S(1)} %get-tuple-element.61), channel_id=1, source_target_pairs={{0,64},{32,96},{64,0},{96,32},{1,65},{33,97},{65,1},{97,33},{2,66}... | collective-permute-start | bytes 73736 | tf_op jit(solution)/shard_map/ppermute | solution.py:507
  129.9 4.7 %collective-permute-start.20 = (f32[24,256]{1,0:T(8,128)S(1)}, f32[24,256]{1,0:T(8,128)S(1)}, u32[]{:S(2)}, u32[]{:S(2)}) collective-permute-start(f32[24,256]{1,0:T(8,128)S(1)} %get-tuple-element.62), channel_id=1, source_target_pairs={{0,96},{32,0},{64,32},{96,64},{1,97},{33,1},{65,33},{97,65},{2,98}... | collective-permute-start | bytes 73736 | tf_op jit(solution)/shard_map/ppermute | solution.py:507
  138.0 16.7 %all-to-all-start.7 = ((f32[16,24,256]{2,1,0:T(8,128)}), f32[16,24,256]{2,1,0:T(8,128)S(1)}, u32[]{:S(2)}, u32[]{:S(2)}) async-start(f32[16,24,256]{2,1,0:T(8,128)} %get-tuple-element.66), calls=%async_computation.7 | async-start | bytes 786432 | tf_op jit(solution)/shard_map/all_to_all | solution.py:515
  154.7 23.4 %all-to-all-start.6 = ((f32[32,16,256]{2,1,0:T(8,128)}), f32[32,16,256]{2,1,0:T(8,128)S(1)}, u32[]{:S(2)}, u32[]{:S(2)}) async-start(f32[32,16,256]{2,1,0:T(8,128)} %rows_next.5), calls=%async_computation.6 | async-start | bytes 1048576 | tf_op jit(solution)/shard_map/all_to_all | solution.py:515
  171.3 6.7 %collective-permute-start.25 = (f32[24,256]{1,0:T(8,128)S(1)}, f32[24,256]{1,0:T(8,128)S(1)}, u32[]{:S(2)}, u32[]{:S(2)}) collective-permute-start(f32[24,256]{1,0:T(8,128)S(1)} %get-tuple-element.68), channel_id=1, source_target_pairs={{0,32},{32,64},{64,96},{96,0},{1,33},{33,65},{65,97},{97,1},{2,34}... | collective-permute-start | bytes 73736 | tf_op jit(solution)/shard_map/ppermute | solution.py:507
  171.4 6.6 %collective-permute-start.26 = (f32[24,256]{1,0:T(8,128)S(1)}, f32[24,256]{1,0:T(8,128)S(1)}, u32[]{:S(2)}, u32[]{:S(2)}) collective-permute-start(f32[24,256]{1,0:T(8,128)S(1)} %get-tuple-element.69), channel_id=1, source_target_pairs={{0,64},{32,96},{64,0},{96,32},{1,65},{33,97},{65,1},{97,33},{2,66}... | collective-permute-start | bytes 73736 | tf_op jit(solution)/shard_map/ppermute | solution.py:507
  173.1 4.9 %collective-permute-start.27 = (f32[24,256]{1,0:T(8,128)S(1)}, f32[24,256]{1,0:T(8,128)S(1)}, u32[]{:S(2)}, u32[]{:S(2)}) collective-permute-start(f32[24,256]{1,0:T(8,128)S(1)} %get-tuple-element.70), channel_id=1, source_target_pairs={{0,96},{32,0},{64,32},{96,64},{1,97},{33,1},{65,33},{97,65},{2,98}... | collective-permute-start | bytes 73736 | tf_op jit(solution)/shard_map/ppermute | solution.py:507
  (15 other events, 37.2 us)

commit v4 on v3

--- a/solution.py
+++ b/solution.py
@@ -14,6 +14,7 @@
 GRP_COL = ("grp", "col_0", "col_1", "col_2")
 ROW_GROUP = 8
 COL_GROUP = 4
+FACTOR_GROUP = 8
 highest = lax.Precision.HIGHEST
 VMEM = pl.BlockSpec(memory_space=pltpu.VMEM)
 SMEM = pl.BlockSpec(memory_space=pltpu.SMEM)
@@ -318,14 +319,39 @@
     down = jnp.ones((16, 128), f32)
     across = jnp.ones((16, 128), f32)
     lower = jnp.zeros((16, 128), f32)
-    for j in range(16):
-        column = jnp.broadcast_to(work[:, j : j + 1], (16, 128))
-        pivot = jnp.broadcast_to(column[j : j + 1], (16, 128))
-        row = jnp.broadcast_to(work[j : j + 1], (16, 128))
-        down = jnp.where(rows == j, pivot, down)
-        across = jnp.where(lanes == j, pivot, across)
-        lower = jnp.where((lanes == j) & (rows >= j), column, lower)
-        work = work - jnp.where(rows > j, column / pivot, 0.0) * row
+
+    def half(x):
+        return jnp.broadcast_to(x, (8, 128))
+
+    def full(x):
+        return jnp.concatenate([x, x], axis=0)
+
+    for base in range(0, 16, FACTOR_GROUP):
+        group = range(FACTOR_GROUP)
+        columns = [jnp.broadcast_to(work[:, base + i : base + i + 1], (16, 128)) for i in group]
+        across_rows = [half(work[base + i : base + i + 1]) for i in group]
+        corner = {
+            (i, k): half(work[base + i : base + i + 1, base + k : base + k + 1])
+            for i in group
+            for k in range(i + 1)
+        }
+        scaled = []
+        for i in group:
+            pivot = corner[i, i]
+            inverse = 1.0 / pivot
+            for k in range(i + 1, FACTOR_GROUP):
+                ratio = corner[k, i] * inverse
+                columns[k] = columns[k] - columns[i] * full(ratio)
+                across_rows[k] = across_rows[k] - across_rows[i] * ratio
+                for m in range(k, FACTOR_GROUP):
+                    corner[m, k] = corner[m, k] - ratio * corner[m, i]
+            scaled.append(across_rows[i] * inverse)
+            at = base + i
+            down = jnp.where(rows == at, full(pivot), down)
+            across = jnp.where(lanes == at, full(pivot), across)
+            lower = jnp.where((lanes == at) & (rows >= at), columns[i], lower)
+        for i in group:
+            work = work - jnp.where(rows > base + i, columns[i], 0.0) * full(scaled[i])
     lower = lower / jnp.sqrt(across)
     inverse = work / jnp.sqrt(down)
     return lower[:, 0:16], inverse[:, 16:32]

time: 209 us -> 202 us (0.967)
  Pallas kernels: 48.4 us -> 41 us
    pallas_call x4, Pallas kernels: 13.5 us -> 7.61 us  [update(): pl.pallas_call(functools.partial(update_kernel, step, node_total), out_sh...]
  transfers between devices with their start and end apart: 36 -> 36, of which waited for: 20 -> 20; matrix products, arithmetic and copies ran while one was open for 0% -> 0% of each run, Pallas kernels for 15% -> 16%
where the time goes in v4:
time: 202 us; the launch traced here: 200 us
  starting transfers between devices  98.2 us (49%)
  Pallas kernels  41 us (20%)
  waiting for transfers between devices  33.9 us (17%)
  blocking collectives  22.9 us (11%)
  local copies, waits for them, and re-layouts  2.05 us (1%)
    all_to_all x8, starting transfers between devices, exchanged(): return lax.all_to_all(value, axes, split_axis=0, concat_axis=0, tiled=True)  69.1 us
    ppermute x24, starting transfers between devices, shifted(): lax.ppermute(value, 'grp', [(i, (i + hop) % size) for i in range(size)])  27.8 us
    all_to_all x2, blocking collectives, exchanged(): return lax.all_to_all(value, axes, split_axis=0, concat_axis=0, tiled=True)  22.9 us
    all_to_all x8, waiting for transfers between devices, exchanged(): return lax.all_to_all(value, axes, split_axis=0, concat_axis=0, tiled=True)  15.5 us
    pallas_call x3, Pallas kernels, rows_next(): pl.pallas_call(rows_next_kernel, name='rows_next', out_shape=jax.ShapeDty...  13.5 us
    ppermute x24, waiting for transfers between devices, shifted(): lax.ppermute(value, 'grp', [(i, (i + hop) % size) for i in range(size)])  12.6 us
    pallas_call x4, Pallas kernels, cols_product(): pl.pallas_call(functools.partial(cols_kernel, first), name='cols_first' i...  11.6 us
    pallas_call x4, Pallas kernels, update(): pl.pallas_call(functools.partial(update_kernel, step, node_total), out_sh...  7.61 us
  transfers between devices with their start and end apart: 36, of which 20 were waited for; matrix products, arithmetic and copies ran while one was open for 0% of the time, Pallas kernels for 16%

profile of v4, /device:TPU:1, one launch (start us, length us, event | category | flops | bytes accessed | tf_op | source)
XLA Modules:
  0.0 199.6 jit_solution(243203942596473885)
XLA Ops:
  2.1 8.4 %all-to-all-start.1 = ((f32[16,16,256]{2,1,0:T(8,128)}), f32[16,16,256]{2,1,0:T(8,128)S(1)}, u32[]{:S(2)}, u32[]{:S(2)}) async-start(f32[16,16,256]{2,1,0:T(8,128)} %broadcast_in_dim.3), calls=%async_computation.1 | async-start | bytes 524288 | tf_op jit(solution)/shard_map/all_to_all | solution.py:541
  11.9 2.6 %collective-permute-start.1 = (f32[16,256]{1,0:T(8,128)}, f32[16,256]{1,0:T(8,128)S(1)}, u32[]{:S(2)}, u32[]{:S(2)}) collective-permute-start(f32[16,256]{1,0:T(8,128)} %refs_5_.1), channel_id=1, source_target_pairs={{0,64},{32,96},{64,0},{96,32},{1,65},{33,97},{65,1},{97,33},{2,66}... | collective-permute-start | bytes 49160 | tf_op jit(solution)/shard_map/ppermute | solution.py:533
  18.2 6.8 %rows_first.1 = (f32[32,24,256]{2,1,0:T(8,128)}, bf16[32,256,256]{2,1,0:T(8,128)(2,1)}, bf16[32,256,256]{2,1,0:T(8,128)(2,1)}) custom-call(s32[1,1,32]{2,1,0:T(1,128)} %row_in.15, s32[1,1,32]{2,1,0:T(1,128)} %col_in.15, s32[1,1]{1,0:T(1,128)S(6)} %copy.8.tile_count, f32[1,1,32,256,256]{4,3,2,1,0:T(8,128)} %tiles.1, f32[16,256]{1,0:T(8,128)} %refs_5_.1, ...), custom_call_target="tpu_custom_call" | custom-call | flops 400000000 | bytes 1048576 | tf_op jit(solution)/shard_map/rows_first/pallas_call | solution.py:224
  25.0 10.7 %all-to-all-start = ((f32[32,24,256]{2,1,0:T(8,128)}), f32[32,24,256]{2,1,0:T(8,128)S(1)}, u32[]{:S(2)}, u32[]{:S(2)}) async-start(f32[32,24,256]{2,1,0:T(8,128)} %get-tuple-element.44), calls=%async_computation | async-start | bytes 1572864 | tf_op jit(solution)/shard_map/all_to_all | solution.py:541
  37.3 2.9 %cols_first.1 = (f32[32,256]{1,0:T(8,128)S(1)}, f32[32,256]{1,0:T(8,128)S(1)}, f32[32,256]{1,0:T(8,128)S(1)}, f32[32,256]{1,0:T(8,128)S(1)}) custom-call(s32[1,1,32]{2,1,0:T(1,128)} %row_in.15, s32[1,1,32]{2,1,0:T(1,128)} %col_in.15, s32[1,1]{1,0:T(1,128)S(6)} %copy.8.tile_count, bf16[32,256,256]{2,1,0:T(8,128)(2,1)} %get-tuple-element.42.hi_in, ...), custom_call_target="tpu_custom_call" | custom-call | flops 400000000 | bytes 1048576 | tf_op jit(solution)/shard_map/cols_first/pallas_call | solution.py:278
  46.2 3.7 %all-to-all-done.refs_0_ = f32[32,24,256]{2,1,0:T(8,128)S(1)} async-done(((f32[32,24,256]{2,1,0:T(8,128)}), f32[32,24,256]{2,1,0:T(8,128)S(1)}, u32[]{:S(2)}, u32[]{:S(2)}) %all-to-all-start) | async-done | bytes 786464 | tf_op jit(solution)/shard_map/all_to_all | solution.py:541
  52.3 3.6 %all-to-all-start.3 = ((f32[16,24,256]{2,1,0:T(8,128)}), f32[16,24,256]{2,1,0:T(8,128)S(1)}, u32[]{:S(2)}, u32[]{:S(2)}) async-start(f32[16,24,256]{2,1,0:T(8,128)} %get-tuple-element.50), calls=%async_computation.3 | async-start | bytes 786432 | tf_op jit(solution)/shard_map/all_to_all | solution.py:541
  56.4 3.5 %collective-permute-start.8 = (f32[16,256]{1,0:T(8,128)S(1)}, f32[16,256]{1,0:T(8,128)S(1)}, u32[]{:S(2)}, u32[]{:S(2)}) collective-permute-start(f32[16,256]{1,0:T(8,128)S(1)} %get-tuple-element.49.own), channel_id=1, source_target_pairs={{0,64},{32,96},{64,0},{96,32},{1,65},{33,97},{65,1},{97,33},{2,66}... | collective-permute-start | bytes 49160 | tf_op jit(solution)/shard_map/ppermute | solution.py:533
  62.8 4.5 %rows_next.3 = f32[32,16,256]{2,1,0:T(8,128)} custom-call(s32[1,1,32]{2,1,0:T(1,128)} %row_in.15, s32[1,1,32]{2,1,0:T(1,128)} %col_in.15, s32[1,1]{1,0:T(1,128)S(6)} %copy.8.tile_count, bf16[32,256,256]{2,1,0:T(8,128)(2,1)} %get-tuple-element.42.hi_in, bf16[32,256,256]{2,1,0:T(8,128)(2,1)} %get-tuple-element.43.lo_in, f32[16,256]{1,0:T(8,128)S(1)} %get-tuple-element.49.own, ...), custom_call_target="tpu_custom_call" | custom-call | flops 400000000 | bytes 1048576 | tf_op jit(solution)/shard_map/rows_next/pallas_call | solution.py:253
  67.3 11.1 %all-to-all-start.2 = ((f32[32,16,256]{2,1,0:T(8,128)}), f32[32,16,256]{2,1,0:T(8,128)S(1)}, u32[]{:S(2)}, u32[]{:S(2)}) async-start(f32[32,16,256]{2,1,0:T(8,128)} %rows_next.3), calls=%async_computation.2 | async-start | bytes 1048576 | tf_op jit(solution)/shard_map/all_to_all | solution.py:541
  80.2 2.9 %cols_next.3 = (f32[24,256]{1,0:T(8,128)S(1)}, f32[24,256]{1,0:T(8,128)S(1)}, f32[24,256]{1,0:T(8,128)S(1)}, f32[24,256]{1,0:T(8,128)S(1)}) custom-call(s32[1,1,32]{2,1,0:T(1,128)} %row_in.15, s32[1,1,32]{2,1,0:T(1,128)} %col_in.15, s32[1,1]{1,0:T(1,128)S(6)} %copy.8.tile_count, bf16[32,256,256]{2,1,0:T(8,128)(2,1)} %get-tuple-element.42.hi_in, ...), custom_call_target="tpu_custom_call" | custom-call | flops 400000000 | bytes 1048576 | tf_op jit(solution)/shard_map/cols_next/pallas_call | solution.py:278
  85.9 4.0 %all-to-all-done.2.refs_0_ = f32[32,16,256]{2,1,0:T(8,128)S(1)} async-done(((f32[32,16,256]{2,1,0:T(8,128)}), f32[32,16,256]{2,1,0:T(8,128)S(1)}, u32[]{:S(2)}, u32[]{:S(2)}) %all-to-all-start.2) | async-done | bytes 524320 | tf_op jit(solution)/shard_map/all_to_all | solution.py:541
  91.8 5.7 %all-to-all-start.5 = ((f32[16,24,256]{2,1,0:T(8,128)}), f32[16,24,256]{2,1,0:T(8,128)S(1)}, u32[]{:S(2)}, u32[]{:S(2)}) async-start(f32[16,24,256]{2,1,0:T(8,128)} %get-tuple-element.58), calls=%async_computation.5 | async-start | bytes 786432 | tf_op jit(solution)/shard_map/all_to_all | solution.py:541
  103.8 4.5 %rows_next.4 = f32[32,16,256]{2,1,0:T(8,128)} custom-call(s32[1,1,32]{2,1,0:T(1,128)} %row_in.15, s32[1,1,32]{2,1,0:T(1,128)} %col_in.15, s32[1,1]{1,0:T(1,128)S(6)} %copy.8.tile_count, bf16[32,256,256]{2,1,0:T(8,128)(2,1)} %get-tuple-element.42.hi_in, bf16[32,256,256]{2,1,0:T(8,128)(2,1)} %get-tuple-element.43.lo_in, f32[16,256]{1,0:T(8,128)S(1)} %get-tuple-element.57.own, ...), custom_call_target="tpu_custom_call" | custom-call | flops 400000000 | bytes 1048576 | tf_op jit(solution)/shard_map/rows_next/pallas_call | solution.py:253
  108.3 11.9 %all-to-all-start.4 = ((f32[32,16,256]{2,1,0:T(8,128)}), f32[32,16,256]{2,1,0:T(8,128)S(1)}, u32[]{:S(2)}, u32[]{:S(2)}) async-start(f32[32,16,256]{2,1,0:T(8,128)} %rows_next.4), calls=%async_computation.4 | async-start | bytes 1048576 | tf_op jit(solution)/shard_map/all_to_all | solution.py:541
  122.1 2.9 %cols_next.4 = (f32[24,256]{1,0:T(8,128)S(1)}, f32[24,256]{1,0:T(8,128)S(1)}, f32[24,256]{1,0:T(8,128)S(1)}, f32[24,256]{1,0:T(8,128)S(1)}) custom-call(s32[1,1,32]{2,1,0:T(1,128)} %row_in.15, s32[1,1,32]{2,1,0:T(1,128)} %col_in.15, s32[1,1]{1,0:T(1,128)S(6)} %copy.8.tile_count, bf16[32,256,256]{2,1,0:T(8,128)(2,1)} %get-tuple-element.42.hi_in, ...), custom_call_target="tpu_custom_call" | custom-call | flops 400000000 | bytes 1048576 | tf_op jit(solution)/shard_map/cols_next/pallas_call | solution.py:278
  127.9 3.8 %all-to-all-done.4.refs_0_ = f32[32,16,256]{2,1,0:T(8,128)S(1)} async-done(((f32[32,16,256]{2,1,0:T(8,128)}), f32[32,16,256]{2,1,0:T(8,128)S(1)}, u32[]{:S(2)}, u32[]{:S(2)}) %all-to-all-start.4) | async-done | bytes 524320 | tf_op jit(solution)/shard_map/all_to_all | solution.py:541
  133.6 5.8 %all-to-all-start.7 = ((f32[16,24,256]{2,1,0:T(8,128)}), f32[16,24,256]{2,1,0:T(8,128)S(1)}, u32[]{:S(2)}, u32[]{:S(2)}) async-start(f32[16,24,256]{2,1,0:T(8,128)} %get-tuple-element.66), calls=%async_computation.7 | async-start | bytes 786432 | tf_op jit(solution)/shard_map/all_to_all | solution.py:541
  145.8 4.5 %rows_next.5 = f32[32,16,256]{2,1,0:T(8,128)} custom-call(s32[1,1,32]{2,1,0:T(1,128)} %row_in.15, s32[1,1,32]{2,1,0:T(1,128)} %col_in.15, s32[1,1]{1,0:T(1,128)S(6)} %copy.8.tile_count, bf16[32,256,256]{2,1,0:T(8,128)(2,1)} %get-tuple-element.42.hi_in, bf16[32,256,256]{2,1,0:T(8,128)(2,1)} %get-tuple-element.43.lo_in, f32[16,256]{1,0:T(8,128)S(1)} %get-tuple-element.65.own, ...), custom_call_target="tpu_custom_call" | custom-call | flops 400000000 | bytes 1048576 | tf_op jit(solution)/shard_map/rows_next/pallas_call | solution.py:253
  150.3 11.9 %all-to-all-start.6 = ((f32[32,16,256]{2,1,0:T(8,128)}), f32[32,16,256]{2,1,0:T(8,128)S(1)}, u32[]{:S(2)}, u32[]{:S(2)}) async-start(f32[32,16,256]{2,1,0:T(8,128)} %rows_next.5), calls=%async_computation.6 | async-start | bytes 1048576 | tf_op jit(solution)/shard_map/all_to_all | solution.py:541
  164.0 2.9 %cols_next.5 = (f32[24,256]{1,0:T(8,128)S(1)}, f32[24,256]{1,0:T(8,128)S(1)}, f32[24,256]{1,0:T(8,128)S(1)}, f32[24,256]{1,0:T(8,128)S(1)}) custom-call(s32[1,1,32]{2,1,0:T(1,128)} %row_in.15, s32[1,1,32]{2,1,0:T(1,128)} %col_in.15, s32[1,1]{1,0:T(1,128)S(6)} %copy.8.tile_count, bf16[32,256,256]{2,1,0:T(8,128)(2,1)} %get-tuple-element.42.hi_in, ...), custom_call_target="tpu_custom_call" | custom-call | flops 400000000 | bytes 1048576 | tf_op jit(solution)/shard_map/cols_next/pallas_call | solution.py:278
  169.6 4.0 %all-to-all-done.6.refs_0_ = f32[32,16,256]{2,1,0:T(8,128)S(1)} async-done(((f32[32,16,256]{2,1,0:T(8,128)}), f32[32,16,256]{2,1,0:T(8,128)S(1)}, u32[]{:S(2)}, u32[]{:S(2)}) %all-to-all-start.6) | async-done | bytes 524320 | tf_op jit(solution)/shard_map/all_to_all | solution.py:541
  175.1 9.5 %all_to_all.50.arrived = f32[8,8,256]{2,1,0:T(8,128)S(1)} all-to-all(f32[8,8,256]{2,1,0:T(8,128)S(1)} %get-tuple-element.72), channel_id=1, replica_groups=mesh['grp'=4,'col_0'=4,'col_1'=4,'col_2'=2] {'col_1','col_2'}, dimensions={0} | all-to-all | bytes 131072 | tf_op jit(solution)/shard_map/all_to_all | solution.py:541
  184.7 13.4 %all_to_all.51.arrived = f32[16,8,256]{2,1,0:T(8,128)S(1)} all-to-all(f32[16,8,256]{2,1,0:T(8,128)S(1)} %fold.1), channel_id=1, replica_groups=mesh['grp'=4,'col_0'=4,'col_1'=4,'col_2'=2] {'grp','col_0'}, dimensions={0} | all-to-all | bytes 262144 | tf_op jit(solution)/shard_map/all_to_all | solution.py:541
  (71 shorter events, 52.6 us)
Async XLA Ops:
  2.1 22.9 %all-to-all-start.1 = ((f32[16,16,256]{2,1,0:T(8,128)}), f32[16,16,256]{2,1,0:T(8,128)S(1)}, u32[]{:S(2)}, u32[]{:S(2)}) async-start(f32[16,16,256]{2,1,0:T(8,128)} %broadcast_in_dim.3), calls=%async_computation.1 | async-start | bytes 524288 | tf_op jit(solution)/shard_map/all_to_all | solution.py:541
  10.5 5.7 %collective-permute-start = (f32[16,256]{1,0:T(8,128)}, f32[16,256]{1,0:T(8,128)S(1)}, u32[]{:S(2)}, u32[]{:S(2)}) collective-permute-start(f32[16,256]{1,0:T(8,128)} %refs_5_.1), channel_id=1, source_target_pairs={{0,32},{32,64},{64,96},{96,0},{1,33},{33,65},{65,97},{97,1},{2,34}... | collective-permute-start | bytes 49160 | tf_op jit(solution)/shard_map/ppermute | solution.py:533
  11.9 4.4 %collective-permute-start.1 = (f32[16,256]{1,0:T(8,128)}, f32[16,256]{1,0:T(8,128)S(1)}, u32[]{:S(2)}, u32[]{:S(2)}) collective-permute-start(f32[16,256]{1,0:T(8,128)} %refs_5_.1), channel_id=1, source_target_pairs={{0,64},{32,96},{64,0},{96,32},{1,65},{33,97},{65,1},{97,33},{2,66}... | collective-permute-start | bytes 49160 | tf_op jit(solution)/shard_map/ppermute | solution.py:533
  25.0 25.0 %all-to-all-start = ((f32[32,24,256]{2,1,0:T(8,128)}), f32[32,24,256]{2,1,0:T(8,128)S(1)}, u32[]{:S(2)}, u32[]{:S(2)}) async-start(f32[32,24,256]{2,1,0:T(8,128)} %get-tuple-element.44), calls=%async_computation | async-start | bytes 1572864 | tf_op jit(solution)/shard_map/all_to_all | solution.py:541
  40.2 4.3 %collective-permute-start.4 = (f32[32,256]{1,0:T(8,128)S(1)}, f32[32,256]{1,0:T(8,128)S(1)}, u32[]{:S(2)}, u32[]{:S(2)}) collective-permute-start(f32[32,256]{1,0:T(8,128)S(1)} %get-tuple-element.46), channel_id=1, source_target_pairs={{0,32},{32,64},{64,96},{96,0},{1,33},{33,65},{65,97},{97,1},{2,34}... | collective-permute-start | bytes 98312 | tf_op jit(solution)/shard_map/ppermute | solution.py:533
  40.5 4.6 %collective-permute-start.5 = (f32[32,256]{1,0:T(8,128)S(1)}, f32[32,256]{1,0:T(8,128)S(1)}, u32[]{:S(2)}, u32[]{:S(2)}) collective-permute-start(f32[32,256]{1,0:T(8,128)S(1)} %get-tuple-element.47), channel_id=1, source_target_pairs={{0,64},{32,96},{64,0},{96,32},{1,65},{33,97},{65,1},{97,33},{2,66}... | collective-permute-start | bytes 98312 | tf_op jit(solution)/shard_map/ppermute | solution.py:533
  52.3 15.0 %all-to-all-start.3 = ((f32[16,24,256]{2,1,0:T(8,128)}), f32[16,24,256]{2,1,0:T(8,128)S(1)}, u32[]{:S(2)}, u32[]{:S(2)}) async-start(f32[16,24,256]{2,1,0:T(8,128)} %get-tuple-element.50), calls=%async_computation.3 | async-start | bytes 786432 | tf_op jit(solution)/shard_map/all_to_all | solution.py:541
  55.8 4.1 %collective-permute-start.7 = (f32[16,256]{1,0:T(8,128)S(1)}, f32[16,256]{1,0:T(8,128)S(1)}, u32[]{:S(2)}, u32[]{:S(2)}) collective-permute-start(f32[16,256]{1,0:T(8,128)S(1)} %get-tuple-element.49.own), channel_id=1, source_target_pairs={{0,32},{32,64},{64,96},{96,0},{1,33},{33,65},{65,97},{97,1},{2,34}... | collective-permute-start | bytes 49160 | tf_op jit(solution)/shard_map/ppermute | solution.py:533
  56.4 4.8 %collective-permute-start.8 = (f32[16,256]{1,0:T(8,128)S(1)}, f32[16,256]{1,0:T(8,128)S(1)}, u32[]{:S(2)}, u32[]{:S(2)}) collective-permute-start(f32[16,256]{1,0:T(8,128)S(1)} %get-tuple-element.49.own), channel_id=1, source_target_pairs={{0,64},{32,96},{64,0},{96,32},{1,65},{33,97},{65,1},{97,33},{2,66}... | collective-permute-start | bytes 49160 | tf_op jit(solution)/shard_map/ppermute | solution.py:533
  67.3 22.6 %all-to-all-start.2 = ((f32[32,16,256]{2,1,0:T(8,128)}), f32[32,16,256]{2,1,0:T(8,128)S(1)}, u32[]{:S(2)}, u32[]{:S(2)}) async-start(f32[32,16,256]{2,1,0:T(8,128)} %rows_next.3), calls=%async_computation.2 | async-start | bytes 1048576 | tf_op jit(solution)/shard_map/all_to_all | solution.py:541
  83.2 6.7 %collective-permute-start.11 = (f32[24,256]{1,0:T(8,128)S(1)}, f32[24,256]{1,0:T(8,128)S(1)}, u32[]{:S(2)}, u32[]{:S(2)}) collective-permute-start(f32[24,256]{1,0:T(8,128)S(1)} %get-tuple-element.52), channel_id=1, source_target_pairs={{0,32},{32,64},{64,96},{96,0},{1,33},{33,65},{65,97},{97,1},{2,34}... | collective-permute-start | bytes 73736 | tf_op jit(solution)/shard_map/ppermute | solution.py:533
  83.2 6.6 %collective-permute-start.12 = (f32[24,256]{1,0:T(8,128)S(1)}, f32[24,256]{1,0:T(8,128)S(1)}, u32[]{:S(2)}, u32[]{:S(2)}) collective-permute-start(f32[24,256]{1,0:T(8,128)S(1)} %get-tuple-element.53), channel_id=1, source_target_pairs={{0,64},{32,96},{64,0},{96,32},{1,65},{33,97},{65,1},{97,33},{2,66}... | collective-permute-start | bytes 73736 | tf_op jit(solution)/shard_map/ppermute | solution.py:533
  85.0 4.9 %collective-permute-start.13 = (f32[24,256]{1,0:T(8,128)S(1)}, f32[24,256]{1,0:T(8,128)S(1)}, u32[]{:S(2)}, u32[]{:S(2)}) collective-permute-start(f32[24,256]{1,0:T(8,128)S(1)} %get-tuple-element.54), channel_id=1, source_target_pairs={{0,96},{32,0},{64,32},{96,64},{1,97},{33,1},{65,33},{97,65},{2,98}... | collective-permute-start | bytes 73736 | tf_op jit(solution)/shard_map/ppermute | solution.py:533
  91.8 16.5 %all-to-all-start.5 = ((f32[16,24,256]{2,1,0:T(8,128)}), f32[16,24,256]{2,1,0:T(8,128)S(1)}, u32[]{:S(2)}, u32[]{:S(2)}) async-start(f32[16,24,256]{2,1,0:T(8,128)} %get-tuple-element.58), calls=%async_computation.5 | async-start | bytes 786432 | tf_op jit(solution)/shard_map/all_to_all | solution.py:541
  98.4 4.1 %collective-permute-start.15 = (f32[16,256]{1,0:T(8,128)S(1)}, f32[16,256]{1,0:T(8,128)S(1)}, u32[]{:S(2)}, u32[]{:S(2)}) collective-permute-start(f32[16,256]{1,0:T(8,128)S(1)} %get-tuple-element.57.own), channel_id=1, source_target_pairs={{0,64},{32,96},{64,0},{96,32},{1,65},{33,97},{65,1},{97,33},{2,66}... | collective-permute-start | bytes 49160 | tf_op jit(solution)/shard_map/ppermute | solution.py:533
  108.3 23.4 %all-to-all-start.4 = ((f32[32,16,256]{2,1,0:T(8,128)}), f32[32,16,256]{2,1,0:T(8,128)S(1)}, u32[]{:S(2)}, u32[]{:S(2)}) async-start(f32[32,16,256]{2,1,0:T(8,128)} %rows_next.4), calls=%async_computation.4 | async-start | bytes 1048576 | tf_op jit(solution)/shard_map/all_to_all | solution.py:541
  125.0 6.7 %collective-permute-start.18 = (f32[24,256]{1,0:T(8,128)S(1)}, f32[24,256]{1,0:T(8,128)S(1)}, u32[]{:S(2)}, u32[]{:S(2)}) collective-permute-start(f32[24,256]{1,0:T(8,128)S(1)} %get-tuple-element.60), channel_id=1, source_target_pairs={{0,32},{32,64},{64,96},{96,0},{1,33},{33,65},{65,97},{97,1},{2,34}... | collective-permute-start | bytes 73736 | tf_op jit(solution)/shard_map/ppermute | solution.py:533
  125.2 6.5 %collective-permute-start.19 = (f32[24,256]{1,0:T(8,128)S(1)}, f32[24,256]{1,0:T(8,128)S(1)}, u32[]{:S(2)}, u32[]{:S(2)}) collective-permute-start(f32[24,256]{1,0:T(8,128)S(1)} %get-tuple-element.61), channel_id=1, source_target_pairs={{0,64},{32,96},{64,0},{96,32},{1,65},{33,97},{65,1},{97,33},{2,66}... | collective-permute-start | bytes 73736 | tf_op jit(solution)/shard_map/ppermute | solution.py:533
  127.0 4.7 %collective-permute-start.20 = (f32[24,256]{1,0:T(8,128)S(1)}, f32[24,256]{1,0:T(8,128)S(1)}, u32[]{:S(2)}, u32[]{:S(2)}) collective-permute-start(f32[24,256]{1,0:T(8,128)S(1)} %get-tuple-element.62), channel_id=1, source_target_pairs={{0,96},{32,0},{64,32},{96,64},{1,97},{33,1},{65,33},{97,65},{2,98}... | collective-permute-start | bytes 73736 | tf_op jit(solution)/shard_map/ppermute | solution.py:533
  133.6 16.7 %all-to-all-start.7 = ((f32[16,24,256]{2,1,0:T(8,128)}), f32[16,24,256]{2,1,0:T(8,128)S(1)}, u32[]{:S(2)}, u32[]{:S(2)}) async-start(f32[16,24,256]{2,1,0:T(8,128)} %get-tuple-element.66), calls=%async_computation.7 | async-start | bytes 786432 | tf_op jit(solution)/shard_map/all_to_all | solution.py:541
  150.3 23.4 %all-to-all-start.6 = ((f32[32,16,256]{2,1,0:T(8,128)}), f32[32,16,256]{2,1,0:T(8,128)S(1)}, u32[]{:S(2)}, u32[]{:S(2)}) async-start(f32[32,16,256]{2,1,0:T(8,128)} %rows_next.5), calls=%async_computation.6 | async-start | bytes 1048576 | tf_op jit(solution)/shard_map/all_to_all | solution.py:541
  166.9 6.7 %collective-permute-start.25 = (f32[24,256]{1,0:T(8,128)S(1)}, f32[24,256]{1,0:T(8,128)S(1)}, u32[]{:S(2)}, u32[]{:S(2)}) collective-permute-start(f32[24,256]{1,0:T(8,128)S(1)} %get-tuple-element.68), channel_id=1, source_target_pairs={{0,32},{32,64},{64,96},{96,0},{1,33},{33,65},{65,97},{97,1},{2,34}... | collective-permute-start | bytes 73736 | tf_op jit(solution)/shard_map/ppermute | solution.py:533
  167.0 6.6 %collective-permute-start.26 = (f32[24,256]{1,0:T(8,128)S(1)}, f32[24,256]{1,0:T(8,128)S(1)}, u32[]{:S(2)}, u32[]{:S(2)}) collective-permute-start(f32[24,256]{1,0:T(8,128)S(1)} %get-tuple-element.69), channel_id=1, source_target_pairs={{0,64},{32,96},{64,0},{96,32},{1,65},{33,97},{65,1},{97,33},{2,66}... | collective-permute-start | bytes 73736 | tf_op jit(solution)/shard_map/ppermute | solution.py:533
  168.7 4.9 %collective-permute-start.27 = (f32[24,256]{1,0:T(8,128)S(1)}, f32[24,256]{1,0:T(8,128)S(1)}, u32[]{:S(2)}, u32[]{:S(2)}) collective-permute-start(f32[24,256]{1,0:T(8,128)S(1)} %get-tuple-element.70), channel_id=1, source_target_pairs={{0,96},{32,0},{64,32},{96,64},{1,97},{33,1},{65,33},{97,65},{2,98}... | collective-permute-start | bytes 73736 | tf_op jit(solution)/shard_map/ppermute | solution.py:533
  (15 other events, 37.2 us)

commit v5 on v4

--- a/solution.py
+++ b/solution.py
@@ -12,7 +12,9 @@
 CORE = "col_2"
 COL = ("col_0", "col_1", "col_2")
 GRP_COL = ("grp", "col_0", "col_1", "col_2")
+HELD = 4
 ROW_GROUP = 8
+LATER_ROW_GROUP = 7
 COL_GROUP = 4
 FACTOR_GROUP = 8
 highest = lax.Precision.HIGHEST
@@ -51,7 +53,24 @@
     out = top[0:16] + top[16:32] + low[0:16]
     if first:
         out = jnp.concatenate([out, top[32:40] + low[16:24]], axis=0)
-    return out * live
+    return jnp.where(live, out, 0.0)
+
+
+def to_tiles(block):
+    halves = [block[8 * r : 8 * r + 8, 128 * c : 128 * c + 128] for r in (0, 1) for c in (0, 1)]
+    return jnp.stack(halves)
+
+
+def from_tiles(tiles):
+    rows = [jnp.concatenate([tiles[2 * r], tiles[2 * r + 1]], axis=1) for r in (0, 1)]
+    return jnp.concatenate(rows, axis=0)
+
+
+def with_degree(result):
+    sums = result[16:24]
+    row = lax.broadcasted_iota(jnp.int32, (8, 128), 0)
+    tile = jnp.where(row == 0, sums[:, 0:128], sums[:, 128:256])
+    return jnp.concatenate([to_tiles(result[0:16]), tile[None]], axis=0)
 
 
 def stacked_lhs(piece, first):
@@ -67,41 +86,49 @@
         lhs_hi[k], lhs_lo[k] = stacked_lhs(piece[...], first)
 
 
-def group_rows(base, place, lhs_hi, lhs_lo, hi, lo, out, first):
+def group_rows(base, size, origin, place, lhs_hi, lhs_lo, hi, lo, out, first):
     tile_row, tile_col, tile_count = place
     results = []
-    for u in range(ROW_GROUP):
+    for u in range(size):
         s = base + u
         k = ((tile_row[0, 0, 0] >> 5) - (tile_col[0, 0, s] >> 5)) & 3
-        live = (s < tile_count[0, 0]).astype(f32)
+        live = s < tile_count[0, 0]
         results.append(
-            products(lhs_hi[k], lhs_lo[k], hi[s], lo[s], ((1,), (1,)), first, live)
+            products(
+                lhs_hi[k], lhs_lo[k], hi[s - origin], lo[s - origin], ((1,), (1,)), first, live
+            )
         )
-    for u in range(ROW_GROUP):
-        out[tile_row[0, 0, base + u] & 31] += results[u]
+    for u in range(size):
+        out[tile_row[0, 0, base + u] & 31] += with_degree(results[u]) if first else results[u]
 
 
 def groups_of(tile_count, group):
     return (tile_count[0, 0] + (group - 1)) // group
 
 
-def group_copies(q, group, source_hi, source_lo, hi, lo, sems):
-    part = pl.ds(q * group, group)
+def later_groups_of(tile_count, group):
+    return (tile_count[0, 0] - HELD + (group - 1)) // group
+
+
+def part_copies(part, at, source_hi, source_lo, hi, lo, sems):
     return (
-        pltpu.make_async_copy(source_hi.at[part], hi.at[part], sems.at[0, q]),
-        pltpu.make_async_copy(source_lo.at[part], lo.at[part], sems.at[1, q]),
+        pltpu.make_async_copy(source_hi.at[part], hi.at[part], sems.at[0, at]),
+        pltpu.make_async_copy(source_lo.at[part], lo.at[part], sems.at[1, at]),
     )
 
 
-def start_groups(tile_count, group, index_copies, *refs):
-    for copy in group_copies(0, group, *refs):
-        copy.start()
-    for copy in index_copies:
-        copy.start()
-
-    @pl.loop(1, groups_of(tile_count, group))
+def group_copies(q, group, *refs):
+    return part_copies(pl.ds(q * group, group), q, *refs)
+
+
+def later_copies(q, group, *refs):
+    return part_copies(pl.ds(HELD + q * group, group), q, *refs)
+
+
+def start_later(tile_count, group, *refs):
+    @pl.loop(0, later_groups_of(tile_count, group))
     def _(q):
-        for copy in group_copies(q, group, *refs):
+        for copy in later_copies(q, group, *refs):
             copy.start()
 
 
@@ -113,7 +140,7 @@
 
 
 def rows_first_kernel(
-    row_in, col_in, tile_count, tiles, own, one, two, three, out, hi_out, lo_out,
+    row_in, col_in, tile_count, tiles, own, one, two, three, out, hi_held, lo_held, hi_out, lo_out,
     buf, hi, lo, lhs_hi, lhs_lo, tile_row, tile_col, sems, out_sems, index_sems
 ):
     group = ROW_GROUP
@@ -146,8 +173,11 @@
         for copy in group_copies(q, group, hi, lo, hi_out, lo_out, out_sems):
             copy.start()
         group_rows(
-            q * group, (tile_row, tile_col, tile_count), lhs_hi, lhs_lo, hi, lo, out, True
+            q * group, group, 0, (tile_row, tile_col, tile_count), lhs_hi, lhs_lo, hi, lo, out, True
         )
+
+    hi_held[...] = hi[0:HELD]
+    lo_held[...] = lo[0:HELD]
 
     @pl.loop(0, count)
     def _(q):
@@ -156,32 +186,62 @@
 
 
 def rows_next_kernel(
-    row_in, col_in, tile_count, hi_in, lo_in, own, one, two, three, out,
+    row_in, col_in, tile_count, hi_held, lo_held, hi_in, lo_in, own, one, two, three, out,
     hi, lo, lhs_hi, lhs_lo, tile_row, tile_col, sems, index_sems
 ):
-    group = ROW_GROUP
+    group = LATER_ROW_GROUP
+    place = (tile_row, tile_col, tile_count)
     index_copies = index_fetch(row_in, col_in, tile_row, tile_col, index_sems)
-    start_groups(tile_count, group, index_copies, hi_in, lo_in, hi, lo, sems)
+    for copy in index_copies:
+        copy.start()
+    start_later(tile_count, group, hi_in, lo_in, hi, lo, sems)
     fill_pieces((own, one, two, three), lhs_hi, lhs_lo, False)
     out[...] = jnp.zeros_like(out)
     for copy in index_copies:
         copy.wait()
-
-    @pl.loop(0, groups_of(tile_count, group))
+    group_rows(0, HELD, 0, place, lhs_hi, lhs_lo, hi_held, lo_held, out, False)
+
+    @pl.loop(0, later_groups_of(tile_count, group))
     def _(q):
-        for copy in group_copies(q, group, hi_in, lo_in, hi, lo, sems):
+        for copy in later_copies(q, group, hi_in, lo_in, hi, lo, sems):
             copy.wait()
-        group_rows(q * group, (tile_row, tile_col, tile_count), lhs_hi, lhs_lo, hi, lo, out, False)
+        group_rows(HELD + q * group, group, 0, place, lhs_hi, lhs_lo, hi, lo, out, False)
+
+
+def group_cols(base, size, place, near, far, hi, lo, acc, first):
+    tile_row, tile_col, tile_count = place
+    results, slots = [], []
+    for u in range(size):
+        s = base + u
+        row = tile_row[0, 0, s] & 31
+        at = row >> 1
+        same = ((row ^ tile_col[0, 0, 0]) & 1) == 0
+        if first:
+            piece = jnp.where(same, near[at], far[at])
+        else:
+            piece = from_tiles(jnp.where(same, near[at, 0:4], far[at, 0:4]))
+        left_hi, left_lo = stacked_lhs(piece, first)
+        live = s < tile_count[0, 0]
+        results.append(products(left_hi, left_lo, hi[s], lo[s], ((1,), (0,)), first, live))
+        slots.append(((tile_col[0, 0, s] >> 5) - (tile_row[0, 0, 0] >> 5)) & 3)
+    for u in range(size):
+        acc[slots[u]] += results[u]
 
 
 def cols_kernel(
-    first, row_in, col_in, tile_count, hi_in, lo_in, near, far, own, one, two, three,
-    hi, lo, acc, tile_row, tile_col, sems, index_sems
+    first, row_in, col_in, tile_count, hi_held, lo_held, hi_in, lo_in, near, far,
+    own, one, two, three, hi, lo, acc, tile_row, tile_col, sems, index_sems
 ):
     group = COL_GROUP
+    place = (tile_row, tile_col, tile_count)
     index_copies = index_fetch(row_in, col_in, tile_row, tile_col, index_sems)
-    start_groups(tile_count, group, index_copies, hi_in, lo_in, hi, lo, sems)
+    for copy in index_copies:
+        copy.start()
+    start_later(tile_count, group, hi_in, lo_in, hi, lo, sems)
     acc[...] = jnp.zeros_like(acc)
+    for copy in index_copies:
+        copy.wait()
+    group_cols(0, HELD, place, near, far, hi_held, lo_held, acc, first)
     if first:
         total = jnp.zeros((16, 16), f32)
         for part in (near, far):
@@ -189,31 +249,16 @@
                 total = total + dot_f32(part[p], part[p], ((1,), (1,)))
         gram = pack_gram(total)
     else:
-        gram = jnp.zeros_like(near[0, 16:24])
+        gram = jnp.zeros_like(near[0, 4])
         for p in range(near.shape[0]):
-            gram = gram + (near[p, 16:24] + far[p, 16:24])
-    for copy in index_copies:
-        copy.wait()
-
-    @pl.loop(0, groups_of(tile_count, group))
+            gram = gram + (near[p, 4] + far[p, 4])
+    gram = jnp.concatenate([gram, jnp.zeros((8, 128), f32)], axis=1)
+
+    @pl.loop(0, later_groups_of(tile_count, group))
     def _(q):
-        for copy in group_copies(q, group, hi_in, lo_in, hi, lo, sems):
+        for copy in later_copies(q, group, hi_in, lo_in, hi, lo, sems):
             copy.wait()
-        results, slots = [], []
-        for u in range(group):
-            s = q * group + u
-            row = tile_row[0, 0, s] & 31
-            place = row >> 1
-            same = ((row ^ tile_col[0, 0, 0]) & 1) == 0
-            piece = jnp.where(same, near[place, 0:16], far[place, 0:16])
-            left_hi, left_lo = stacked_lhs(piece, first)
-            live = (s < tile_count[0, 0]).astype(f32)
-            results.append(
-                products(left_hi, left_lo, hi[s], lo[s], ((1,), (0,)), first, live)
-            )
-            slots.append(((tile_col[0, 0, s] >> 5) - (tile_row[0, 0, 0] >> 5)) & 3)
-        for u in range(group):
-            acc[slots[u]] += results[u]
+        group_cols(HELD + q * group, group, place, near, far, hi, lo, acc, first)
 
     for k, out in enumerate((own, one, two, three)):
         out[...] = jnp.concatenate([acc[k], gram], axis=0)
@@ -225,12 +270,14 @@
         rows_first_kernel,
         name="rows_first",
         out_shape=(
-            jax.ShapeDtypeStruct((32, 24, size), f32),
+            jax.ShapeDtypeStruct((32, 5, 8, 128), f32),
+            pltpu.VMEM((HELD, size, size), bf16),
+            pltpu.VMEM((HELD, size, size), bf16),
             pltpu.MemorySpace.HBM((slots, size, size), bf16),
             pltpu.MemorySpace.HBM((slots, size, size), bf16),
         ),
         in_specs=[HBM, HBM, SMEM] + [HBM] + [VMEM] * 4,
-        out_specs=(VMEM, HBM, HBM),
+        out_specs=(VMEM, VMEM, VMEM, HBM, HBM),
         scratch_shapes=[
             pltpu.VMEM((slots, size, size), f32),
             pltpu.VMEM((slots, size, size), bf16),
@@ -248,13 +295,13 @@
     )(*place, tiles, *pieces)
 
 
-def rows_next(place, hi, lo, pieces):
-    slots, size = hi.shape[0], hi.shape[1]
+def rows_next(place, parts, pieces):
+    slots, size = parts[2].shape[0], parts[2].shape[1]
     return pl.pallas_call(
         rows_next_kernel,
         name="rows_next",
         out_shape=jax.ShapeDtypeStruct((32, 16, size), f32),
-        in_specs=[HBM, HBM, SMEM] + [HBM] * 2 + [VMEM] * 4,
+        in_specs=[VMEM, VMEM, SMEM] + [VMEM] * 2 + [HBM] * 2 + [VMEM] * 4,
         out_specs=VMEM,
         scratch_shapes=[
             pltpu.VMEM((slots, size, size), bf16),
@@ -263,23 +310,23 @@
             pltpu.VMEM((4, 16, size), bf16),
             pltpu.SMEM((1, 1, slots), jnp.int32),
             pltpu.SMEM((1, 1, slots), jnp.int32),
-            pltpu.SemaphoreType.DMA((2, slots // ROW_GROUP)),
+            pltpu.SemaphoreType.DMA((2, (slots - HELD) // LATER_ROW_GROUP)),
             pltpu.SemaphoreType.DMA((2,)),
         ],
         compiler_params=limits(20),
         cost_estimate=cost(400_000_000),
-    )(*place, hi, lo, *pieces)
-
-
-def cols_product(first, place, hi, lo, near, far):
+    )(*place, *parts, *pieces)
+
+
+def cols_product(first, place, parts, near, far):
     height = 24 if first else 16
-    slots, size = hi.shape[0], hi.shape[1]
+    slots, size = parts[2].shape[0], parts[2].shape[1]
     out = jax.ShapeDtypeStruct((height + 8, size), f32)
     return pl.pallas_call(
         functools.partial(cols_kernel, first),
         name="cols_first" if first else "cols_next",
         out_shape=(out,) * 4,
-        in_specs=[HBM, HBM, SMEM] + [HBM] * 2 + [VMEM] * 2,
+        in_specs=[VMEM, VMEM, SMEM] + [VMEM] * 2 + [HBM] * 2 + [VMEM] * 2,
         out_specs=(VMEM,) * 4,
         scratch_shapes=[
             pltpu.VMEM((slots, size, size), bf16),
@@ -287,22 +334,21 @@
             pltpu.VMEM((4, height, size), f32),
             pltpu.SMEM((1, 1, slots), jnp.int32),
             pltpu.SMEM((1, 1, slots), jnp.int32),
-            pltpu.SemaphoreType.DMA((2, slots // COL_GROUP)),
+            pltpu.SemaphoreType.DMA((2, (slots - HELD) // COL_GROUP)),
             pltpu.SemaphoreType.DMA((2,)),
         ],
         compiler_params=limits(20),
         cost_estimate=cost(400_000_000),
-    )(*place, hi, lo, near, far)
-
-
-def unpack_gram(packed):
-    return jnp.concatenate([packed[:, 0:128], packed[:, 128:256]], axis=0)
-
-
-def pack_gram(gram):
-    width = gram.shape[1]
-    if width < 128:
-        gram = jnp.concatenate([gram, jnp.zeros((16, 128 - width), f32)], axis=1)
+    )(*place, *parts, near, far)
+
+
+def unpack_gram(packed, width):
+    return jnp.concatenate([packed[:, 0:width], packed[:, width : 2 * width]], axis=0)
+
+
+def pack_gram(gram, width=64):
+    if gram.shape[1] < width:
+        gram = jnp.concatenate([gram, jnp.zeros((16, width - gram.shape[1]), f32)], axis=1)
     return jnp.concatenate([gram[0:8], gram[8:16]], axis=1)
 
 
@@ -367,19 +413,22 @@
     (start,) = take(1) if step == 0 else (None,)
     outs = refs
     side = own[...] + one[...] + two[...] + three[...]
-    height = arrived.shape[1]
-    total = side[0:height]
-    for p in range(arrived.shape[0]):
+    height = side.shape[0] - 8
+    total = arrived[0]
+    for p in range(1, arrived.shape[0]):
         total = total + arrived[p]
-    gram = unpack_gram(side[height : height + 8]) * (1.0 / node_total)
+    gram = unpack_gram(side[height : height + 8], 64) * (1.0 / node_total)
+    if step == 0:
+        level = side[16:17] + jnp.concatenate([total[4, 0:1], total[4, 1:2]], axis=1)
+        total = from_tiles(total[0:4])
+    total = total + side[0:16]
     if step == 0:
         packed, piece_out, state, degree_out, lower_out = outs
-        level = total[16:17]
         lower, inverse = factor_and_inverse(gram[:, 0:16])
         block = start[...]
         applied = level * block - total[0:16]
         both = dot_f32(inverse, jnp.concatenate([block, applied], axis=1), ((1,), (0,)))
-        degree_out[...] = total[16:24]
+        degree_out[...] = jnp.broadcast_to(level, degree_out.shape)
         stack = both
         new_vectors = both[:, 0:256]
         new_applied = both[:, 256:512]
@@ -426,20 +475,20 @@
         basis = jnp.concatenate([stack[:, 0:256], both[:, 0:256]], axis=0)
     partial = dot_f32(new_applied, jnp.concatenate([basis, new_applied], axis=0), ((1,), (1,)))
     piece_out[...] = new_applied
-    gram_rows = pack_gram(partial)
     if step == ITERS - 1:
-        for p in range(packed.shape[0]):
-            packed[p] = gram_rows
-    else:
-        message = jnp.concatenate([new_applied, gram_rows], axis=0)
+        message = pack_gram(partial, 128)
         for p in range(packed.shape[0]):
             packed[p] = message
+    else:
+        message = jnp.concatenate([to_tiles(new_applied), pack_gram(partial)[None]], axis=0)
+        for p in range(packed.shape[0]):
+            packed[p] = message
 
 
 def update(step, node_total, arrived, sides, state, degree, shift, start):
-    size = arrived.shape[2]
+    size = sides[0].shape[1]
     shapes = [
-        jax.ShapeDtypeStruct((8, 8, size) if step == ITERS - 1 else (16, 24, size), f32),
+        jax.ShapeDtypeStruct((8, 8, size) if step == ITERS - 1 else (16, 5, 8, 128), f32),
         jax.ShapeDtypeStruct((16, size), f32),
         jax.ShapeDtypeStruct((16 * (step + 1), 2 * size), f32),
     ]
@@ -489,7 +538,7 @@
     packed = arrived[0]
     for p in range(1, arrived.shape[0]):
         packed = packed + arrived[p]
-    gram = unpack_gram(packed) * (1.0 / node_total)
+    gram = unpack_gram(packed, 128) * (1.0 / node_total)
     width = 16 * ITERS
     coeffs = gram[:, 0:width]
     square = gram[:, width : width + 16] - dot_f32(coeffs, coeffs, ((1,), (1,)))
@@ -528,6 +577,26 @@
     )(*args)
 
 
+def first_message_kernel(block, packed, piece):
+    piece[...] = block[...]
+    for p in range(packed.shape[0]):
+        packed[p] = block[...]
+
+
+def first_message(block):
+    return pl.pallas_call(
+        first_message_kernel,
+        name="first_message",
+        out_shape=(
+            jax.ShapeDtypeStruct((16, *block.shape), f32),
+            pltpu.VMEM(block.shape, f32),
+        ),
+        in_specs=[VMEM],
+        out_specs=(VMEM, VMEM),
+        compiler_params=limits(4),
+    )(block)
+
+
 def shifted(value, hop):
     size = lax.axis_size("grp")
     return lax.ppermute(value, "grp", [(i, (i + hop) % size) for i in range(size)])
@@ -544,34 +613,43 @@
 def body(start_block, tile_values, tile_row, tile_col, tile_count):
     grp_size = lax.axis_size("grp")
     node_total = float(start_block.shape[1] * grp_size * lax.axis_size(COL))
-    message = jnp.broadcast_to(start_block, (lax.axis_size(ZX), *start_block.shape))
-    place = tuple(
-        pltpu.with_memory_space_constraint(part, pltpu.MemorySpace.HBM)
-        for part in (tile_row, tile_col)
-    )
-    place = (*place, tile_count)
-    start_block = pltpu.with_memory_space_constraint(start_block, pltpu.MemorySpace.HBM)
+    HBM_SPACE = pltpu.MemorySpace.HBM
+
+    def placed_in(space):
+        index = [pltpu.with_memory_space_constraint(part, space) for part in (tile_row, tile_col)]
+        return (*index, tile_count)
+
+    first_place, place = placed_in(HBM_SPACE), placed_in(pltpu.VMEM)
+    raw_block = start_block
+    start_block = pltpu.with_memory_space_constraint(start_block, HBM_SPACE)
     tile_values = pltpu.with_memory_space_constraint(tile_values, pltpu.MemorySpace.HBM)
-    piece = start_block
-    state = degree = shift = hi = lo = None
+    message, piece = first_message(start_block)
+    origin = piece
+    state = degree = shift = parts = None
     lowers, coeffs = [], []
     for step in range(ITERS):
         first = step == 0
         pieces = [piece]
         for hop in range(1, grp_size):
-            pieces.append(shifted(piece, hop))
+            pieces.append(shifted(raw_block if first else piece, hop))
         near = exchanged(message, ZX)
         if first:
-            rows, hi, lo = rows_first(place, tile_values, pieces)
-            hi = pltpu.with_memory_space_constraint(hi, pltpu.MemorySpace.HBM)
-            lo = pltpu.with_memory_space_constraint(lo, pltpu.MemorySpace.HBM)
+            rows, *parts = rows_first(first_place, tile_values, pieces)
+            parts = [
+                pltpu.with_memory_space_constraint(part, space)
+                for part, space in zip(
+                    parts, (pltpu.VMEM,) * 2 + (pltpu.MemorySpace.HBM,) * 2, strict=True
+                )
+            ]
         else:
-            rows = rows_next(place, hi, lo, pieces)
+            rows = rows_next(place, parts, pieces)
         far = swapped(near)
         arrived = exchanged(rows, COL)
-        sides = cols_product(first, place, hi, lo, near, far)
-        sides = [sides[0]] + [shifted(sides[hop], hop) for hop in range(1, grp_size)]
-        outs = update(step, node_total, arrived, sides, state, degree, shift, start_block)
+        cols = cols_product(first, place, parts, near, far)
+        sides = [cols[0]]
+        for hop in range(1, grp_size):
+            sides.append(shifted(cols[hop], hop))
+        outs = update(step, node_total, arrived, sides, state, degree, shift, origin)
         message, piece, state = outs[0:3]
         if first:
             degree = outs[3]

time: 202 us -> 199 us (0.985)
  local copies, waits for them, and re-layouts: 2.05 us -> 0.01 us
    ppermute x24, starting transfers between devices: 27.8 us -> 30.6 us  [shifted(): lax.ppermute(value, 'grp', [(i, (i + hop) % size) for i in range(size)])]
    ppermute x24, waiting for transfers between devices: 12.6 us -> 15.2 us  [shifted(): lax.ppermute(value, 'grp', [(i, (i + hop) % size) for i in range(size)])]
    all_to_all x8, starting transfers between devices: 69.1 us -> 66.7 us  [exchanged(): return lax.all_to_all(value, axes, split_axis=0, concat_axis=0, tiled=True)]
  transfers between devices with their start and end apart: 36 -> 36, of which waited for: 20 -> 18; matrix products, arithmetic and copies ran while one was open for 0% -> 0% of each run, Pallas kernels for 16% -> 15%
where the time goes in v5:
time: 199 us; the launch traced here: 197 us
  starting transfers between devices  98.7 us (50%)
  Pallas kernels  39.4 us (20%)
  waiting for transfers between devices  34.3 us (17%)
  blocking collectives  23.3 us (12%)
    all_to_all x8, starting transfers between devices, exchanged(): return lax.all_to_all(value, axes, split_axis=0, concat_axis=0, tiled=True)  66.7 us
    ppermute x24, starting transfers between devices, shifted(): lax.ppermute(value, 'grp', [(i, (i + hop) % size) for i in range(size)])  30.6 us
    all_to_all x2, blocking collectives, exchanged(): return lax.all_to_all(value, axes, split_axis=0, concat_axis=0, tiled=True)  23.3 us
    ppermute x24, waiting for transfers between devices, shifted(): lax.ppermute(value, 'grp', [(i, (i + hop) % size) for i in range(size)])  15.2 us
    all_to_all x8, waiting for transfers between devices, exchanged(): return lax.all_to_all(value, axes, split_axis=0, concat_axis=0, tiled=True)  13.6 us
    pallas_call x3, Pallas kernels, rows_next(): pl.pallas_call(rows_next_kernel, name='rows_next', out_shape=jax.ShapeDty...  12.6 us
    pallas_call x4, Pallas kernels, cols_product(): pl.pallas_call(functools.partial(cols_kernel, first), name='cols_first' i...  10.6 us
    pallas_call x4, Pallas kernels, update(): pl.pallas_call(functools.partial(update_kernel, step, node_total), out_sh...  7.2 us
  transfers between devices with their start and end apart: 36, of which 18 were waited for; matrix products, arithmetic and copies ran while one was open for 0% of the time, Pallas kernels for 15%

profile of v5, /device:TPU:1, one launch (start us, length us, event | category | flops | bytes accessed | tf_op | source)
XLA Modules:
  0.0 197.3 jit_solution(8670506330980374214)
XLA Ops:
  2.1 8.4 %all-to-all-start.1 = ((f32[16,16,256]{2,1,0:T(8,128)}), f32[16,16,256]{2,1,0:T(8,128)S(1)}, u32[]{:S(2)}, u32[]{:S(2)}) async-start(f32[16,16,256]{2,1,0:T(8,128)} %get-tuple-element.52), calls=%async_computation.1 | async-start | bytes 524288 | tf_op jit(solution)/shard_map/all_to_all | solution.py:610
  18.0 6.0 %rows_first.1 = (f32[32,5,8,128]{3,2,1,0:T(8,128)}, bf16[4,256,256]{2,1,0:T(8,128)(2,1)S(1)}, bf16[4,256,256]{2,1,0:T(8,128)(2,1)S(1)}, bf16[32,256,256]{2,1,0:T(8,128)(2,1)}, bf16[32,256,256]{2,1,0:T(8,128)(2,1)}) custom-call(s32[1,1,32]{2,1,0:T(1,128)} %row_in.15, s32[1,1,32]{2,1,0:T(1,128)} %col_in.15, s32[1,1]{1,0:T(1,128)S(6)} %copy.8.tile_count, ...), custom_call_target="tpu_custom_call" | custom-call | flops 400000000 | bytes 1048576 | tf_op jit(solution)/shard_map/rows_first/pallas_call | solution.py:269
  24.0 10.6 %all-to-all-start = ((f32[32,5,8,128]{3,2,1,0:T(8,128)}), f32[32,5,8,128]{3,2,1,0:T(8,128)S(1)}, u32[]{:S(2)}, u32[]{:S(2)}) async-start(f32[32,5,8,128]{3,2,1,0:T(8,128)} %get-tuple-element.51), calls=%async_computation | async-start | bytes 1310720 | tf_op jit(solution)/shard_map/all_to_all | solution.py:610
  44.4 3.0 %all-to-all-done.refs_0_ = f32[32,5,8,128]{3,2,1,0:T(8,128)S(1)} async-done(((f32[32,5,8,128]{3,2,1,0:T(8,128)}), f32[32,5,8,128]{3,2,1,0:T(8,128)S(1)}, u32[]{:S(2)}, u32[]{:S(2)}) %all-to-all-start) | async-done | bytes 655392 | tf_op jit(solution)/shard_map/all_to_all | solution.py:610
  49.1 4.3 %all-to-all-start.3 = ((f32[16,5,8,128]{3,2,1,0:T(8,128)}), f32[16,5,8,128]{3,2,1,0:T(8,128)S(1)}, u32[]{:S(2)}, u32[]{:S(2)}) async-start(f32[16,5,8,128]{3,2,1,0:T(8,128)} %get-tuple-element.58), calls=%async_computation.3 | async-start | bytes 655360 | tf_op jit(solution)/shard_map/all_to_all | solution.py:610
  53.3 3.6 %collective-permute-start.9 = (f32[16,256]{1,0:T(8,128)S(1)}, f32[16,256]{1,0:T(8,128)S(1)}, u32[]{:S(2)}, u32[]{:S(2)}) collective-permute-start(f32[16,256]{1,0:T(8,128)S(1)} %get-tuple-element.57.own), channel_id=1, source_target_pairs={{0,96},{32,0},{64,32},{96,64},{1,97},{33,1},{65,33},{97,65},{2,98}... | collective-permute-start | bytes 49160 | tf_op jit(solution)/shard_map/ppermute | solution.py:602
  57.8 3.5 %collective-permute-done.8.two = f32[16,256]{1,0:T(8,128)S(1)} collective-permute-done((f32[16,256]{1,0:T(8,128)S(1)}, f32[16,256]{1,0:T(8,128)S(1)}, u32[]{:S(2)}, u32[]{:S(2)}) %collective-permute-start.8) | collective-permute-done | bytes 16416 | tf_op jit(solution)/shard_map/ppermute | solution.py:602
  61.4 4.2 %rows_next.3 = f32[32,16,256]{2,1,0:T(8,128)} custom-call(s32[1,1,32]{2,1,0:T(1,128)S(1)} %copy-done, s32[1,1,32]{2,1,0:T(1,128)S(1)} %copy-done.1, s32[1,1]{1,0:T(1,128)S(6)} %copy.8.tile_count, bf16[4,256,256]{2,1,0:T(8,128)(2,1)S(1)} %get-tuple-element.47.hi_held, bf16[4,256,256]{2,1,0:T(8,128)(2,1)S(1)} %get-tuple-element.48.lo_held, ...), custom_call_target="tpu_custom_call" | custom-call | flops 400000000 | bytes 1048576 | tf_op jit(solution)/shard_map/rows_next/pallas_call | solution.py:300
  65.6 10.3 %all-to-all-start.2 = ((f32[32,16,256]{2,1,0:T(8,128)}), f32[32,16,256]{2,1,0:T(8,128)S(1)}, u32[]{:S(2)}, u32[]{:S(2)}) async-start(f32[32,16,256]{2,1,0:T(8,128)} %rows_next.3), calls=%async_computation.2 | async-start | bytes 1048576 | tf_op jit(solution)/shard_map/all_to_all | solution.py:610
  83.7 3.6 %all-to-all-done.2.refs_0_ = f32[32,16,256]{2,1,0:T(8,128)S(1)} async-done(((f32[32,16,256]{2,1,0:T(8,128)}), f32[32,16,256]{2,1,0:T(8,128)S(1)}, u32[]{:S(2)}, u32[]{:S(2)}) %all-to-all-start.2) | async-done | bytes 524320 | tf_op jit(solution)/shard_map/all_to_all | solution.py:610
  89.3 5.6 %all-to-all-start.5 = ((f32[16,5,8,128]{3,2,1,0:T(8,128)}), f32[16,5,8,128]{3,2,1,0:T(8,128)S(1)}, u32[]{:S(2)}, u32[]{:S(2)}) async-start(f32[16,5,8,128]{3,2,1,0:T(8,128)} %get-tuple-element.66), calls=%async_computation.5 | async-start | bytes 655360 | tf_op jit(solution)/shard_map/all_to_all | solution.py:610
  94.9 3.3 %collective-permute-start.16 = (f32[16,256]{1,0:T(8,128)S(1)}, f32[16,256]{1,0:T(8,128)S(1)}, u32[]{:S(2)}, u32[]{:S(2)}) collective-permute-start(f32[16,256]{1,0:T(8,128)S(1)} %get-tuple-element.65.own), channel_id=1, source_target_pairs={{0,96},{32,0},{64,32},{96,64},{1,97},{33,1},{65,33},{97,65},{2,98}... | collective-permute-start | bytes 49160 | tf_op jit(solution)/shard_map/ppermute | solution.py:602
  99.1 3.4 %collective-permute-done.15.two = f32[16,256]{1,0:T(8,128)S(1)} collective-permute-done((f32[16,256]{1,0:T(8,128)S(1)}, f32[16,256]{1,0:T(8,128)S(1)}, u32[]{:S(2)}, u32[]{:S(2)}) %collective-permute-start.15) | collective-permute-done | bytes 16416 | tf_op jit(solution)/shard_map/ppermute | solution.py:602
  102.4 4.2 %rows_next.4 = f32[32,16,256]{2,1,0:T(8,128)} custom-call(s32[1,1,32]{2,1,0:T(1,128)S(1)} %copy-done, s32[1,1,32]{2,1,0:T(1,128)S(1)} %copy-done.1, s32[1,1]{1,0:T(1,128)S(6)} %copy.8.tile_count, bf16[4,256,256]{2,1,0:T(8,128)(2,1)S(1)} %get-tuple-element.47.hi_held, bf16[4,256,256]{2,1,0:T(8,128)(2,1)S(1)} %get-tuple-element.48.lo_held, ...), custom_call_target="tpu_custom_call" | custom-call | flops 400000000 | bytes 1048576 | tf_op jit(solution)/shard_map/rows_next/pallas_call | solution.py:300
  106.6 10.9 %all-to-all-start.4 = ((f32[32,16,256]{2,1,0:T(8,128)}), f32[32,16,256]{2,1,0:T(8,128)S(1)}, u32[]{:S(2)}, u32[]{:S(2)}) async-start(f32[32,16,256]{2,1,0:T(8,128)} %rows_next.4), calls=%async_computation.4 | async-start | bytes 1048576 | tf_op jit(solution)/shard_map/all_to_all | solution.py:610
  125.6 3.4 %all-to-all-done.4.refs_0_ = f32[32,16,256]{2,1,0:T(8,128)S(1)} async-done(((f32[32,16,256]{2,1,0:T(8,128)}), f32[32,16,256]{2,1,0:T(8,128)S(1)}, u32[]{:S(2)}, u32[]{:S(2)}) %all-to-all-start.4) | async-done | bytes 524320 | tf_op jit(solution)/shard_map/all_to_all | solution.py:610
  131.0 5.7 %all-to-all-start.7 = ((f32[16,5,8,128]{3,2,1,0:T(8,128)}), f32[16,5,8,128]{3,2,1,0:T(8,128)S(1)}, u32[]{:S(2)}, u32[]{:S(2)}) async-start(f32[16,5,8,128]{3,2,1,0:T(8,128)} %get-tuple-element.74), calls=%async_computation.7 | async-start | bytes 655360 | tf_op jit(solution)/shard_map/all_to_all | solution.py:610
  136.7 3.3 %collective-permute-start.23 = (f32[16,256]{1,0:T(8,128)S(1)}, f32[16,256]{1,0:T(8,128)S(1)}, u32[]{:S(2)}, u32[]{:S(2)}) collective-permute-start(f32[16,256]{1,0:T(8,128)S(1)} %get-tuple-element.73.own), channel_id=1, source_target_pairs={{0,96},{32,0},{64,32},{96,64},{1,97},{33,1},{65,33},{97,65},{2,98}... | collective-permute-start | bytes 49160 | tf_op jit(solution)/shard_map/ppermute | solution.py:602
  140.9 3.4 %collective-permute-done.22.two = f32[16,256]{1,0:T(8,128)S(1)} collective-permute-done((f32[16,256]{1,0:T(8,128)S(1)}, f32[16,256]{1,0:T(8,128)S(1)}, u32[]{:S(2)}, u32[]{:S(2)}) %collective-permute-start.22) | collective-permute-done | bytes 16416 | tf_op jit(solution)/shard_map/ppermute | solution.py:602
  144.2 4.2 %rows_next.5 = f32[32,16,256]{2,1,0:T(8,128)} custom-call(s32[1,1,32]{2,1,0:T(1,128)S(1)} %copy-done, s32[1,1,32]{2,1,0:T(1,128)S(1)} %copy-done.1, s32[1,1]{1,0:T(1,128)S(6)} %copy.8.tile_count, bf16[4,256,256]{2,1,0:T(8,128)(2,1)S(1)} %get-tuple-element.47.hi_held, bf16[4,256,256]{2,1,0:T(8,128)(2,1)S(1)} %get-tuple-element.48.lo_held, ...), custom_call_target="tpu_custom_call" | custom-call | flops 400000000 | bytes 1048576 | tf_op jit(solution)/shard_map/rows_next/pallas_call | solution.py:300
  148.4 10.9 %all-to-all-start.6 = ((f32[32,16,256]{2,1,0:T(8,128)}), f32[32,16,256]{2,1,0:T(8,128)S(1)}, u32[]{:S(2)}, u32[]{:S(2)}) async-start(f32[32,16,256]{2,1,0:T(8,128)} %rows_next.5), calls=%async_computation.6 | async-start | bytes 1048576 | tf_op jit(solution)/shard_map/all_to_all | solution.py:610
  167.2 3.6 %all-to-all-done.6.refs_0_ = f32[32,16,256]{2,1,0:T(8,128)S(1)} async-done(((f32[32,16,256]{2,1,0:T(8,128)}), f32[32,16,256]{2,1,0:T(8,128)S(1)}, u32[]{:S(2)}, u32[]{:S(2)}) %all-to-all-start.6) | async-done | bytes 524320 | tf_op jit(solution)/shard_map/all_to_all | solution.py:610
  172.4 9.1 %all_to_all.50.arrived = f32[8,8,256]{2,1,0:T(8,128)S(1)} all-to-all(f32[8,8,256]{2,1,0:T(8,128)S(1)} %get-tuple-element.80), channel_id=1, replica_groups=mesh['grp'=4,'col_0'=4,'col_1'=4,'col_2'=2] {'col_1','col_2'}, dimensions={0} | all-to-all | bytes 131072 | tf_op jit(solution)/shard_map/all_to_all | solution.py:610
  181.6 14.2 %all_to_all.51.arrived = f32[16,8,256]{2,1,0:T(8,128)S(1)} all-to-all(f32[16,8,256]{2,1,0:T(8,128)S(1)} %fold.1), channel_id=1, replica_groups=mesh['grp'=4,'col_0'=4,'col_1'=4,'col_2'=2] {'grp','col_0'}, dimensions={0} | all-to-all | bytes 262144 | tf_op jit(solution)/shard_map/all_to_all | solution.py:610
  (69 shorter events, 53.1 us)
Async XLA Ops:
  2.1 21.9 %all-to-all-start.1 = ((f32[16,16,256]{2,1,0:T(8,128)}), f32[16,16,256]{2,1,0:T(8,128)S(1)}, u32[]{:S(2)}, u32[]{:S(2)}) async-start(f32[16,16,256]{2,1,0:T(8,128)} %get-tuple-element.52), calls=%async_computation.1 | async-start | bytes 524288 | tf_op jit(solution)/shard_map/all_to_all | solution.py:610
  10.5 5.1 %collective-permute-start = (f32[16,256]{1,0:T(8,128)}, f32[16,256]{1,0:T(8,128)S(1)}, u32[]{:S(2)}, u32[]{:S(2)}) collective-permute-start(f32[16,256]{1,0:T(8,128)} %block.1), channel_id=1, source_target_pairs={{0,32},{32,64},{64,96},{96,0},{1,33},{33,65},{65,97},{97,1},{2,34}... | collective-permute-start | bytes 49160 | tf_op jit(solution)/shard_map/ppermute | solution.py:602
  13.4 4.6 %collective-permute-start.1 = (f32[16,256]{1,0:T(8,128)}, f32[16,256]{1,0:T(8,128)S(1)}, u32[]{:S(2)}, u32[]{:S(2)}) collective-permute-start(f32[16,256]{1,0:T(8,128)} %block.1), channel_id=1, source_target_pairs={{0,64},{32,96},{64,0},{96,32},{1,65},{33,97},{65,1},{97,33},{2,66}... | collective-permute-start | bytes 49160 | tf_op jit(solution)/shard_map/ppermute | solution.py:602
  24.0 23.4 %all-to-all-start = ((f32[32,5,8,128]{3,2,1,0:T(8,128)}), f32[32,5,8,128]{3,2,1,0:T(8,128)S(1)}, u32[]{:S(2)}, u32[]{:S(2)}) async-start(f32[32,5,8,128]{3,2,1,0:T(8,128)} %get-tuple-element.51), calls=%async_computation | async-start | bytes 1310720 | tf_op jit(solution)/shard_map/all_to_all | solution.py:610
  39.1 4.3 %collective-permute-start.4 = (f32[32,256]{1,0:T(8,128)S(1)}, f32[32,256]{1,0:T(8,128)S(1)}, u32[]{:S(2)}, u32[]{:S(2)}) collective-permute-start(f32[32,256]{1,0:T(8,128)S(1)} %get-tuple-element.54), channel_id=1, source_target_pairs={{0,32},{32,64},{64,96},{96,0},{1,33},{33,65},{65,97},{97,1},{2,34}... | collective-permute-start | bytes 98312 | tf_op jit(solution)/shard_map/ppermute | solution.py:602
  39.2 4.6 %collective-permute-start.5 = (f32[32,256]{1,0:T(8,128)S(1)}, f32[32,256]{1,0:T(8,128)S(1)}, u32[]{:S(2)}, u32[]{:S(2)}) collective-permute-start(f32[32,256]{1,0:T(8,128)S(1)} %get-tuple-element.55), channel_id=1, source_target_pairs={{0,64},{32,96},{64,0},{96,32},{1,65},{33,97},{65,1},{97,33},{2,66}... | collective-permute-start | bytes 98312 | tf_op jit(solution)/shard_map/ppermute | solution.py:602
  49.1 16.5 %all-to-all-start.3 = ((f32[16,5,8,128]{3,2,1,0:T(8,128)}), f32[16,5,8,128]{3,2,1,0:T(8,128)S(1)}, u32[]{:S(2)}, u32[]{:S(2)}) async-start(f32[16,5,8,128]{3,2,1,0:T(8,128)} %get-tuple-element.58), calls=%async_computation.3 | async-start | bytes 655360 | tf_op jit(solution)/shard_map/all_to_all | solution.py:610
  53.3 4.5 %collective-permute-start.9 = (f32[16,256]{1,0:T(8,128)S(1)}, f32[16,256]{1,0:T(8,128)S(1)}, u32[]{:S(2)}, u32[]{:S(2)}) collective-permute-start(f32[16,256]{1,0:T(8,128)S(1)} %get-tuple-element.57.own), channel_id=1, source_target_pairs={{0,96},{32,0},{64,32},{96,64},{1,97},{33,1},{65,33},{97,65},{2,98}... | collective-permute-start | bytes 49160 | tf_op jit(solution)/shard_map/ppermute | solution.py:602
  57.0 4.4 %collective-permute-start.8 = (f32[16,256]{1,0:T(8,128)S(1)}, f32[16,256]{1,0:T(8,128)S(1)}, u32[]{:S(2)}, u32[]{:S(2)}) collective-permute-start(f32[16,256]{1,0:T(8,128)S(1)} %get-tuple-element.57.own), channel_id=1, source_target_pairs={{0,64},{32,96},{64,0},{96,32},{1,65},{33,97},{65,1},{97,33},{2,66}... | collective-permute-start | bytes 49160 | tf_op jit(solution)/shard_map/ppermute | solution.py:602
  57.0 4.4 %collective-permute-start.7 = (f32[16,256]{1,0:T(8,128)S(1)}, f32[16,256]{1,0:T(8,128)S(1)}, u32[]{:S(2)}, u32[]{:S(2)}) collective-permute-start(f32[16,256]{1,0:T(8,128)S(1)} %get-tuple-element.57.own), channel_id=1, source_target_pairs={{0,32},{32,64},{64,96},{96,0},{1,33},{33,65},{65,97},{97,1},{2,34}... | collective-permute-start | bytes 49160 | tf_op jit(solution)/shard_map/ppermute | solution.py:602
  65.6 21.7 %all-to-all-start.2 = ((f32[32,16,256]{2,1,0:T(8,128)}), f32[32,16,256]{2,1,0:T(8,128)S(1)}, u32[]{:S(2)}, u32[]{:S(2)}) async-start(f32[32,16,256]{2,1,0:T(8,128)} %rows_next.3), calls=%async_computation.2 | async-start | bytes 1048576 | tf_op jit(solution)/shard_map/all_to_all | solution.py:610
  80.1 7.1 %collective-permute-start.11 = (f32[24,256]{1,0:T(8,128)S(1)}, f32[24,256]{1,0:T(8,128)S(1)}, u32[]{:S(2)}, u32[]{:S(2)}) collective-permute-start(f32[24,256]{1,0:T(8,128)S(1)} %get-tuple-element.60), channel_id=1, source_target_pairs={{0,32},{32,64},{64,96},{96,0},{1,33},{33,65},{65,97},{97,1},{2,34}... | collective-permute-start | bytes 73736 | tf_op jit(solution)/shard_map/ppermute | solution.py:602
  80.2 7.1 %collective-permute-start.12 = (f32[24,256]{1,0:T(8,128)S(1)}, f32[24,256]{1,0:T(8,128)S(1)}, u32[]{:S(2)}, u32[]{:S(2)}) collective-permute-start(f32[24,256]{1,0:T(8,128)S(1)} %get-tuple-element.61), channel_id=1, source_target_pairs={{0,64},{32,96},{64,0},{96,32},{1,65},{33,97},{65,1},{97,33},{2,66}... | collective-permute-start | bytes 73736 | tf_op jit(solution)/shard_map/ppermute | solution.py:602
  81.9 5.4 %collective-permute-start.13 = (f32[24,256]{1,0:T(8,128)S(1)}, f32[24,256]{1,0:T(8,128)S(1)}, u32[]{:S(2)}, u32[]{:S(2)}) collective-permute-start(f32[24,256]{1,0:T(8,128)S(1)} %get-tuple-element.62), channel_id=1, source_target_pairs={{0,96},{32,0},{64,32},{96,64},{1,97},{33,1},{65,33},{97,65},{2,98}... | collective-permute-start | bytes 73736 | tf_op jit(solution)/shard_map/ppermute | solution.py:602
  89.3 17.3 %all-to-all-start.5 = ((f32[16,5,8,128]{3,2,1,0:T(8,128)}), f32[16,5,8,128]{3,2,1,0:T(8,128)S(1)}, u32[]{:S(2)}, u32[]{:S(2)}) async-start(f32[16,5,8,128]{3,2,1,0:T(8,128)} %get-tuple-element.66), calls=%async_computation.5 | async-start | bytes 655360 | tf_op jit(solution)/shard_map/all_to_all | solution.py:610
  106.6 22.4 %all-to-all-start.4 = ((f32[32,16,256]{2,1,0:T(8,128)}), f32[32,16,256]{2,1,0:T(8,128)S(1)}, u32[]{:S(2)}, u32[]{:S(2)}) async-start(f32[32,16,256]{2,1,0:T(8,128)} %rows_next.4), calls=%async_computation.4 | async-start | bytes 1048576 | tf_op jit(solution)/shard_map/all_to_all | solution.py:610
  122.0 7.0 %collective-permute-start.18 = (f32[24,256]{1,0:T(8,128)S(1)}, f32[24,256]{1,0:T(8,128)S(1)}, u32[]{:S(2)}, u32[]{:S(2)}) collective-permute-start(f32[24,256]{1,0:T(8,128)S(1)} %get-tuple-element.68), channel_id=1, source_target_pairs={{0,32},{32,64},{64,96},{96,0},{1,33},{33,65},{65,97},{97,1},{2,34}... | collective-permute-start | bytes 73736 | tf_op jit(solution)/shard_map/ppermute | solution.py:602
  122.1 6.9 %collective-permute-start.19 = (f32[24,256]{1,0:T(8,128)S(1)}, f32[24,256]{1,0:T(8,128)S(1)}, u32[]{:S(2)}, u32[]{:S(2)}) collective-permute-start(f32[24,256]{1,0:T(8,128)S(1)} %get-tuple-element.69), channel_id=1, source_target_pairs={{0,64},{32,96},{64,0},{96,32},{1,65},{33,97},{65,1},{97,33},{2,66}... | collective-permute-start | bytes 73736 | tf_op jit(solution)/shard_map/ppermute | solution.py:602
  123.7 5.3 %collective-permute-start.20 = (f32[24,256]{1,0:T(8,128)S(1)}, f32[24,256]{1,0:T(8,128)S(1)}, u32[]{:S(2)}, u32[]{:S(2)}) collective-permute-start(f32[24,256]{1,0:T(8,128)S(1)} %get-tuple-element.70), channel_id=1, source_target_pairs={{0,96},{32,0},{64,32},{96,64},{1,97},{33,1},{65,33},{97,65},{2,98}... | collective-permute-start | bytes 73736 | tf_op jit(solution)/shard_map/ppermute | solution.py:602
  131.0 17.5 %all-to-all-start.7 = ((f32[16,5,8,128]{3,2,1,0:T(8,128)}), f32[16,5,8,128]{3,2,1,0:T(8,128)S(1)}, u32[]{:S(2)}, u32[]{:S(2)}) async-start(f32[16,5,8,128]{3,2,1,0:T(8,128)} %get-tuple-element.74), calls=%async_computation.7 | async-start | bytes 655360 | tf_op jit(solution)/shard_map/all_to_all | solution.py:610
  148.4 22.4 %all-to-all-start.6 = ((f32[32,16,256]{2,1,0:T(8,128)}), f32[32,16,256]{2,1,0:T(8,128)S(1)}, u32[]{:S(2)}, u32[]{:S(2)}) async-start(f32[32,16,256]{2,1,0:T(8,128)} %rows_next.5), calls=%async_computation.6 | async-start | bytes 1048576 | tf_op jit(solution)/shard_map/all_to_all | solution.py:610
  163.7 7.1 %collective-permute-start.25 = (f32[24,256]{1,0:T(8,128)S(1)}, f32[24,256]{1,0:T(8,128)S(1)}, u32[]{:S(2)}, u32[]{:S(2)}) collective-permute-start(f32[24,256]{1,0:T(8,128)S(1)} %get-tuple-element.76), channel_id=1, source_target_pairs={{0,32},{32,64},{64,96},{96,0},{1,33},{33,65},{65,97},{97,1},{2,34}... | collective-permute-start | bytes 73736 | tf_op jit(solution)/shard_map/ppermute | solution.py:602
  163.7 7.1 %collective-permute-start.26 = (f32[24,256]{1,0:T(8,128)S(1)}, f32[24,256]{1,0:T(8,128)S(1)}, u32[]{:S(2)}, u32[]{:S(2)}) collective-permute-start(f32[24,256]{1,0:T(8,128)S(1)} %get-tuple-element.77), channel_id=1, source_target_pairs={{0,64},{32,96},{64,0},{96,32},{1,65},{33,97},{65,1},{97,33},{2,66}... | collective-permute-start | bytes 73736 | tf_op jit(solution)/shard_map/ppermute | solution.py:602
  165.4 5.4 %collective-permute-start.27 = (f32[24,256]{1,0:T(8,128)S(1)}, f32[24,256]{1,0:T(8,128)S(1)}, u32[]{:S(2)}, u32[]{:S(2)}) collective-permute-start(f32[24,256]{1,0:T(8,128)S(1)} %get-tuple-element.78), channel_id=1, source_target_pairs={{0,96},{32,0},{64,32},{96,64},{1,97},{33,1},{65,33},{97,65},{2,98}... | collective-permute-start | bytes 73736 | tf_op jit(solution)/shard_map/ppermute | solution.py:602
  (14 other events, 75.6 us)

commit v6 on v5

--- a/solution.py
+++ b/solution.py
@@ -12,9 +12,9 @@
 CORE = "col_2"
 COL = ("col_0", "col_1", "col_2")
 GRP_COL = ("grp", "col_0", "col_1", "col_2")
-HELD = 4
-ROW_GROUP = 8
-LATER_ROW_GROUP = 7
+HELD = 8
+ROW_GROUP = HELD
+LATER_ROW_GROUP = 8
 COL_GROUP = 4
 FACTOR_GROUP = 8
 highest = lax.Precision.HIGHEST
@@ -164,7 +164,13 @@
     for copy in index_copies:
         copy.wait()
 
-    @pl.loop(0, count)
+    place = (tile_row, tile_col, tile_count)
+    arriving(0).wait()
+    for u in range(HELD):
+        hi_held[u], lo_held[u] = split(buf[u])
+    group_rows(0, HELD, 0, place, lhs_hi, lhs_lo, hi_held, lo_held, out, True)
+
+    @pl.loop(1, count)
     def _(q):
         arriving(q).wait()
         for u in range(group):
@@ -172,14 +178,9 @@
             hi[s], lo[s] = split(buf[s])
         for copy in group_copies(q, group, hi, lo, hi_out, lo_out, out_sems):
             copy.start()
-        group_rows(
-            q * group, group, 0, (tile_row, tile_col, tile_count), lhs_hi, lhs_lo, hi, lo, out, True
-        )
-
-    hi_held[...] = hi[0:HELD]
-    lo_held[...] = lo[0:HELD]
-
-    @pl.loop(0, count)
+        group_rows(q * group, group, 0, place, lhs_hi, lhs_lo, hi, lo, out, True)
+
+    @pl.loop(1, count)
     def _(q):
         for copy in group_copies(q, group, hi, lo, hi_out, lo_out, out_sems):
             copy.wait()

time: 199 us -> 197 us (0.990)
  waiting for transfers between devices: 34.3 us -> 36.8 us
  Pallas kernels: 39.4 us -> 37.1 us
  starting transfers between devices: 98.7 us -> 96.7 us
    all_to_all x8, waiting for transfers between devices: 13.6 us -> 15.7 us  [exchanged(): return lax.all_to_all(value, axes, split_axis=0, concat_axis=0, tiled=True)]
  transfers between devices with their start and end apart: 36 -> 36, of which waited for: 18 -> 18; matrix products, arithmetic and copies ran while one was open for 0% -> 0% of each run, Pallas kernels for 15% -> 14%
where the time goes in v6:
time: 197 us; the launch traced here: 195 us
  starting transfers between devices  96.7 us (49%)
  Pallas kernels  37.1 us (19%)
  waiting for transfers between devices  36.8 us (19%)
  blocking collectives  22.7 us (12%)
    all_to_all x8, starting transfers between devices, exchanged(): return lax.all_to_all(value, axes, split_axis=0, concat_axis=0, tiled=True)  65.1 us
    ppermute x24, starting transfers between devices, shifted(): lax.ppermute(value, 'grp', [(i, (i + hop) % size) for i in range(size)])  30.3 us
    all_to_all x2, blocking collectives, exchanged(): return lax.all_to_all(value, axes, split_axis=0, concat_axis=0, tiled=True)  22.7 us
    all_to_all x8, waiting for transfers between devices, exchanged(): return lax.all_to_all(value, axes, split_axis=0, concat_axis=0, tiled=True)  15.7 us
    ppermute x24, waiting for transfers between devices, shifted(): lax.ppermute(value, 'grp', [(i, (i + hop) % size) for i in range(size)])  15.6 us
    pallas_call x3, Pallas kernels, rows_next(): pl.pallas_call(rows_next_kernel, name='rows_next', out_shape=jax.ShapeDty...  11.3 us
    pallas_call x4, Pallas kernels, cols_product(): pl.pallas_call(functools.partial(cols_kernel, first), name='cols_first' i...  9.58 us
    pallas_call x4, Pallas kernels, update(): pl.pallas_call(functools.partial(update_kernel, step, node_total), out_sh...  7.21 us
  transfers between devices with their start and end apart: 36, of which 18 were waited for; matrix products, arithmetic and copies ran while one was open for 0% of the time, Pallas kernels for 14%

profile of v6, /device:TPU:1, one launch (start us, length us, event | category | flops | bytes accessed | tf_op | source)
XLA Modules:
  0.0 194.8 jit_solution(9474987860355430635)
XLA Ops:
  2.1 8.4 %all-to-all-start.1 = ((f32[16,16,256]{2,1,0:T(8,128)}), f32[16,16,256]{2,1,0:T(8,128)S(1)}, u32[]{:S(2)}, u32[]{:S(2)}) async-start(f32[16,16,256]{2,1,0:T(8,128)} %get-tuple-element.52), calls=%async_computation.1 | async-start | bytes 524288 | tf_op jit(solution)/shard_map/all_to_all | solution.py:611
  18.0 6.0 %rows_first.1 = (f32[32,5,8,128]{3,2,1,0:T(8,128)}, bf16[8,256,256]{2,1,0:T(8,128)(2,1)S(1)}, bf16[8,256,256]{2,1,0:T(8,128)(2,1)S(1)}, bf16[32,256,256]{2,1,0:T(8,128)(2,1)}, bf16[32,256,256]{2,1,0:T(8,128)(2,1)}) custom-call(s32[1,1,32]{2,1,0:T(1,128)} %row_in.15, s32[1,1,32]{2,1,0:T(1,128)} %col_in.15, s32[1,1]{1,0:T(1,128)S(6)} %copy.8.tile_count, ...), custom_call_target="tpu_custom_call" | custom-call | flops 400000000 | bytes 1048576 | tf_op jit(solution)/shard_map/rows_first/pallas_call | solution.py:270
  24.0 10.3 %all-to-all-start = ((f32[32,5,8,128]{3,2,1,0:T(8,128)}), f32[32,5,8,128]{3,2,1,0:T(8,128)S(1)}, u32[]{:S(2)}, u32[]{:S(2)}) async-start(f32[32,5,8,128]{3,2,1,0:T(8,128)} %get-tuple-element.51), calls=%async_computation | async-start | bytes 1310720 | tf_op jit(solution)/shard_map/all_to_all | solution.py:611
  44.1 3.1 %all-to-all-done.refs_0_ = f32[32,5,8,128]{3,2,1,0:T(8,128)S(1)} async-done(((f32[32,5,8,128]{3,2,1,0:T(8,128)}), f32[32,5,8,128]{3,2,1,0:T(8,128)S(1)}, u32[]{:S(2)}, u32[]{:S(2)}) %all-to-all-start) | async-done | bytes 655392 | tf_op jit(solution)/shard_map/all_to_all | solution.py:611
  48.8 4.2 %all-to-all-start.3 = ((f32[16,5,8,128]{3,2,1,0:T(8,128)}), f32[16,5,8,128]{3,2,1,0:T(8,128)S(1)}, u32[]{:S(2)}, u32[]{:S(2)}) async-start(f32[16,5,8,128]{3,2,1,0:T(8,128)} %get-tuple-element.58), calls=%async_computation.3 | async-start | bytes 655360 | tf_op jit(solution)/shard_map/all_to_all | solution.py:611
  53.0 3.7 %collective-permute-start.9 = (f32[16,256]{1,0:T(8,128)S(1)}, f32[16,256]{1,0:T(8,128)S(1)}, u32[]{:S(2)}, u32[]{:S(2)}) collective-permute-start(f32[16,256]{1,0:T(8,128)S(1)} %get-tuple-element.57.own), channel_id=1, source_target_pairs={{0,96},{32,0},{64,32},{96,64},{1,97},{33,1},{65,33},{97,65},{2,98}... | collective-permute-start | bytes 49160 | tf_op jit(solution)/shard_map/ppermute | solution.py:603
  57.5 3.5 %collective-permute-done.8.two = f32[16,256]{1,0:T(8,128)S(1)} collective-permute-done((f32[16,256]{1,0:T(8,128)S(1)}, f32[16,256]{1,0:T(8,128)S(1)}, u32[]{:S(2)}, u32[]{:S(2)}) %collective-permute-start.8) | collective-permute-done | bytes 16416 | tf_op jit(solution)/shard_map/ppermute | solution.py:603
  61.1 3.8 %rows_next.3 = f32[32,16,256]{2,1,0:T(8,128)} custom-call(s32[1,1,32]{2,1,0:T(1,128)S(1)} %copy-done, s32[1,1,32]{2,1,0:T(1,128)S(1)} %copy-done.1, s32[1,1]{1,0:T(1,128)S(6)} %copy.8.tile_count, bf16[8,256,256]{2,1,0:T(8,128)(2,1)S(1)} %get-tuple-element.47.hi_held, bf16[8,256,256]{2,1,0:T(8,128)(2,1)S(1)} %get-tuple-element.48.lo_held, ...), custom_call_target="tpu_custom_call" | custom-call | flops 400000000 | bytes 1048576 | tf_op jit(solution)/shard_map/rows_next/pallas_call | solution.py:301
  64.9 10.6 %all-to-all-start.2 = ((f32[32,16,256]{2,1,0:T(8,128)}), f32[32,16,256]{2,1,0:T(8,128)S(1)}, u32[]{:S(2)}, u32[]{:S(2)}) async-start(f32[32,16,256]{2,1,0:T(8,128)} %rows_next.3), calls=%async_computation.2 | async-start | bytes 1048576 | tf_op jit(solution)/shard_map/all_to_all | solution.py:611
  82.7 4.2 %all-to-all-done.2.refs_0_ = f32[32,16,256]{2,1,0:T(8,128)S(1)} async-done(((f32[32,16,256]{2,1,0:T(8,128)}), f32[32,16,256]{2,1,0:T(8,128)S(1)}, u32[]{:S(2)}, u32[]{:S(2)}) %all-to-all-start.2) | async-done | bytes 524320 | tf_op jit(solution)/shard_map/all_to_all | solution.py:611
  89.0 4.9 %all-to-all-start.5 = ((f32[16,5,8,128]{3,2,1,0:T(8,128)}), f32[16,5,8,128]{3,2,1,0:T(8,128)S(1)}, u32[]{:S(2)}, u32[]{:S(2)}) async-start(f32[16,5,8,128]{3,2,1,0:T(8,128)} %get-tuple-element.66), calls=%async_computation.5 | async-start | bytes 655360 | tf_op jit(solution)/shard_map/all_to_all | solution.py:611
  93.9 3.6 %collective-permute-start.16 = (f32[16,256]{1,0:T(8,128)S(1)}, f32[16,256]{1,0:T(8,128)S(1)}, u32[]{:S(2)}, u32[]{:S(2)}) collective-permute-start(f32[16,256]{1,0:T(8,128)S(1)} %get-tuple-element.65.own), channel_id=1, source_target_pairs={{0,96},{32,0},{64,32},{96,64},{1,97},{33,1},{65,33},{97,65},{2,98}... | collective-permute-start | bytes 49160 | tf_op jit(solution)/shard_map/ppermute | solution.py:603
  98.4 3.5 %collective-permute-done.15.two = f32[16,256]{1,0:T(8,128)S(1)} collective-permute-done((f32[16,256]{1,0:T(8,128)S(1)}, f32[16,256]{1,0:T(8,128)S(1)}, u32[]{:S(2)}, u32[]{:S(2)}) %collective-permute-start.15) | collective-permute-done | bytes 16416 | tf_op jit(solution)/shard_map/ppermute | solution.py:603
  101.9 3.8 %rows_next.4 = f32[32,16,256]{2,1,0:T(8,128)} custom-call(s32[1,1,32]{2,1,0:T(1,128)S(1)} %copy-done, s32[1,1,32]{2,1,0:T(1,128)S(1)} %copy-done.1, s32[1,1]{1,0:T(1,128)S(6)} %copy.8.tile_count, bf16[8,256,256]{2,1,0:T(8,128)(2,1)S(1)} %get-tuple-element.47.hi_held, bf16[8,256,256]{2,1,0:T(8,128)(2,1)S(1)} %get-tuple-element.48.lo_held, ...), custom_call_target="tpu_custom_call" | custom-call | flops 400000000 | bytes 1048576 | tf_op jit(solution)/shard_map/rows_next/pallas_call | solution.py:301
  105.7 10.9 %all-to-all-start.4 = ((f32[32,16,256]{2,1,0:T(8,128)}), f32[32,16,256]{2,1,0:T(8,128)S(1)}, u32[]{:S(2)}, u32[]{:S(2)}) async-start(f32[32,16,256]{2,1,0:T(8,128)} %rows_next.4), calls=%async_computation.4 | async-start | bytes 1048576 | tf_op jit(solution)/shard_map/all_to_all | solution.py:611
  123.8 4.2 %all-to-all-done.4.refs_0_ = f32[32,16,256]{2,1,0:T(8,128)S(1)} async-done(((f32[32,16,256]{2,1,0:T(8,128)}), f32[32,16,256]{2,1,0:T(8,128)S(1)}, u32[]{:S(2)}, u32[]{:S(2)}) %all-to-all-start.4) | async-done | bytes 524320 | tf_op jit(solution)/shard_map/all_to_all | solution.py:611
  130.0 4.9 %all-to-all-start.7 = ((f32[16,5,8,128]{3,2,1,0:T(8,128)}), f32[16,5,8,128]{3,2,1,0:T(8,128)S(1)}, u32[]{:S(2)}, u32[]{:S(2)}) async-start(f32[16,5,8,128]{3,2,1,0:T(8,128)} %get-tuple-element.74), calls=%async_computation.7 | async-start | bytes 655360 | tf_op jit(solution)/shard_map/all_to_all | solution.py:611
  134.9 3.6 %collective-permute-start.23 = (f32[16,256]{1,0:T(8,128)S(1)}, f32[16,256]{1,0:T(8,128)S(1)}, u32[]{:S(2)}, u32[]{:S(2)}) collective-permute-start(f32[16,256]{1,0:T(8,128)S(1)} %get-tuple-element.73.own), channel_id=1, source_target_pairs={{0,96},{32,0},{64,32},{96,64},{1,97},{33,1},{65,33},{97,65},{2,98}... | collective-permute-start | bytes 49160 | tf_op jit(solution)/shard_map/ppermute | solution.py:603
  139.3 3.5 %collective-permute-done.22.two = f32[16,256]{1,0:T(8,128)S(1)} collective-permute-done((f32[16,256]{1,0:T(8,128)S(1)}, f32[16,256]{1,0:T(8,128)S(1)}, u32[]{:S(2)}, u32[]{:S(2)}) %collective-permute-start.22) | collective-permute-done | bytes 16416 | tf_op jit(solution)/shard_map/ppermute | solution.py:603
  142.9 3.8 %rows_next.5 = f32[32,16,256]{2,1,0:T(8,128)} custom-call(s32[1,1,32]{2,1,0:T(1,128)S(1)} %copy-done, s32[1,1,32]{2,1,0:T(1,128)S(1)} %copy-done.1, s32[1,1]{1,0:T(1,128)S(6)} %copy.8.tile_count, bf16[8,256,256]{2,1,0:T(8,128)(2,1)S(1)} %get-tuple-element.47.hi_held, bf16[8,256,256]{2,1,0:T(8,128)(2,1)S(1)} %get-tuple-element.48.lo_held, ...), custom_call_target="tpu_custom_call" | custom-call | flops 400000000 | bytes 1048576 | tf_op jit(solution)/shard_map/rows_next/pallas_call | solution.py:301
  146.7 10.9 %all-to-all-start.6 = ((f32[32,16,256]{2,1,0:T(8,128)}), f32[32,16,256]{2,1,0:T(8,128)S(1)}, u32[]{:S(2)}, u32[]{:S(2)}) async-start(f32[32,16,256]{2,1,0:T(8,128)} %rows_next.5), calls=%async_computation.6 | async-start | bytes 1048576 | tf_op jit(solution)/shard_map/all_to_all | solution.py:611
  164.7 4.2 %all-to-all-done.6.refs_0_ = f32[32,16,256]{2,1,0:T(8,128)S(1)} async-done(((f32[32,16,256]{2,1,0:T(8,128)}), f32[32,16,256]{2,1,0:T(8,128)S(1)}, u32[]{:S(2)}, u32[]{:S(2)}) %all-to-all-start.6) | async-done | bytes 524320 | tf_op jit(solution)/shard_map/all_to_all | solution.py:611
  170.6 8.8 %all_to_all.50.arrived = f32[8,8,256]{2,1,0:T(8,128)S(1)} all-to-all(f32[8,8,256]{2,1,0:T(8,128)S(1)} %get-tuple-element.80), channel_id=1, replica_groups=mesh['grp'=4,'col_0'=4,'col_1'=4,'col_2'=2] {'col_1','col_2'}, dimensions={0} | all-to-all | bytes 131072 | tf_op jit(solution)/shard_map/all_to_all | solution.py:611
  179.4 13.9 %all_to_all.51.arrived = f32[16,8,256]{2,1,0:T(8,128)S(1)} all-to-all(f32[16,8,256]{2,1,0:T(8,128)S(1)} %fold.1), channel_id=1, replica_groups=mesh['grp'=4,'col_0'=4,'col_1'=4,'col_2'=2] {'grp','col_0'}, dimensions={0} | all-to-all | bytes 262144 | tf_op jit(solution)/shard_map/all_to_all | solution.py:611
  (69 shorter events, 51.0 us)
Async XLA Ops:
  2.1 21.9 %all-to-all-start.1 = ((f32[16,16,256]{2,1,0:T(8,128)}), f32[16,16,256]{2,1,0:T(8,128)S(1)}, u32[]{:S(2)}, u32[]{:S(2)}) async-start(f32[16,16,256]{2,1,0:T(8,128)} %get-tuple-element.52), calls=%async_computation.1 | async-start | bytes 524288 | tf_op jit(solution)/shard_map/all_to_all | solution.py:611
  10.5 5.1 %collective-permute-start = (f32[16,256]{1,0:T(8,128)}, f32[16,256]{1,0:T(8,128)S(1)}, u32[]{:S(2)}, u32[]{:S(2)}) collective-permute-start(f32[16,256]{1,0:T(8,128)} %block.1), channel_id=1, source_target_pairs={{0,32},{32,64},{64,96},{96,0},{1,33},{33,65},{65,97},{97,1},{2,34}... | collective-permute-start | bytes 49160 | tf_op jit(solution)/shard_map/ppermute | solution.py:603
  13.4 4.6 %collective-permute-start.1 = (f32[16,256]{1,0:T(8,128)}, f32[16,256]{1,0:T(8,128)S(1)}, u32[]{:S(2)}, u32[]{:S(2)}) collective-permute-start(f32[16,256]{1,0:T(8,128)} %block.1), channel_id=1, source_target_pairs={{0,64},{32,96},{64,0},{96,32},{1,65},{33,97},{65,1},{97,33},{2,66}... | collective-permute-start | bytes 49160 | tf_op jit(solution)/shard_map/ppermute | solution.py:603
  24.0 23.2 %all-to-all-start = ((f32[32,5,8,128]{3,2,1,0:T(8,128)}), f32[32,5,8,128]{3,2,1,0:T(8,128)S(1)}, u32[]{:S(2)}, u32[]{:S(2)}) async-start(f32[32,5,8,128]{3,2,1,0:T(8,128)} %get-tuple-element.51), calls=%async_computation | async-start | bytes 1310720 | tf_op jit(solution)/shard_map/all_to_all | solution.py:611
  38.9 4.6 %collective-permute-start.5 = (f32[32,256]{1,0:T(8,128)S(1)}, f32[32,256]{1,0:T(8,128)S(1)}, u32[]{:S(2)}, u32[]{:S(2)}) collective-permute-start(f32[32,256]{1,0:T(8,128)S(1)} %get-tuple-element.55), channel_id=1, source_target_pairs={{0,64},{32,96},{64,0},{96,32},{1,65},{33,97},{65,1},{97,33},{2,66}... | collective-permute-start | bytes 98312 | tf_op jit(solution)/shard_map/ppermute | solution.py:603
  48.8 16.1 %all-to-all-start.3 = ((f32[16,5,8,128]{3,2,1,0:T(8,128)}), f32[16,5,8,128]{3,2,1,0:T(8,128)S(1)}, u32[]{:S(2)}, u32[]{:S(2)}) async-start(f32[16,5,8,128]{3,2,1,0:T(8,128)} %get-tuple-element.58), calls=%async_computation.3 | async-start | bytes 655360 | tf_op jit(solution)/shard_map/all_to_all | solution.py:611
  53.0 4.5 %collective-permute-start.9 = (f32[16,256]{1,0:T(8,128)S(1)}, f32[16,256]{1,0:T(8,128)S(1)}, u32[]{:S(2)}, u32[]{:S(2)}) collective-permute-start(f32[16,256]{1,0:T(8,128)S(1)} %get-tuple-element.57.own), channel_id=1, source_target_pairs={{0,96},{32,0},{64,32},{96,64},{1,97},{33,1},{65,33},{97,65},{2,98}... | collective-permute-start | bytes 49160 | tf_op jit(solution)/shard_map/ppermute | solution.py:603
  56.7 4.4 %collective-permute-start.8 = (f32[16,256]{1,0:T(8,128)S(1)}, f32[16,256]{1,0:T(8,128)S(1)}, u32[]{:S(2)}, u32[]{:S(2)}) collective-permute-start(f32[16,256]{1,0:T(8,128)S(1)} %get-tuple-element.57.own), channel_id=1, source_target_pairs={{0,64},{32,96},{64,0},{96,32},{1,65},{33,97},{65,1},{97,33},{2,66}... | collective-permute-start | bytes 49160 | tf_op jit(solution)/shard_map/ppermute | solution.py:603
  64.9 22.1 %all-to-all-start.2 = ((f32[32,16,256]{2,1,0:T(8,128)}), f32[32,16,256]{2,1,0:T(8,128)S(1)}, u32[]{:S(2)}, u32[]{:S(2)}) async-start(f32[32,16,256]{2,1,0:T(8,128)} %rows_next.3), calls=%async_computation.2 | async-start | bytes 1048576 | tf_op jit(solution)/shard_map/all_to_all | solution.py:611
  79.5 7.5 %collective-permute-start.11 = (f32[24,256]{1,0:T(8,128)S(1)}, f32[24,256]{1,0:T(8,128)S(1)}, u32[]{:S(2)}, u32[]{:S(2)}) collective-permute-start(f32[24,256]{1,0:T(8,128)S(1)} %get-tuple-element.60), channel_id=1, source_target_pairs={{0,32},{32,64},{64,96},{96,0},{1,33},{33,65},{65,97},{97,1},{2,34}... | collective-permute-start | bytes 73736 | tf_op jit(solution)/shard_map/ppermute | solution.py:603
  79.6 7.4 %collective-permute-start.12 = (f32[24,256]{1,0:T(8,128)S(1)}, f32[24,256]{1,0:T(8,128)S(1)}, u32[]{:S(2)}, u32[]{:S(2)}) collective-permute-start(f32[24,256]{1,0:T(8,128)S(1)} %get-tuple-element.61), channel_id=1, source_target_pairs={{0,64},{32,96},{64,0},{96,32},{1,65},{33,97},{65,1},{97,33},{2,66}... | collective-permute-start | bytes 73736 | tf_op jit(solution)/shard_map/ppermute | solution.py:603
  80.8 6.1 %collective-permute-start.13 = (f32[24,256]{1,0:T(8,128)S(1)}, f32[24,256]{1,0:T(8,128)S(1)}, u32[]{:S(2)}, u32[]{:S(2)}) collective-permute-start(f32[24,256]{1,0:T(8,128)S(1)} %get-tuple-element.62), channel_id=1, source_target_pairs={{0,96},{32,0},{64,32},{96,64},{1,97},{33,1},{65,33},{97,65},{2,98}... | collective-permute-start | bytes 73736 | tf_op jit(solution)/shard_map/ppermute | solution.py:603
  89.0 16.7 %all-to-all-start.5 = ((f32[16,5,8,128]{3,2,1,0:T(8,128)}), f32[16,5,8,128]{3,2,1,0:T(8,128)S(1)}, u32[]{:S(2)}, u32[]{:S(2)}) async-start(f32[16,5,8,128]{3,2,1,0:T(8,128)} %get-tuple-element.66), calls=%async_computation.5 | async-start | bytes 655360 | tf_op jit(solution)/shard_map/all_to_all | solution.py:611
  93.9 4.5 %collective-permute-start.16 = (f32[16,256]{1,0:T(8,128)S(1)}, f32[16,256]{1,0:T(8,128)S(1)}, u32[]{:S(2)}, u32[]{:S(2)}) collective-permute-start(f32[16,256]{1,0:T(8,128)S(1)} %get-tuple-element.65.own), channel_id=1, source_target_pairs={{0,96},{32,0},{64,32},{96,64},{1,97},{33,1},{65,33},{97,65},{2,98}... | collective-permute-start | bytes 49160 | tf_op jit(solution)/shard_map/ppermute | solution.py:603
  105.7 22.3 %all-to-all-start.4 = ((f32[32,16,256]{2,1,0:T(8,128)}), f32[32,16,256]{2,1,0:T(8,128)S(1)}, u32[]{:S(2)}, u32[]{:S(2)}) async-start(f32[32,16,256]{2,1,0:T(8,128)} %rows_next.4), calls=%async_computation.4 | async-start | bytes 1048576 | tf_op jit(solution)/shard_map/all_to_all | solution.py:611
  120.5 7.5 %collective-permute-start.18 = (f32[24,256]{1,0:T(8,128)S(1)}, f32[24,256]{1,0:T(8,128)S(1)}, u32[]{:S(2)}, u32[]{:S(2)}) collective-permute-start(f32[24,256]{1,0:T(8,128)S(1)} %get-tuple-element.68), channel_id=1, source_target_pairs={{0,32},{32,64},{64,96},{96,0},{1,33},{33,65},{65,97},{97,1},{2,34}... | collective-permute-start | bytes 73736 | tf_op jit(solution)/shard_map/ppermute | solution.py:603
  120.6 7.4 %collective-permute-start.19 = (f32[24,256]{1,0:T(8,128)S(1)}, f32[24,256]{1,0:T(8,128)S(1)}, u32[]{:S(2)}, u32[]{:S(2)}) collective-permute-start(f32[24,256]{1,0:T(8,128)S(1)} %get-tuple-element.69), channel_id=1, source_target_pairs={{0,64},{32,96},{64,0},{96,32},{1,65},{33,97},{65,1},{97,33},{2,66}... | collective-permute-start | bytes 73736 | tf_op jit(solution)/shard_map/ppermute | solution.py:603
  121.9 6.1 %collective-permute-start.20 = (f32[24,256]{1,0:T(8,128)S(1)}, f32[24,256]{1,0:T(8,128)S(1)}, u32[]{:S(2)}, u32[]{:S(2)}) collective-permute-start(f32[24,256]{1,0:T(8,128)S(1)} %get-tuple-element.70), channel_id=1, source_target_pairs={{0,96},{32,0},{64,32},{96,64},{1,97},{33,1},{65,33},{97,65},{2,98}... | collective-permute-start | bytes 73736 | tf_op jit(solution)/shard_map/ppermute | solution.py:603
  130.0 16.7 %all-to-all-start.7 = ((f32[16,5,8,128]{3,2,1,0:T(8,128)}), f32[16,5,8,128]{3,2,1,0:T(8,128)S(1)}, u32[]{:S(2)}, u32[]{:S(2)}) async-start(f32[16,5,8,128]{3,2,1,0:T(8,128)} %get-tuple-element.74), calls=%async_computation.7 | async-start | bytes 655360 | tf_op jit(solution)/shard_map/all_to_all | solution.py:611
  134.9 4.5 %collective-permute-start.23 = (f32[16,256]{1,0:T(8,128)S(1)}, f32[16,256]{1,0:T(8,128)S(1)}, u32[]{:S(2)}, u32[]{:S(2)}) collective-permute-start(f32[16,256]{1,0:T(8,128)S(1)} %get-tuple-element.73.own), channel_id=1, source_target_pairs={{0,96},{32,0},{64,32},{96,64},{1,97},{33,1},{65,33},{97,65},{2,98}... | collective-permute-start | bytes 49160 | tf_op jit(solution)/shard_map/ppermute | solution.py:603
  146.7 22.3 %all-to-all-start.6 = ((f32[32,16,256]{2,1,0:T(8,128)}), f32[32,16,256]{2,1,0:T(8,128)S(1)}, u32[]{:S(2)}, u32[]{:S(2)}) async-start(f32[32,16,256]{2,1,0:T(8,128)} %rows_next.5), calls=%async_computation.6 | async-start | bytes 1048576 | tf_op jit(solution)/shard_map/all_to_all | solution.py:611
  161.5 7.5 %collective-permute-start.25 = (f32[24,256]{1,0:T(8,128)S(1)}, f32[24,256]{1,0:T(8,128)S(1)}, u32[]{:S(2)}, u32[]{:S(2)}) collective-permute-start(f32[24,256]{1,0:T(8,128)S(1)} %get-tuple-element.76), channel_id=1, source_target_pairs={{0,32},{32,64},{64,96},{96,0},{1,33},{33,65},{65,97},{97,1},{2,34}... | collective-permute-start | bytes 73736 | tf_op jit(solution)/shard_map/ppermute | solution.py:603
  161.6 7.4 %collective-permute-start.26 = (f32[24,256]{1,0:T(8,128)S(1)}, f32[24,256]{1,0:T(8,128)S(1)}, u32[]{:S(2)}, u32[]{:S(2)}) collective-permute-start(f32[24,256]{1,0:T(8,128)S(1)} %get-tuple-element.77), channel_id=1, source_target_pairs={{0,64},{32,96},{64,0},{96,32},{1,65},{33,97},{65,1},{97,33},{2,66}... | collective-permute-start | bytes 73736 | tf_op jit(solution)/shard_map/ppermute | solution.py:603
  162.8 6.1 %collective-permute-start.27 = (f32[24,256]{1,0:T(8,128)S(1)}, f32[24,256]{1,0:T(8,128)S(1)}, u32[]{:S(2)}, u32[]{:S(2)}) collective-permute-start(f32[24,256]{1,0:T(8,128)S(1)} %get-tuple-element.78), channel_id=1, source_target_pairs={{0,96},{32,0},{64,32},{96,64},{1,97},{33,1},{65,33},{97,65},{2,98}... | collective-permute-start | bytes 73736 | tf_op jit(solution)/shard_map/ppermute | solution.py:603
  (14 other events, 75.7 us)

commit v7 on v6

--- a/solution.py
+++ b/solution.py
@@ -13,6 +13,7 @@
 COL = ("col_0", "col_1", "col_2")
 GRP_COL = ("grp", "col_0", "col_1", "col_2")
 HELD = 8
+AHEAD = 4
 ROW_GROUP = HELD
 LATER_ROW_GROUP = 8
 COL_GROUP = 4
@@ -140,7 +141,7 @@
 
 
 def rows_first_kernel(
-    row_in, col_in, tile_count, tiles, own, one, two, three, out, hi_held, lo_held, hi_out, lo_out,
+    row_in, col_in, tile_count, tiles, ahead, own, one, two, three, out, hi_held, lo_held, hi_out, lo_out,
     buf, hi, lo, lhs_hi, lhs_lo, tile_row, tile_col, sems, out_sems, index_sems
 ):
     group = ROW_GROUP
@@ -150,7 +151,9 @@
         part = pl.ds(q * group, group)
         return pltpu.make_async_copy(tiles.at[0, 0, part], buf.at[part], sems.at[q])
 
-    arriving(0).start()
+    rest = pl.ds(AHEAD, HELD - AHEAD)
+    rest_copy = pltpu.make_async_copy(tiles.at[0, 0, rest], buf.at[rest], sems.at[0])
+    rest_copy.start()
     index_copies = index_fetch(row_in, col_in, tile_row, tile_col, index_sems)
     for copy in index_copies:
         copy.start()
@@ -165,10 +168,13 @@
         copy.wait()
 
     place = (tile_row, tile_col, tile_count)
-    arriving(0).wait()
-    for u in range(HELD):
+    for u in range(AHEAD):
+        hi_held[u], lo_held[u] = split(ahead[u])
+    group_rows(0, AHEAD, 0, place, lhs_hi, lhs_lo, hi_held, lo_held, out, True)
+    rest_copy.wait()
+    for u in range(AHEAD, HELD):
         hi_held[u], lo_held[u] = split(buf[u])
-    group_rows(0, HELD, 0, place, lhs_hi, lhs_lo, hi_held, lo_held, out, True)
+    group_rows(AHEAD, HELD - AHEAD, 0, place, lhs_hi, lhs_lo, hi_held, lo_held, out, True)
 
     @pl.loop(1, count)
     def _(q):
@@ -265,19 +271,19 @@
         out[...] = jnp.concatenate([acc[k], gram], axis=0)
 
 
-def rows_first(place, tiles, pieces):
+def rows_first(place, tiles, ahead, pieces):
     slots, size = tiles.shape[2], tiles.shape[3]
     return pl.pallas_call(
         rows_first_kernel,
         name="rows_first",
         out_shape=(
-            jax.ShapeDtypeStruct((32, 5, 8, 128), f32),
+            pltpu.MemorySpace.HBM((32, 5, 8, 128), f32),
             pltpu.VMEM((HELD, size, size), bf16),
             pltpu.VMEM((HELD, size, size), bf16),
             pltpu.MemorySpace.HBM((slots, size, size), bf16),
             pltpu.MemorySpace.HBM((slots, size, size), bf16),
         ),
-        in_specs=[HBM, HBM, SMEM] + [HBM] + [VMEM] * 4,
+        in_specs=[HBM, HBM, SMEM] + [HBM] + [VMEM] * 5,
         out_specs=(VMEM, VMEM, VMEM, HBM, HBM),
         scratch_shapes=[
             pltpu.VMEM((slots, size, size), f32),
@@ -293,7 +299,7 @@
         ],
         compiler_params=limits(28),
         cost_estimate=cost(400_000_000),
-    )(*place, tiles, *pieces)
+    )(*place, tiles, ahead, *pieces)
 
 
 def rows_next(place, parts, pieces):
@@ -578,24 +584,32 @@
     )(*args)
 
 
-def first_message_kernel(block, packed, piece):
-    piece[...] = block[...]
+def first_message_kernel(block, tiles, packed, piece, ahead, sems):
+    piece_copy = pltpu.make_async_copy(block, piece, sems.at[0])
+    ahead_copy = pltpu.make_async_copy(tiles.at[0, 0, pl.ds(0, AHEAD)], ahead, sems.at[1])
+    piece_copy.start()
+    ahead_copy.start()
+    piece_copy.wait()
     for p in range(packed.shape[0]):
-        packed[p] = block[...]
-
-
-def first_message(block):
+        packed[p] = piece[...]
+    ahead_copy.wait()
+
+
+def first_message(block, tiles):
+    size = tiles.shape[3]
     return pl.pallas_call(
         first_message_kernel,
         name="first_message",
         out_shape=(
             jax.ShapeDtypeStruct((16, *block.shape), f32),
             pltpu.VMEM(block.shape, f32),
+            pltpu.VMEM((AHEAD, size, size), f32),
         ),
-        in_specs=[VMEM],
-        out_specs=(VMEM, VMEM),
-        compiler_params=limits(4),
-    )(block)
+        in_specs=[HBM, HBM],
+        out_specs=(VMEM, VMEM, VMEM),
+        scratch_shapes=[pltpu.SemaphoreType.DMA((2,))],
+        compiler_params=limits(6),
+    )(block, tiles)
 
 
 def shifted(value, hop):
@@ -624,7 +638,8 @@
     raw_block = start_block
     start_block = pltpu.with_memory_space_constraint(start_block, HBM_SPACE)
     tile_values = pltpu.with_memory_space_constraint(tile_values, pltpu.MemorySpace.HBM)
-    message, piece = first_message(start_block)
+    message, piece, ahead = first_message(start_block, tile_values)
+    ahead = pltpu.with_memory_space_constraint(ahead, pltpu.VMEM)
     origin = piece
     state = degree = shift = parts = None
     lowers, coeffs = [], []
@@ -635,7 +650,7 @@
             pieces.append(shifted(raw_block if first else piece, hop))
         near = exchanged(message, ZX)
         if first:
-            rows, *parts = rows_first(first_place, tile_values, pieces)
+            rows, *parts = rows_first(first_place, tile_values, ahead, pieces)
             parts = [
                 pltpu.with_memory_space_constraint(part, space)
                 for part, space in zip(

time: 197 us -> 194 us (0.985)
    ppermute x24, starting transfers between devices: 30.3 us -> 26.7 us  [shifted(): lax.ppermute(value, 'grp', [(i, (i + hop) % size) for i in range(size)])]
    all_to_all x8, starting transfers between devices: 65.1 us -> 68.7 us  [exchanged(): return lax.all_to_all(value, axes, split_axis=0, concat_axis=0, tiled=True)]
    ppermute x24, waiting for transfers between devices: 15.6 us -> 13.2 us  [shifted(): lax.ppermute(value, 'grp', [(i, (i + hop) % size) for i in range(size)])]
  transfers between devices with their start and end apart: 36 -> 36, of which waited for: 18 -> 21; matrix products, arithmetic and copies ran while one was open for 0% -> 0% of each run, Pallas kernels for 14% -> 14%
where the time goes in v7:
time: 194 us; the launch traced here: 192 us
  starting transfers between devices  96.6 us (50%)
  Pallas kernels  37.2 us (19%)
  waiting for transfers between devices  34.9 us (18%)
  blocking collectives  22.2 us (11%)
    all_to_all x8, starting transfers between devices, exchanged(): return lax.all_to_all(value, axes, split_axis=0, concat_axis=0, tiled=True)  68.7 us
    ppermute x24, starting transfers between devices, shifted(): lax.ppermute(value, 'grp', [(i, (i + hop) % size) for i in range(size)])  26.7 us
    all_to_all x2, blocking collectives, exchanged(): return lax.all_to_all(value, axes, split_axis=0, concat_axis=0, tiled=True)  22.2 us
    all_to_all x8, waiting for transfers between devices, exchanged(): return lax.all_to_all(value, axes, split_axis=0, concat_axis=0, tiled=True)  16.2 us
    ppermute x24, waiting for transfers between devices, shifted(): lax.ppermute(value, 'grp', [(i, (i + hop) % size) for i in range(size)])  13.2 us
    pallas_call x3, Pallas kernels, rows_next(): pl.pallas_call(rows_next_kernel, name='rows_next', out_shape=jax.ShapeDty...  11.3 us
    pallas_call x4, Pallas kernels, cols_product(): pl.pallas_call(functools.partial(cols_kernel, first), name='cols_first' i...  9.57 us
    pallas_call x4, Pallas kernels, update(): pl.pallas_call(functools.partial(update_kernel, step, node_total), out_sh...  7.25 us
  transfers between devices with their start and end apart: 36, of which 21 were waited for; matrix products, arithmetic and copies ran while one was open for 0% of the time, Pallas kernels for 14%

profile of v7, /device:TPU:1, one launch (start us, length us, event | category | flops | bytes accessed | tf_op | source)
XLA Modules:
  0.0 192.5 jit_solution(8804339104728830015)
XLA Ops:
  2.6 8.4 %all-to-all-start.1 = ((f32[16,16,256]{2,1,0:T(8,128)}), f32[16,16,256]{2,1,0:T(8,128)S(1)}, u32[]{:S(2)}, u32[]{:S(2)}) async-start(f32[16,16,256]{2,1,0:T(8,128)} %get-tuple-element.54), calls=%async_computation.1 | async-start | bytes 524288 | tf_op jit(solution)/shard_map/all_to_all | solution.py:625
  12.4 2.6 %collective-permute-start.1 = (f32[16,256]{1,0:T(8,128)S(1)}, f32[16,256]{1,0:T(8,128)S(1)}, u32[]{:S(2)}, u32[]{:S(2)}) collective-permute-start(f32[16,256]{1,0:T(8,128)S(1)} %copy-done.2), channel_id=1, source_target_pairs={{0,64},{32,96},{64,0},{96,32},{1,65},{33,97},{65,1},{97,33},{2,66}... | collective-permute-start | bytes 49160 | tf_op jit(solution)/shard_map/ppermute | solution.py:617
  17.9 5.5 %rows_first.1 = (f32[32,5,8,128]{3,2,1,0:T(8,128)}, bf16[8,256,256]{2,1,0:T(8,128)(2,1)S(1)}, bf16[8,256,256]{2,1,0:T(8,128)(2,1)S(1)}, bf16[32,256,256]{2,1,0:T(8,128)(2,1)}, bf16[32,256,256]{2,1,0:T(8,128)(2,1)}) custom-call(s32[1,1,32]{2,1,0:T(1,128)} %row_in.15, s32[1,1,32]{2,1,0:T(1,128)} %col_in.15, s32[1,1]{1,0:T(1,128)S(6)} %copy.8.tile_count, ...), custom_call_target="tpu_custom_call" | custom-call | flops 400000000 | bytes 1048576 | tf_op jit(solution)/shard_map/rows_first/pallas_call | solution.py:276
  23.5 10.5 %all-to-all-start = ((f32[32,5,8,128]{3,2,1,0:T(8,128)}), f32[32,5,8,128]{3,2,1,0:T(8,128)S(1)}, u32[]{:S(2)}, u32[]{:S(2)}) async-start(f32[32,5,8,128]{3,2,1,0:T(8,128)} %get-tuple-element.53), calls=%async_computation | async-start | bytes 1310720 | tf_op jit(solution)/shard_map/all_to_all | solution.py:625
  35.7 2.9 %cols_first.1 = (f32[32,256]{1,0:T(8,128)S(1)}, f32[32,256]{1,0:T(8,128)S(1)}, f32[32,256]{1,0:T(8,128)S(1)}, f32[32,256]{1,0:T(8,128)S(1)}) custom-call(s32[1,1,32]{2,1,0:T(1,128)S(1)} %copy-done, s32[1,1,32]{2,1,0:T(1,128)S(1)} %copy-done.1, s32[1,1]{1,0:T(1,128)S(6)} %copy.8.tile_count, bf16[8,256,256]{2,1,0:T(8,128)(2,1)S(1)} %get-tuple-element.49.hi_held, ...), custom_call_target="tpu_custom_call" | custom-call | flops 400000000 | bytes 1048576 | tf_op jit(solution)/shard_map/cols_first/pallas_call | solution.py:332
  38.6 2.9 %collective-permute-start.5 = (f32[32,256]{1,0:T(8,128)S(1)}, f32[32,256]{1,0:T(8,128)S(1)}, u32[]{:S(2)}, u32[]{:S(2)}) collective-permute-start(f32[32,256]{1,0:T(8,128)S(1)} %get-tuple-element.57), channel_id=1, source_target_pairs={{0,64},{32,96},{64,0},{96,32},{1,65},{33,97},{65,1},{97,33},{2,66}... | collective-permute-start | bytes 98312 | tf_op jit(solution)/shard_map/ppermute | solution.py:617
  48.5 4.5 %all-to-all-start.3 = ((f32[16,5,8,128]{3,2,1,0:T(8,128)}), f32[16,5,8,128]{3,2,1,0:T(8,128)S(1)}, u32[]{:S(2)}, u32[]{:S(2)}) async-start(f32[16,5,8,128]{3,2,1,0:T(8,128)} %get-tuple-element.60), calls=%async_computation.3 | async-start | bytes 655360 | tf_op jit(solution)/shard_map/all_to_all | solution.py:625
  53.6 2.9 %collective-permute-start.8 = (f32[16,256]{1,0:T(8,128)S(1)}, f32[16,256]{1,0:T(8,128)S(1)}, u32[]{:S(2)}, u32[]{:S(2)}) collective-permute-start(f32[16,256]{1,0:T(8,128)S(1)} %get-tuple-element.59.own), channel_id=1, source_target_pairs={{0,64},{32,96},{64,0},{96,32},{1,65},{33,97},{65,1},{97,33},{2,66}... | collective-permute-start | bytes 49160 | tf_op jit(solution)/shard_map/ppermute | solution.py:617
  59.4 3.8 %rows_next.3 = f32[32,16,256]{2,1,0:T(8,128)} custom-call(s32[1,1,32]{2,1,0:T(1,128)S(1)} %copy-done, s32[1,1,32]{2,1,0:T(1,128)S(1)} %copy-done.1, s32[1,1]{1,0:T(1,128)S(6)} %copy.8.tile_count, bf16[8,256,256]{2,1,0:T(8,128)(2,1)S(1)} %get-tuple-element.49.hi_held, bf16[8,256,256]{2,1,0:T(8,128)(2,1)S(1)} %get-tuple-element.50.lo_held, ...), custom_call_target="tpu_custom_call" | custom-call | flops 400000000 | bytes 1048576 | tf_op jit(solution)/shard_map/rows_next/pallas_call | solution.py:307
  63.2 11.6 %all-to-all-start.2 = ((f32[32,16,256]{2,1,0:T(8,128)}), f32[32,16,256]{2,1,0:T(8,128)S(1)}, u32[]{:S(2)}, u32[]{:S(2)}) async-start(f32[32,16,256]{2,1,0:T(8,128)} %rows_next.3), calls=%async_computation.2 | async-start | bytes 1048576 | tf_op jit(solution)/shard_map/all_to_all | solution.py:625
  81.4 4.7 %all-to-all-done.2.refs_0_ = f32[32,16,256]{2,1,0:T(8,128)S(1)} async-done(((f32[32,16,256]{2,1,0:T(8,128)}), f32[32,16,256]{2,1,0:T(8,128)S(1)}, u32[]{:S(2)}, u32[]{:S(2)}) %all-to-all-start.2) | async-done | bytes 524320 | tf_op jit(solution)/shard_map/all_to_all | solution.py:625
  88.2 4.9 %all-to-all-start.5 = ((f32[16,5,8,128]{3,2,1,0:T(8,128)}), f32[16,5,8,128]{3,2,1,0:T(8,128)S(1)}, u32[]{:S(2)}, u32[]{:S(2)}) async-start(f32[16,5,8,128]{3,2,1,0:T(8,128)} %get-tuple-element.68), calls=%async_computation.5 | async-start | bytes 655360 | tf_op jit(solution)/shard_map/all_to_all | solution.py:625
  94.1 2.5 %collective-permute-start.15 = (f32[16,256]{1,0:T(8,128)S(1)}, f32[16,256]{1,0:T(8,128)S(1)}, u32[]{:S(2)}, u32[]{:S(2)}) collective-permute-start(f32[16,256]{1,0:T(8,128)S(1)} %get-tuple-element.67.own), channel_id=1, source_target_pairs={{0,64},{32,96},{64,0},{96,32},{1,65},{33,97},{65,1},{97,33},{2,66}... | collective-permute-start | bytes 49160 | tf_op jit(solution)/shard_map/ppermute | solution.py:617
  99.5 3.8 %rows_next.4 = f32[32,16,256]{2,1,0:T(8,128)} custom-call(s32[1,1,32]{2,1,0:T(1,128)S(1)} %copy-done, s32[1,1,32]{2,1,0:T(1,128)S(1)} %copy-done.1, s32[1,1]{1,0:T(1,128)S(6)} %copy.8.tile_count, bf16[8,256,256]{2,1,0:T(8,128)(2,1)S(1)} %get-tuple-element.49.hi_held, bf16[8,256,256]{2,1,0:T(8,128)(2,1)S(1)} %get-tuple-element.50.lo_held, ...), custom_call_target="tpu_custom_call" | custom-call | flops 400000000 | bytes 1048576 | tf_op jit(solution)/shard_map/rows_next/pallas_call | solution.py:307
  103.3 11.9 %all-to-all-start.4 = ((f32[32,16,256]{2,1,0:T(8,128)}), f32[32,16,256]{2,1,0:T(8,128)S(1)}, u32[]{:S(2)}, u32[]{:S(2)}) async-start(f32[32,16,256]{2,1,0:T(8,128)} %rows_next.4), calls=%async_computation.4 | async-start | bytes 1048576 | tf_op jit(solution)/shard_map/all_to_all | solution.py:625
  116.9 2.2 %cols_next.4 = (f32[24,256]{1,0:T(8,128)S(1)}, f32[24,256]{1,0:T(8,128)S(1)}, f32[24,256]{1,0:T(8,128)S(1)}, f32[24,256]{1,0:T(8,128)S(1)}) custom-call(s32[1,1,32]{2,1,0:T(1,128)S(1)} %copy-done, s32[1,1,32]{2,1,0:T(1,128)S(1)} %copy-done.1, s32[1,1]{1,0:T(1,128)S(6)} %copy.8.tile_count, bf16[8,256,256]{2,1,0:T(8,128)(2,1)S(1)} %get-tuple-element.49.hi_held, ...), custom_call_target="tpu_custom_call" | custom-call | flops 400000000 | bytes 1048576 | tf_op jit(solution)/shard_map/cols_next/pallas_call | solution.py:332
  121.9 4.7 %all-to-all-done.4.refs_0_ = f32[32,16,256]{2,1,0:T(8,128)S(1)} async-done(((f32[32,16,256]{2,1,0:T(8,128)}), f32[32,16,256]{2,1,0:T(8,128)S(1)}, u32[]{:S(2)}, u32[]{:S(2)}) %all-to-all-start.4) | async-done | bytes 524320 | tf_op jit(solution)/shard_map/all_to_all | solution.py:625
  128.7 4.9 %all-to-all-start.7 = ((f32[16,5,8,128]{3,2,1,0:T(8,128)}), f32[16,5,8,128]{3,2,1,0:T(8,128)S(1)}, u32[]{:S(2)}, u32[]{:S(2)}) async-start(f32[16,5,8,128]{3,2,1,0:T(8,128)} %get-tuple-element.76), calls=%async_computation.7 | async-start | bytes 655360 | tf_op jit(solution)/shard_map/all_to_all | solution.py:625
  134.5 2.5 %collective-permute-start.22 = (f32[16,256]{1,0:T(8,128)S(1)}, f32[16,256]{1,0:T(8,128)S(1)}, u32[]{:S(2)}, u32[]{:S(2)}) collective-permute-start(f32[16,256]{1,0:T(8,128)S(1)} %get-tuple-element.75.own), channel_id=1, source_target_pairs={{0,64},{32,96},{64,0},{96,32},{1,65},{33,97},{65,1},{97,33},{2,66}... | collective-permute-start | bytes 49160 | tf_op jit(solution)/shard_map/ppermute | solution.py:617
  139.9 3.8 %rows_next.5 = f32[32,16,256]{2,1,0:T(8,128)} custom-call(s32[1,1,32]{2,1,0:T(1,128)S(1)} %copy-done, s32[1,1,32]{2,1,0:T(1,128)S(1)} %copy-done.1, s32[1,1]{1,0:T(1,128)S(6)} %copy.8.tile_count, bf16[8,256,256]{2,1,0:T(8,128)(2,1)S(1)} %get-tuple-element.49.hi_held, bf16[8,256,256]{2,1,0:T(8,128)(2,1)S(1)} %get-tuple-element.50.lo_held, ...), custom_call_target="tpu_custom_call" | custom-call | flops 400000000 | bytes 1048576 | tf_op jit(solution)/shard_map/rows_next/pallas_call | solution.py:307
  143.7 11.9 %all-to-all-start.6 = ((f32[32,16,256]{2,1,0:T(8,128)}), f32[32,16,256]{2,1,0:T(8,128)S(1)}, u32[]{:S(2)}, u32[]{:S(2)}) async-start(f32[32,16,256]{2,1,0:T(8,128)} %rows_next.5), calls=%async_computation.6 | async-start | bytes 1048576 | tf_op jit(solution)/shard_map/all_to_all | solution.py:625
  162.4 4.7 %all-to-all-done.6.refs_0_ = f32[32,16,256]{2,1,0:T(8,128)S(1)} async-done(((f32[32,16,256]{2,1,0:T(8,128)}), f32[32,16,256]{2,1,0:T(8,128)S(1)}, u32[]{:S(2)}, u32[]{:S(2)}) %all-to-all-start.6) | async-done | bytes 524320 | tf_op jit(solution)/shard_map/all_to_all | solution.py:625
  168.7 8.8 %all_to_all.50.arrived = f32[8,8,256]{2,1,0:T(8,128)S(1)} all-to-all(f32[8,8,256]{2,1,0:T(8,128)S(1)} %get-tuple-element.82), channel_id=1, replica_groups=mesh['grp'=4,'col_0'=4,'col_1'=4,'col_2'=2] {'col_1','col_2'}, dimensions={0} | all-to-all | bytes 131072 | tf_op jit(solution)/shard_map/all_to_all | solution.py:625
  177.5 13.4 %all_to_all.51.arrived = f32[16,8,256]{2,1,0:T(8,128)S(1)} all-to-all(f32[16,8,256]{2,1,0:T(8,128)S(1)} %fold.1), channel_id=1, replica_groups=mesh['grp'=4,'col_0'=4,'col_1'=4,'col_2'=2] {'grp','col_0'}, dimensions={0} | all-to-all | bytes 262144 | tf_op jit(solution)/shard_map/all_to_all | solution.py:625
  (71 shorter events, 50.5 us)
Async XLA Ops:
  2.6 20.9 %all-to-all-start.1 = ((f32[16,16,256]{2,1,0:T(8,128)}), f32[16,16,256]{2,1,0:T(8,128)S(1)}, u32[]{:S(2)}, u32[]{:S(2)}) async-start(f32[16,16,256]{2,1,0:T(8,128)} %get-tuple-element.54), calls=%async_computation.1 | async-start | bytes 524288 | tf_op jit(solution)/shard_map/all_to_all | solution.py:625
  11.1 5.7 %collective-permute-start = (f32[16,256]{1,0:T(8,128)S(1)}, f32[16,256]{1,0:T(8,128)S(1)}, u32[]{:S(2)}, u32[]{:S(2)}) collective-permute-start(f32[16,256]{1,0:T(8,128)S(1)} %copy-done.2), channel_id=1, source_target_pairs={{0,32},{32,64},{64,96},{96,0},{1,33},{33,65},{65,97},{97,1},{2,34}... | collective-permute-start | bytes 49160 | tf_op jit(solution)/shard_map/ppermute | solution.py:617
  12.4 4.4 %collective-permute-start.1 = (f32[16,256]{1,0:T(8,128)S(1)}, f32[16,256]{1,0:T(8,128)S(1)}, u32[]{:S(2)}, u32[]{:S(2)}) collective-permute-start(f32[16,256]{1,0:T(8,128)S(1)} %copy-done.2), channel_id=1, source_target_pairs={{0,64},{32,96},{64,0},{96,32},{1,65},{33,97},{65,1},{97,33},{2,66}... | collective-permute-start | bytes 49160 | tf_op jit(solution)/shard_map/ppermute | solution.py:617
  23.5 23.4 %all-to-all-start = ((f32[32,5,8,128]{3,2,1,0:T(8,128)}), f32[32,5,8,128]{3,2,1,0:T(8,128)S(1)}, u32[]{:S(2)}, u32[]{:S(2)}) async-start(f32[32,5,8,128]{3,2,1,0:T(8,128)} %get-tuple-element.53), calls=%async_computation | async-start | bytes 1310720 | tf_op jit(solution)/shard_map/all_to_all | solution.py:625
  38.5 4.3 %collective-permute-start.4 = (f32[32,256]{1,0:T(8,128)S(1)}, f32[32,256]{1,0:T(8,128)S(1)}, u32[]{:S(2)}, u32[]{:S(2)}) collective-permute-start(f32[32,256]{1,0:T(8,128)S(1)} %get-tuple-element.56), channel_id=1, source_target_pairs={{0,32},{32,64},{64,96},{96,0},{1,33},{33,65},{65,97},{97,1},{2,34}... | collective-permute-start | bytes 98312 | tf_op jit(solution)/shard_map/ppermute | solution.py:617
  38.6 5.0 %collective-permute-start.5 = (f32[32,256]{1,0:T(8,128)S(1)}, f32[32,256]{1,0:T(8,128)S(1)}, u32[]{:S(2)}, u32[]{:S(2)}) collective-permute-start(f32[32,256]{1,0:T(8,128)S(1)} %get-tuple-element.57), channel_id=1, source_target_pairs={{0,64},{32,96},{64,0},{96,32},{1,65},{33,97},{65,1},{97,33},{2,66}... | collective-permute-start | bytes 98312 | tf_op jit(solution)/shard_map/ppermute | solution.py:617
  48.5 14.6 %all-to-all-start.3 = ((f32[16,5,8,128]{3,2,1,0:T(8,128)}), f32[16,5,8,128]{3,2,1,0:T(8,128)S(1)}, u32[]{:S(2)}, u32[]{:S(2)}) async-start(f32[16,5,8,128]{3,2,1,0:T(8,128)} %get-tuple-element.60), calls=%async_computation.3 | async-start | bytes 655360 | tf_op jit(solution)/shard_map/all_to_all | solution.py:625
  53.6 4.2 %collective-permute-start.8 = (f32[16,256]{1,0:T(8,128)S(1)}, f32[16,256]{1,0:T(8,128)S(1)}, u32[]{:S(2)}, u32[]{:S(2)}) collective-permute-start(f32[16,256]{1,0:T(8,128)S(1)} %get-tuple-element.59.own), channel_id=1, source_target_pairs={{0,64},{32,96},{64,0},{96,32},{1,65},{33,97},{65,1},{97,33},{2,66}... | collective-permute-start | bytes 49160 | tf_op jit(solution)/shard_map/ppermute | solution.py:617
  63.2 23.0 %all-to-all-start.2 = ((f32[32,16,256]{2,1,0:T(8,128)}), f32[32,16,256]{2,1,0:T(8,128)S(1)}, u32[]{:S(2)}, u32[]{:S(2)}) async-start(f32[32,16,256]{2,1,0:T(8,128)} %rows_next.3), calls=%async_computation.2 | async-start | bytes 1048576 | tf_op jit(solution)/shard_map/all_to_all | solution.py:625
  78.7 7.5 %collective-permute-start.11 = (f32[24,256]{1,0:T(8,128)S(1)}, f32[24,256]{1,0:T(8,128)S(1)}, u32[]{:S(2)}, u32[]{:S(2)}) collective-permute-start(f32[24,256]{1,0:T(8,128)S(1)} %get-tuple-element.62), channel_id=1, source_target_pairs={{0,32},{32,64},{64,96},{96,0},{1,33},{33,65},{65,97},{97,1},{2,34}... | collective-permute-start | bytes 73736 | tf_op jit(solution)/shard_map/ppermute | solution.py:617
  78.8 7.4 %collective-permute-start.12 = (f32[24,256]{1,0:T(8,128)S(1)}, f32[24,256]{1,0:T(8,128)S(1)}, u32[]{:S(2)}, u32[]{:S(2)}) collective-permute-start(f32[24,256]{1,0:T(8,128)S(1)} %get-tuple-element.63), channel_id=1, source_target_pairs={{0,64},{32,96},{64,0},{96,32},{1,65},{33,97},{65,1},{97,33},{2,66}... | collective-permute-start | bytes 73736 | tf_op jit(solution)/shard_map/ppermute | solution.py:617
  80.5 5.7 %collective-permute-start.13 = (f32[24,256]{1,0:T(8,128)S(1)}, f32[24,256]{1,0:T(8,128)S(1)}, u32[]{:S(2)}, u32[]{:S(2)}) collective-permute-start(f32[24,256]{1,0:T(8,128)S(1)} %get-tuple-element.64), channel_id=1, source_target_pairs={{0,96},{32,0},{64,32},{96,64},{1,97},{33,1},{65,33},{97,65},{2,98}... | collective-permute-start | bytes 73736 | tf_op jit(solution)/shard_map/ppermute | solution.py:617
  88.2 15.1 %all-to-all-start.5 = ((f32[16,5,8,128]{3,2,1,0:T(8,128)}), f32[16,5,8,128]{3,2,1,0:T(8,128)S(1)}, u32[]{:S(2)}, u32[]{:S(2)}) async-start(f32[16,5,8,128]{3,2,1,0:T(8,128)} %get-tuple-element.68), calls=%async_computation.5 | async-start | bytes 655360 | tf_op jit(solution)/shard_map/all_to_all | solution.py:625
  94.1 4.1 %collective-permute-start.15 = (f32[16,256]{1,0:T(8,128)S(1)}, f32[16,256]{1,0:T(8,128)S(1)}, u32[]{:S(2)}, u32[]{:S(2)}) collective-permute-start(f32[16,256]{1,0:T(8,128)S(1)} %get-tuple-element.67.own), channel_id=1, source_target_pairs={{0,64},{32,96},{64,0},{96,32},{1,65},{33,97},{65,1},{97,33},{2,66}... | collective-permute-start | bytes 49160 | tf_op jit(solution)/shard_map/ppermute | solution.py:617
  103.3 23.4 %all-to-all-start.4 = ((f32[32,16,256]{2,1,0:T(8,128)}), f32[32,16,256]{2,1,0:T(8,128)S(1)}, u32[]{:S(2)}, u32[]{:S(2)}) async-start(f32[32,16,256]{2,1,0:T(8,128)} %rows_next.4), calls=%async_computation.4 | async-start | bytes 1048576 | tf_op jit(solution)/shard_map/all_to_all | solution.py:625
  119.2 7.5 %collective-permute-start.18 = (f32[24,256]{1,0:T(8,128)S(1)}, f32[24,256]{1,0:T(8,128)S(1)}, u32[]{:S(2)}, u32[]{:S(2)}) collective-permute-start(f32[24,256]{1,0:T(8,128)S(1)} %get-tuple-element.70), channel_id=1, source_target_pairs={{0,32},{32,64},{64,96},{96,0},{1,33},{33,65},{65,97},{97,1},{2,34}... | collective-permute-start | bytes 73736 | tf_op jit(solution)/shard_map/ppermute | solution.py:617
  119.3 7.4 %collective-permute-start.19 = (f32[24,256]{1,0:T(8,128)S(1)}, f32[24,256]{1,0:T(8,128)S(1)}, u32[]{:S(2)}, u32[]{:S(2)}) collective-permute-start(f32[24,256]{1,0:T(8,128)S(1)} %get-tuple-element.71), channel_id=1, source_target_pairs={{0,64},{32,96},{64,0},{96,32},{1,65},{33,97},{65,1},{97,33},{2,66}... | collective-permute-start | bytes 73736 | tf_op jit(solution)/shard_map/ppermute | solution.py:617
  121.0 5.7 %collective-permute-start.20 = (f32[24,256]{1,0:T(8,128)S(1)}, f32[24,256]{1,0:T(8,128)S(1)}, u32[]{:S(2)}, u32[]{:S(2)}) collective-permute-start(f32[24,256]{1,0:T(8,128)S(1)} %get-tuple-element.72), channel_id=1, source_target_pairs={{0,96},{32,0},{64,32},{96,64},{1,97},{33,1},{65,33},{97,65},{2,98}... | collective-permute-start | bytes 73736 | tf_op jit(solution)/shard_map/ppermute | solution.py:617
  128.7 15.1 %all-to-all-start.7 = ((f32[16,5,8,128]{3,2,1,0:T(8,128)}), f32[16,5,8,128]{3,2,1,0:T(8,128)S(1)}, u32[]{:S(2)}, u32[]{:S(2)}) async-start(f32[16,5,8,128]{3,2,1,0:T(8,128)} %get-tuple-element.76), calls=%async_computation.7 | async-start | bytes 655360 | tf_op jit(solution)/shard_map/all_to_all | solution.py:625
  134.5 4.1 %collective-permute-start.22 = (f32[16,256]{1,0:T(8,128)S(1)}, f32[16,256]{1,0:T(8,128)S(1)}, u32[]{:S(2)}, u32[]{:S(2)}) collective-permute-start(f32[16,256]{1,0:T(8,128)S(1)} %get-tuple-element.75.own), channel_id=1, source_target_pairs={{0,64},{32,96},{64,0},{96,32},{1,65},{33,97},{65,1},{97,33},{2,66}... | collective-permute-start | bytes 49160 | tf_op jit(solution)/shard_map/ppermute | solution.py:617
  143.7 23.4 %all-to-all-start.6 = ((f32[32,16,256]{2,1,0:T(8,128)}), f32[32,16,256]{2,1,0:T(8,128)S(1)}, u32[]{:S(2)}, u32[]{:S(2)}) async-start(f32[32,16,256]{2,1,0:T(8,128)} %rows_next.5), calls=%async_computation.6 | async-start | bytes 1048576 | tf_op jit(solution)/shard_map/all_to_all | solution.py:625
  159.6 7.5 %collective-permute-start.25 = (f32[24,256]{1,0:T(8,128)S(1)}, f32[24,256]{1,0:T(8,128)S(1)}, u32[]{:S(2)}, u32[]{:S(2)}) collective-permute-start(f32[24,256]{1,0:T(8,128)S(1)} %get-tuple-element.78), channel_id=1, source_target_pairs={{0,32},{32,64},{64,96},{96,0},{1,33},{33,65},{65,97},{97,1},{2,34}... | collective-permute-start | bytes 73736 | tf_op jit(solution)/shard_map/ppermute | solution.py:617
  159.7 7.4 %collective-permute-start.26 = (f32[24,256]{1,0:T(8,128)S(1)}, f32[24,256]{1,0:T(8,128)S(1)}, u32[]{:S(2)}, u32[]{:S(2)}) collective-permute-start(f32[24,256]{1,0:T(8,128)S(1)} %get-tuple-element.79), channel_id=1, source_target_pairs={{0,64},{32,96},{64,0},{96,32},{1,65},{33,97},{65,1},{97,33},{2,66}... | collective-permute-start | bytes 73736 | tf_op jit(solution)/shard_map/ppermute | solution.py:617
  161.4 5.7 %collective-permute-start.27 = (f32[24,256]{1,0:T(8,128)S(1)}, f32[24,256]{1,0:T(8,128)S(1)}, u32[]{:S(2)}, u32[]{:S(2)}) collective-permute-start(f32[24,256]{1,0:T(8,128)S(1)} %get-tuple-element.80), channel_id=1, source_target_pairs={{0,96},{32,0},{64,32},{96,64},{1,97},{33,1},{65,33},{97,65},{2,98}... | collective-permute-start | bytes 73736 | tf_op jit(solution)/shard_map/ppermute | solution.py:617
  (15 other events, 79.2 us)
